TPU v7x, 8 devices: a whole 2x2x1 slice. The times are simulated.
8 devices in a mesh: dp: 1 (over z), row: 2 (over y), col: 4 (over x, core).
Axes of the slice: x: 2, y: 2, z: 1, core: 2. Of those that a mesh axis runs over, the one named last changes fastest.
Arguments:
- x: bfloat16 [24, 256, 6144], P(('dp', 'row'), None, 'col')
- ln_scale: float32 [6144], P('col')
- w_qkv: bfloat16 [6144, 18432], P('col', 'row')
- q_scale: float32 [128], replicated
- k_scale: float32 [128], replicated
- w_out: bfloat16 [6144, 6144], P('row', 'col')
- w_up: bfloat16 [6144, 24576], P('col', 'row')
- b_up: float32 [24576], P('row')
- w_down: bfloat16 [24576, 6144], P('row', 'col')
- b_down: float32 [6144], P('col')
Outputs:
- output: bfloat16 [24, 256, 6144], P(('dp', 'row'), None, 'col')
All inputs are finite; a program needn't handle non-finite values.
Results may differ from a plain program's by a relative error of at most 0.011318.
Values are sent between devices in bfloat16 or wider.
A program may use at most 1 GiB of HBM per device.

v0:
```python
import jax
import jax.numpy as jnp
from jax import lax
from jax.sharding import PartitionSpec as P

NORM_EPS = 1e-6


def layer_norm_rows(values, gain_vec):
    row_mean = jnp.mean(values, axis=-1, keepdims=True)
    row_var = jnp.mean(values * values, axis=-1, keepdims=True) - row_mean * row_mean
    return (values - row_mean) * lax.rsqrt(row_var + NORM_EPS) * gain_vec


def solution(mesh):
    col_size = mesh.shape['col']

    def local_layer(x_loc, ln_scale, w_qkv, q_scale, k_scale, w_out, w_up, b_up, w_down, b_down):
        head_dim = q_scale.shape[0]
        full_width = x_loc.shape[-1] * col_size
        x_f32 = x_loc.astype(jnp.float32)
        ln_stats = jnp.concatenate([jnp.sum(x_f32, axis=-1, keepdims=True), jnp.sum(x_f32 * x_f32, axis=-1, keepdims=True)], axis=-1)
        ln_stats = lax.psum(ln_stats, 'col')
        row_mean = ln_stats[..., 0:1] / full_width
        row_var = ln_stats[..., 1:2] / full_width - row_mean * row_mean
        normed = ((x_f32 - row_mean) * lax.rsqrt(row_var + NORM_EPS) * ln_scale).astype(jnp.bfloat16)
        n_full = lax.all_gather(normed, 'row', axis=0, tiled=True)
        qkv_part = jnp.einsum('bsd,de->bse', n_full, w_qkv, preferred_element_type=jnp.float32).astype(jnp.bfloat16)
        up_part = jnp.einsum('bsd,df->bsf', n_full, w_up, preferred_element_type=jnp.float32).astype(jnp.bfloat16)
        qkv_proj = lax.psum_scatter(qkv_part, 'col', scatter_dimension=0, tiled=True)
        up_proj = lax.psum_scatter(up_part, 'col', scatter_dimension=0, tiled=True)
        img_count, seq_len, qkv_width = qkv_proj.shape
        heads_loc = qkv_width // (3 * head_dim)
        qkv_heads = qkv_proj.reshape(img_count, seq_len, heads_loc, 3, head_dim)
        q_normed = layer_norm_rows(qkv_heads[:, :, :, 0].astype(jnp.float32), q_scale).astype(jnp.bfloat16)
        k_normed = layer_norm_rows(qkv_heads[:, :, :, 1].astype(jnp.float32), k_scale).astype(jnp.bfloat16)
        scores = jnp.einsum('bshd,bthd->bhst', q_normed, k_normed, preferred_element_type=jnp.float32) * head_dim ** -0.5
        attn_prob = jax.nn.softmax(scores, axis=-1).astype(jnp.bfloat16)
        attn_out = jnp.einsum('bhst,bthd->bshd', attn_prob, qkv_heads[:, :, :, 2], preferred_element_type=jnp.float32).astype(jnp.bfloat16).reshape(img_count, seq_len, heads_loc * head_dim)
        gelu_out = jax.nn.gelu(up_proj.astype(jnp.float32) + b_up, approximate=True).astype(jnp.bfloat16)
        attn_full = lax.all_gather(attn_out, 'col', axis=0, tiled=True)
        gelu_full = lax.all_gather(gelu_out, 'col', axis=0, tiled=True)
        out_part = (jnp.einsum('bse,ed->bsd', attn_full, w_out, preferred_element_type=jnp.float32) + jnp.einsum('bsf,fd->bsd', gelu_full, w_down, preferred_element_type=jnp.float32)).astype(jnp.bfloat16)
        out_loc = lax.psum_scatter(out_part, 'row', scatter_dimension=0, tiled=True)
        return (x_f32 + out_loc.astype(jnp.float32) + b_down).astype(jnp.bfloat16)

    x_spec = P(('dp', 'row'), None, 'col')
    return jax.shard_map(local_layer, mesh=mesh,
                         in_specs=(x_spec, P('col'), P('col', 'row'), P(), P(), P('row', 'col'), P('col', 'row'), P('row'), P('row', 'col'), P('col')),
                         out_specs=x_spec, check_vma=False)
```

profile of v0, /device:TPU:0, one launch (start us, length us, event | category | flops | bytes accessed | tf_op | source)
XLA Modules:
  0.0 3643.5 jit_solution(1403057850043685115)
XLA Ops:
  6.5 0.0 all-gather.4.cloned.1.call-start
  6.5 6.4 convert_reduce_fusion
  13.0 13.2 psum.7
  26.2 8.8 fusion.31
  35.0 0.0 all-gather.4.cloned.1.call-update
  35.0 0.3 reduce-scatter.6.cloned.1.call-start
  35.3 221.5 %all-gather.4.cloned.1.call-done = bf16[24,256,1536]{2,1,0:T(8,128)(2,1)} async-done(((bf16[12,256,1536]{2,1,0:T(8,128)(2,1)}), bf16[24,256,1536]{2,1,0:T(8,128)(2,1)}) %all-gather.4.cloned.1.call-update) | async-done | bytes 18874384 | tf_op jit(solution)/shard_map/all_gather | solution.py:27
  256.8 246.7 %convolution_convert_fusion = bf16[24,256,12288]{2,1,0:T(8,128)(2,1)} fusion(bf16[24,256,1536]{2,1,0:T(8,128)(2,1)} %all-gather.4.cloned.1.call-done, bf16[1536,12288]{1,0:T(8,128)(2,1)} %param.16), kind=kOutput, calls=%fused_computation.2 | convolution fusion | flops 232003731456 | bytes 207618048 | tf_op jit(solution)/shard_map/bsd,df->bsf/dot_general | solution.py:29
  503.5 0.0 reduce-scatter.6.cloned.1.call-update
  503.5 0.4 reduce-scatter.4.cloned.1.call-start
  504.0 193.1 %convolution_convert_fusion.1 = bf16[24,256,9216]{2,1,0:T(8,128)(2,1)} fusion(bf16[24,256,1536]{2,1,0:T(8,128)(2,1)} %all-gather.4.cloned.1.call-done, bf16[1536,9216]{1,0:T(8,128)(2,1)} %param.12), kind=kOutput, calls=%fused_computation.11 | convolution fusion | flops 174002798592 | bytes 160432128 | tf_op jit(solution)/shard_map/bsd,de->bse/dot_general | solution.py:28
  697.0 0.0 copy-start
  697.0 0.0 reduce-scatter.4.cloned.1.call-update
  697.1 0.0 all-gather.8.cloned.1.call-start
  697.1 777.5 %reduce-scatter.6.cloned.1.call-done = bf16[6,256,12288]{2,1,0:T(8,128)(2,1)} async-done(((bf16[24,256,12288]{2,1,0:T(8,128)(2,1)}), bf16[6,256,12288]{2,1,0:T(8,128)(2,1)}) %reduce-scatter.6.cloned.1.call-update) | async-done | bytes 37748752 | tf_op jit(solution)/shard_map/reduce_scatter | solution.py:31
  1474.6 0.0 copy-done
  1474.6 31.6 fusion.8
  1506.2 0.0 all-gather.8.cloned.1.call-update
  1506.2 0.2 all-gather.6.cloned.1.call-start
  1506.4 723.8 %reduce-scatter.4.cloned.1.call-done = bf16[6,256,9216]{2,1,0:T(8,128)(2,1)} async-done(((bf16[24,256,9216]{2,1,0:T(8,128)(2,1)}), bf16[6,256,9216]{2,1,0:T(8,128)(2,1)}) %reduce-scatter.4.cloned.1.call-update) | async-done | bytes 28311568 | tf_op jit(solution)/shard_map/reduce_scatter | solution.py:30
  2230.2 40.3 %copy.22 = bf16[6,256,9216]{1,2,0:T(8,128)(2,1)} copy(bf16[6,256,9216]{2,1,0:T(8,128)(2,1)} %reduce-scatter.4.cloned.1.call-done) | data formatting | bytes 56623104 | tf_op jit(solution)/shard_map/reduce_scatter | solution.py:30
  2270.6 0.0 copy-start.1
  2270.6 0.0 copy-start.2
  2270.6 18.2 convert_reduce_fusion.2
  2288.8 13.2 fusion.23
  2302.0 0.1 broadcast_multiply_fusion
  2302.1 0.0 copy-done.1
  2302.1 0.0 copy-done.2
  2302.1 24.6 fusion.36
  2326.7 40.5 %fusion.55 = (f32[6,24,256]{2,1,0:T(8,128)S(1)}, f32[6,24,256,256]{2,3,1,0:T(8,128)}) fusion(f32[6,24,256,256]{2,3,1,0:T(8,128)} %fusion.36), kind=kOutput, calls=%fused_computation.74 | output fusion | flops 37748992 | bytes 75644928 | tf_op jit(solution)/shard_map/sub | solution.py:38
  2367.2 19.6 fusion.48
  2386.8 12.7 copy.27
  2399.5 0.0 all-gather.6.cloned.1.call-update
  2399.5 0.0 reduce-scatter.8.cloned.1.call-start
  2399.6 700.0 %all-gather.8.cloned.1.call-done = bf16[24,256,12288]{2,1,0:T(8,128)(2,1)} async-done(((bf16[6,256,12288]{2,1,0:T(8,128)(2,1)}), bf16[24,256,12288]{2,1,0:T(8,128)(2,1)}) %all-gather.8.cloned.1.call-update) | async-done | bytes 150994960 | tf_op jit(solution)/shard_map/all_gather | solution.py:42
  3099.6 249.1 %fusion.9 = f32[24,256,1536]{2,1,0:T(8,128)} fusion(bf16[24,256,12288]{2,1,0:T(8,128)(2,1)} %all-gather.8.cloned.1.call-done, bf16[12288,1536]{1,0:T(8,128)(2,1)} %param.18), kind=kOutput, calls=%fused_computation.12 | convolution fusion | flops 231928233984 | bytes 226492416 | tf_op jit(solution)/shard_map/bsf,fd->bsd/dot_general | solution.py:43
  3348.7 0.0 all-gather.6.cloned.1.call-done
  3348.7 0.0 copy-start.3
  3348.7 67.9 %add_convert_fusion = bf16[24,256,1536]{2,1,0:T(8,128)(2,1)} fusion(f32[24,256,1536]{2,1,0:T(8,128)} %fusion.9, bf16[24,256,3072]{2,1,0:T(8,128)(2,1)} %all-gather.6.cloned.1.call-done, bf16[3072,1536]{1,0:T(8,128)(2,1)} %param.15), kind=kOutput, calls=%fused_computation.15 | convolution fusion | flops 58000932864 | bytes 103809024 | tf_op jit(solution)/shard_map/bse,ed->bsd/dot_general | solution.py:43
  3416.6 0.0 reduce-scatter.8.cloned.1.call-update
  3416.7 208.8 %reduce-scatter.8.cloned.1.call-done = bf16[12,256,1536]{2,1,0:T(8,128)(2,1)} async-done(((bf16[24,256,1536]{2,1,0:T(8,128)(2,1)}), bf16[12,256,1536]{2,1,0:T(8,128)(2,1)}) %reduce-scatter.8.cloned.1.call-update) | async-done | bytes 9437200 | tf_op jit(solution)/shard_map/reduce_scatter | solution.py:44
  3625.4 0.0 copy-done.3
  3625.4 10.8 fusion.33
  (2 shorter events, 0.0 us)
Async XLA Ops:
  6.5 250.3 %all-gather.4.cloned.1.call-start = ((), (), s32[]{:S(2)}) async-start(), calls=%async_computation.3 | async-start | bytes 28311552 | tf_op jit(solution)/shard_map/all_gather | solution.py:27
  35.0 1439.5 %reduce-scatter.6.cloned.1.call-start = ((), (), s32[]{:S(2)}) async-start(), calls=%async_computation.6 | async-start | bytes 188743680 | tf_op jit(solution)/shard_map/reduce_scatter | solution.py:31
  503.5 1726.7 %reduce-scatter.4.cloned.1.call-start = ((), (), s32[]{:S(2)}) async-start(), calls=%async_computation.4 | async-start | bytes 141557760 | tf_op jit(solution)/shard_map/reduce_scatter | solution.py:30
  697.0 777.6 %copy-start = (f32[12288]{0:T(1024)S(1)}, f32[12288]{0:T(1024)}, u32[]{:S(2)}) copy-start(f32[12288]{0:T(1024)} %param.17) | copy-start | bytes 147460
  697.1 2402.5 %all-gather.8.cloned.1.call-start = ((), (), s32[]{:S(2)}) async-start(), calls=%async_computation.7 | async-start | bytes 188743680 | tf_op jit(solution)/shard_map/all_gather | solution.py:42
  1506.2 1842.5 %all-gather.6.cloned.1.call-start = ((), (), s32[]{:S(2)}) async-start(), calls=%async_computation.5 | async-start | bytes 47185920 | tf_op jit(solution)/shard_map/all_gather | solution.py:41
  2270.6 31.5 copy-start.1
  2270.6 31.5 copy-start.2
  2399.5 1225.9 %reduce-scatter.8.cloned.1.call-start = ((), (), s32[]{:S(2)}) async-start(), calls=%async_computation.8 | async-start | bytes 28311552 | tf_op jit(solution)/shard_map/reduce_scatter | solution.py:44
  3348.7 276.7 %copy-start.3 = (f32[1536]{0:T(1024)S(1)}, f32[1536]{0:T(1024)}, u32[]{:S(2)}) copy-start(f32[1536]{0:T(1024)} %param.19) | copy-start | bytes 18436
Sparse Core Ops, SparseCore 0:
  35.2 221.5 all-gather.3
  503.6 970.9 reduce-scatter.5
  1477.1 753.0 reduce-scatter.3
  2231.6 867.9 all-gather.7
  3101.0 224.3 all-gather.5
  3416.8 208.6 reduce-scatter.7
where the time goes:
time: 3650 us; the launch traced here: 3640 us
  waiting for transfers between devices  2630 us (72%)
  matrix products  801 us (22%)
  other arithmetic  130 us (4%)
  local copies, waits for them, and re-layouts  53.1 us (1%)
    reduce_scatter x1, waiting for transfers between devices, local_layer(): up_proj = lax.psum_scatter(up_part, 'col', scatter_dimension=0, tiled=True)  777 us
    reduce_scatter x1, waiting for transfers between devices, local_layer(): lax.psum_scatter(qkv_part, 'col', scatter_dimension=0, tiled=True)  724 us
    all_gather x1, waiting for transfers between devices, local_layer(): gelu_full = lax.all_gather(gelu_out, 'col', axis=0, tiled=True)  700 us
    dot_general x1, matrix products, local_layer(): jnp.einsum('bsf,fd->bsd', gelu_full, w_down, preferred_element_type=jnp.f...  249 us
    dot_general x1, matrix products, local_layer(): jnp.einsum('bsd,df->bsf', n_full, w_up, preferred_element_type=jnp.float32)  247 us
    all_gather x1, waiting for transfers between devices, local_layer(): n_full = lax.all_gather(normed, 'row', axis=0, tiled=True)  222 us
    reduce_scatter x1, waiting for transfers between devices, local_layer(): out_loc = lax.psum_scatter(out_part, 'row', scatter_dimension=0, tiled=True)  209 us
    dot_general x1, matrix products, local_layer(): jnp.einsum('bsd,de->bse', n_full, w_qkv, preferred_element_type=jnp.float32)  193 us
  transfers between devices with their start and end apart: 6, of which 5 were waited for; matrix products, arithmetic and copies ran while one was open for 18% of the time, Pallas kernels for 0%

commit v1 on v0

v1 whole, which is shorter than its diff:
```python
import functools
import jax
import jax.numpy as jnp
from jax import lax
from jax.experimental import pallas as pl
from jax.experimental.pallas import tpu as pltpu
from jax.sharding import PartitionSpec as P


NORM_EPS = 1e-6
VMEM_LIMIT = 60 * 1024 * 1024
UP_PIECES = 4
OUT_PIECES = (512, 512, 256, 256)
Y_PIECES = 4


def layer_norm_rows(values, gain_vec):
    row_mean = jnp.mean(values, axis=-1, keepdims=True)
    row_var = jnp.mean(values * values, axis=-1, keepdims=True) - row_mean * row_mean
    return (values - row_mean) * lax.rsqrt(row_var + NORM_EPS) * gain_vec


def tile_of(size, want):
    tile = min(size, want)
    while size % tile:
        tile //= 2
    return tile


def normalise_tile(n_blocks, *refs):
    x_refs, gain_refs, out_refs = refs[:n_blocks], refs[n_blocks:2 * n_blocks], refs[2 * n_blocks:]
    full_width = n_blocks * x_refs[0].shape[1]
    total, squares = 0.0, 0.0
    for x_ref in x_refs:
        values = x_ref[...].astype(jnp.float32)
        total = total + jnp.sum(values, axis=-1, keepdims=True)
        squares = squares + jnp.sum(values * values, axis=-1, keepdims=True)
    row_mean = total / full_width
    row_var = squares / full_width - row_mean * row_mean
    inv = lax.rsqrt(row_var + NORM_EPS)
    for x_ref, gain_ref, out_ref in zip(x_refs, gain_refs, out_refs):
        out_ref[...] = ((x_ref[...].astype(jnp.float32) - row_mean) * inv * gain_ref[...]).astype(jnp.bfloat16)


def normalise(x_list, gain_list):
    rows, depth = x_list[0].shape
    n_blocks = len(x_list)
    bm = tile_of(rows, 256)
    row_block = pl.BlockSpec((bm, depth), lambda i: (i, 0))
    return pl.pallas_call(
        functools.partial(normalise_tile, n_blocks),
        out_shape=[jax.ShapeDtypeStruct((rows, depth), jnp.bfloat16)] * n_blocks,
        grid=(rows // bm,),
        in_specs=[row_block] * n_blocks + [pl.BlockSpec((1, depth), lambda i: (0, 0))] * n_blocks,
        out_specs=[row_block] * n_blocks,
        compiler_params=pltpu.CompilerParams(vmem_limit_bytes=VMEM_LIMIT),
        cost_estimate=pl.CostEstimate(flops=600 * rows * depth * n_blocks, bytes_accessed=4 * rows * depth * n_blocks, transcendentals=0),
    )(*x_list, *[g.reshape(1, depth) for g in gain_list])


def block_matmul(n_blocks, with_gelu, *refs):
    n_refs, w_refs = refs[:n_blocks], refs[n_blocks:2 * n_blocks]
    out_ref = refs[-1]
    acc = jnp.dot(n_refs[0][...], w_refs[0][...], preferred_element_type=jnp.float32)
    for n_ref, w_ref in zip(n_refs[1:], w_refs[1:]):
        acc = acc + jnp.dot(n_ref[...], w_ref[...], preferred_element_type=jnp.float32)
    out = acc.astype(jnp.bfloat16)
    if with_gelu:
        bias_ref = refs[2 * n_blocks]
        out = jax.nn.gelu(out.astype(jnp.float32) + bias_ref[...], approximate=True).astype(jnp.bfloat16)
    out_ref[...] = out


def project_in(n_list, w_list, bias):
    rows, depth = n_list[0].shape
    cols = w_list[0].shape[1]
    n_blocks = len(n_list)
    bm, bn = tile_of(rows, 512), 768 if cols % 768 == 0 else tile_of(cols, 512)
    in_specs = [pl.BlockSpec((bm, depth), lambda j, i: (i, 0))] * n_blocks
    in_specs += [pl.BlockSpec((depth, bn), lambda j, i: (0, j))] * n_blocks
    operands = [*n_list, *w_list]
    if bias is not None:
        in_specs.append(pl.BlockSpec((1, bn), lambda j, i: (0, j)))
        operands.append(bias.reshape(1, cols))
    flops = 2 * rows * depth * n_blocks * cols
    return pl.pallas_call(
        functools.partial(block_matmul, n_blocks, bias is not None),
        out_shape=jax.ShapeDtypeStruct((rows, cols), jnp.bfloat16),
        grid=(cols // bn, rows // bm),
        in_specs=in_specs,
        out_specs=pl.BlockSpec((bm, bn), lambda j, i: (i, j)),
        compiler_params=pltpu.CompilerParams(vmem_limit_bytes=VMEM_LIMIT),
        cost_estimate=pl.CostEstimate(flops=flops, bytes_accessed=4 * n_blocks * depth * (rows + cols), transcendentals=0),
    )(*operands)


def out_matmul(n_hidden, n_adds, n_parts, has_res, *refs):
    out_ref = refs[-1]
    hidden_refs, w_ref = refs[:n_hidden], refs[n_hidden]
    rest = refs[n_hidden + 1:-1]
    acc, start = None, 0
    for h_ref in hidden_refs:
        stop = start + h_ref.shape[1]
        term = jnp.dot(h_ref[...], w_ref[start:stop], preferred_element_type=jnp.float32)
        acc = term if acc is None else acc + term
        start = stop
    for add_ref in rest[:n_adds]:
        acc = acc + add_ref[...].astype(jnp.float32)
    rest = rest[n_adds:]
    if has_res:
        acc = rest[n_parts][...].astype(jnp.float32) + acc + rest[n_parts + 1][...]
    if not n_parts:
        out_ref[...] = acc.astype(out_ref.dtype)
    start = 0
    for part_ref in rest[:n_parts]:
        stop = start + part_ref.shape[1]
        out_ref[:, start:stop] = (acc[:, start:stop] + part_ref[...].astype(jnp.float32)).astype(out_ref.dtype)
        start = stop


def project_out(hidden, w, adds, parts=(), residual=None, bias=None, window=(0, 1)):
    rows = hidden[0].shape[0]
    index, count = window
    depth, cols = w.shape[0], w.shape[1] // count
    bm = tile_of(rows, 512)
    row_block = lambda width: pl.BlockSpec((bm, width), lambda i: (i, 0))
    in_specs = [row_block(h.shape[1]) for h in hidden] + [pl.BlockSpec((depth, cols), lambda i: (0, index))]
    in_specs += [pl.BlockSpec((bm, cols), lambda i: (i, index))] * len(adds)
    in_specs += [row_block(p.shape[1]) for p in parts]
    operands = [*hidden, w, *adds, *parts]
    out_type = jnp.bfloat16
    if residual is not None:
        in_specs += [row_block(cols), pl.BlockSpec((1, cols), lambda i: (0, 0))]
        operands += [residual, bias.reshape(1, cols)]
        out_type = jnp.float32
    return pl.pallas_call(
        functools.partial(out_matmul, len(hidden), len(adds), len(parts), residual is not None),
        out_shape=jax.ShapeDtypeStruct((rows, cols), out_type),
        grid=(rows // bm,),
        in_specs=in_specs,
        out_specs=row_block(cols),
        compiler_params=pltpu.CompilerParams(vmem_limit_bytes=VMEM_LIMIT),
        cost_estimate=pl.CostEstimate(flops=2 * rows * depth * cols, bytes_accessed=2 * (rows + cols) * depth, transcendentals=0),
    )(*operands)


def add_parts(main_ref, *refs):
    out_ref, start = refs[-1], 0
    for part_ref in refs[:-1]:
        stop = start + part_ref.shape[1]
        out_ref[:, start:stop] = (main_ref[:, start:stop] + part_ref[...].astype(jnp.float32)).astype(out_ref.dtype)
        start = stop


def add_last(main_ref, part_ref, held_ref, out_ref):
    out_ref[...] = (main_ref[...] + part_ref[...].astype(jnp.float32)).astype(out_ref.dtype)


def join_parts(main, parts):
    rows, cols = main.shape
    bm = tile_of(rows, 512)
    row_block = lambda width: pl.BlockSpec((bm, width), lambda i: (i, 0))
    return pl.pallas_call(
        add_parts,
        out_shape=jax.ShapeDtypeStruct((rows, cols), jnp.bfloat16),
        grid=(rows // bm,),
        in_specs=[row_block(cols)] + [row_block(p.shape[1]) for p in parts],
        out_specs=row_block(cols),
        compiler_params=pltpu.CompilerParams(vmem_limit_bytes=VMEM_LIMIT),
        cost_estimate=pl.CostEstimate(flops=2 * rows * cols, bytes_accessed=8 * rows * cols, transcendentals=0),
    )(main, *parts)


def join_last(main, part, held):
    rows, cols = main.shape
    size = part.shape[1]
    bm = tile_of(rows, 1024)
    last = cols // size - 1
    tail_block = pl.BlockSpec((bm, size), lambda i: (i, last))
    return pl.pallas_call(
        add_last,
        out_shape=jax.ShapeDtypeStruct((rows, cols), jnp.bfloat16),
        grid=(rows // bm,),
        in_specs=[tail_block, pl.BlockSpec((bm, size), lambda i: (i, 0)), pl.BlockSpec(memory_space=pl.ANY)],
        out_specs=tail_block,
        input_output_aliases={2: 0},
        compiler_params=pltpu.CompilerParams(vmem_limit_bytes=VMEM_LIMIT),
        cost_estimate=pl.CostEstimate(flops=2 * rows * size, bytes_accessed=8 * rows * size, transcendentals=0),
    )(main, part, held)


def attend(head_dim, qs_ref, ks_ref, *refs):
    out_ref, done = refs[-1], 0
    for qkv_ref in refs[:-1]:
        for base in range(0, qkv_ref.shape[1], 3 * head_dim):
            q = layer_norm_rows(qkv_ref[:, base:base + head_dim].astype(jnp.float32), qs_ref[...]).astype(jnp.bfloat16)
            k = layer_norm_rows(qkv_ref[:, base + head_dim:base + 2 * head_dim].astype(jnp.float32), ks_ref[...]).astype(jnp.bfloat16)
            v = qkv_ref[:, base + 2 * head_dim:base + 3 * head_dim]
            s = lax.dot_general(q, k, (((1,), (1,)), ((), ())), preferred_element_type=jnp.float32) * head_dim ** -0.5
            e = jnp.exp(s - jnp.max(s, axis=-1, keepdims=True))
            p = (e / jnp.sum(e, axis=-1, keepdims=True)).astype(jnp.bfloat16)
            out_ref[:, done:done + head_dim] = jnp.dot(p, v, preferred_element_type=jnp.float32).astype(jnp.bfloat16)
            done += head_dim


def attention(qkv_list, q_scale, k_scale, seq_len):
    rows = qkv_list[0].shape[0]
    widths = [q.shape[1] for q in qkv_list]
    head_dim = q_scale.shape[0]
    out_width = sum(widths) // 3
    scale_spec = pl.BlockSpec((1, head_dim), lambda i: (0, 0))
    flops = 4 * rows * seq_len * out_width
    return pl.pallas_call(
        functools.partial(attend, head_dim),
        out_shape=jax.ShapeDtypeStruct((rows, out_width), jnp.bfloat16),
        grid=(rows // seq_len,),
        in_specs=[scale_spec, scale_spec] + [pl.BlockSpec((seq_len, w), lambda i: (i, 0)) for w in widths],
        out_specs=pl.BlockSpec((seq_len, out_width), lambda i: (i, 0)),
        compiler_params=pltpu.CompilerParams(vmem_limit_bytes=VMEM_LIMIT),
        cost_estimate=pl.CostEstimate(flops=8 * flops, bytes_accessed=2 * rows * sum(widths), transcendentals=0),
    )(q_scale.reshape(1, head_dim), k_scale.reshape(1, head_dim), *qkv_list)


def solution(mesh):
    col_size = mesh.shape['col']
    row_size = mesh.shape['row']

    def partner(arr, shift):
        return lax.ppermute(arr, 'col', [(i, i ^ shift) for i in range(col_size)])

    def over_row(arr):
        return lax.ppermute(arr, 'row', [(i, i ^ 1) for i in range(row_size)])

    def layer(x_loc, ln_scale, w_qkv, q_scale, k_scale, w_out, w_up, b_up, w_down, b_down):
        col = lax.axis_index('col')
        imgs, seq_len, width = x_loc.shape
        x_rows = x_loc.reshape(imgs * seq_len, width)

        def piece_cols(w, shift, start, size):
            span = w.shape[1] // col_size
            return lax.dynamic_slice(w, (0, (col ^ shift) * span + start), (w.shape[0], size))

        def piece_rows(w, shift, start, size):
            span = w.shape[0] // col_size
            return lax.dynamic_slice(w, ((col ^ shift) * span, start), (span, size))

        def in_weights(w, start, size):
            return [piece_cols(w, 0, start, size)] + [
                partner(piece_cols(w, s, start, size), s) for s in (1, 2, 3)]

        def out_piece(shift, start, size):
            return jnp.concatenate([piece_rows(w_out, shift, start, size), piece_rows(w_down, shift, start, size)], axis=0)

        gains = [ln_scale] + [partner(ln_scale, s) for s in (1, 2, 3)]
        x1 = partner(x_rows, 1)
        x2 = partner(x_rows, 2)
        z0 = over_row(x_rows)
        x3 = partner(x2, 1)
        z2 = over_row(x2)
        z1 = partner(z0, 1)
        z3 = partner(z2, 1)
        own = normalise([x_rows, x1, x2, x3], gains)
        oth = normalise([z0, z1, z2, z3], gains)

        head_cols = 3 * q_scale.shape[0]
        qkv_cols = w_qkv.shape[1] // col_size
        up_cols = w_up.shape[1] // col_size
        qkv_step, up_step = 2 * head_cols, up_cols // UP_PIECES
        qkv_own, qkv_oth, g_own, g_oth = [], [], [], []
        for i in range(qkv_cols // qkv_step):
            w = in_weights(w_qkv, i * qkv_step, qkv_step)
            qkv_own.append(project_in(own, w, None))
            qkv_oth.append(project_in(oth, w, None))
        attn_own = attention(qkv_own, q_scale, k_scale, seq_len)
        attn_oth = attention(qkv_oth, q_scale, k_scale, seq_len)
        for i in range(UP_PIECES):
            w = in_weights(w_up, i * up_step, up_step)
            bias = lax.dynamic_slice(b_up, (col * up_cols + i * up_step,), (up_step,))
            g_own.append(project_in(own, w, bias))
            g_oth.append(project_in(oth, w, bias))
        hid_own, hid_oth = [attn_own, *g_own], [attn_oth, *g_oth]

        out_cols = w_out.shape[1]
        wo_0 = out_piece(0, 0, out_cols)
        wo_1 = partner(out_piece(1, 0, out_cols), 1)
        d1_oth = partner(project_out(hid_oth, wo_1, []), 1)
        d1_own = partner(project_out(hid_own, wo_1, []), 1)
        y0 = [over_row(project_out(hid_oth, wo_0, [d1_oth], window=(i, Y_PIECES))) for i in range(Y_PIECES)]
        x_parts, start = [], 0
        for size in OUT_PIECES:
            wo_3 = partner(out_piece(3, start, size), 3)
            wo_2 = partner(out_piece(2, start, size), 2)
            d3_oth = partner(project_out(hid_oth, wo_3, []), 1)
            d3_own = partner(project_out(hid_own, wo_3, []), 1)
            y2 = over_row(project_out(hid_oth, wo_2, [d3_oth]))
            x_parts.append(partner(project_out(hid_own, wo_2, [d3_own, y2]), 2))
            start += size
        main = project_out(hid_own, wo_0, [d1_own], parts=y0, residual=x_rows, bias=b_down)
        out = join_last(main, x_parts[-1], join_parts(main, x_parts[:-1]))
        return out.reshape(imgs, seq_len, width)

    x_spec = P(('dp', 'row'), None, 'col')
    return jax.shard_map(layer, mesh=mesh,
                         in_specs=(x_spec, P('col'), P('col', 'row'), P(), P(), P('row', 'col'), P('col', 'row'), P('row'), P('row', 'col'), P('col')),
                         out_specs=x_spec, check_vma=False)
```

time: 3650 us -> 2200 us (0.60)
  waiting for transfers between devices: 2630 us -> 876 us
  Pallas kernels: 0 us -> 1150 us
  matrix products: 801 us -> 0 us
  other arithmetic: 130 us -> 28.7 us
  starting transfers between devices: 1 us -> 57.1 us
    reduce_scatter x3 -> x0, waiting for transfers between devices: 1710 us -> none  [the longest x1 777 us: local_layer(): up_proj = lax.psum_scatter(up_part, 'col', scatter_dimension=0, tiled=True)]
    pallas_call x0 -> x43, Pallas kernels: none -> 1150 us  [the longest x14 542 us: project_in(): pl.pallas_call(functools.partial(block_matmul, n_blocks, bias is not None...]
    all_gather x3 -> x0, waiting for transfers between devices: 921 us -> none  [the longest x1 700 us: local_layer(): gelu_full = lax.all_gather(gelu_out, 'col', axis=0, tiled=True)]
    ppermute x0 -> x62, waiting for transfers between devices: none -> 876 us  [the longest x52 639 us: partner(): return lax.ppermute(arr, 'col', [(i, i ^ shift) for i in range(col_size)])]
    dot_general x6 -> x0, matrix products: 801 us -> none  [the longest x1 249 us: local_layer(): jnp.einsum('bsf,fd->bsd', gelu_full, w_down, preferred_element_type=jnp.f...]
    dynamic_slice x0 -> x9, local copies, waits for them, and re-layouts: none -> 73.1 us  [the longest x2 44.5 us: piece_cols(): lax.dynamic_slice(w, (0, (col ^ shift) * span + start), (w.shape[0], size))]
    ppermute x0 -> x62, starting transfers between devices: none -> 57.1 us  [the longest x52 44.3 us: partner(): return lax.ppermute(arr, 'col', [(i, i ^ shift) for i in range(col_size)])]
    convert_element_type x3 -> x0, other arithmetic: 51.2 us -> none  [the longest x1 31.6 us: local_layer(): jax.nn.gelu(up_proj.astype(jnp.float32) + b_up, approximate=True)]
  transfers between devices with their start and end apart: 6 -> 62, of which waited for: 5 -> 23; matrix products, arithmetic and copies ran while one was open for 18% -> 5% of each run, Pallas kernels for 0% -> 52%
where the time goes in v1:
time: 2200 us; the launch traced here: 2190 us
  Pallas kernels  1150 us (52%)
  waiting for transfers between devices  876 us (40%)
  local copies, waits for them, and re-layouts  79 us (4%)
  starting transfers between devices  57.1 us (3%)
  other arithmetic  28.7 us (1%)
    ppermute x52, waiting for transfers between devices, partner(): return lax.ppermute(arr, 'col', [(i, i ^ shift) for i in range(col_size)])  639 us
    pallas_call x14, Pallas kernels, project_in(): pl.pallas_call(functools.partial(block_matmul, n_blocks, bias is not None...  542 us
    pallas_call x23, Pallas kernels, project_out(): pl.pallas_call(functools.partial(out_matmul, len(hidden), len(adds), len(...  471 us
    ppermute x10, waiting for transfers between devices, over_row(): return lax.ppermute(arr, 'row', [(i, i ^ 1) for i in range(row_size)])  237 us
    pallas_call x2, Pallas kernels, normalise(): pl.pallas_call(functools.partial(normalise_tile, n_blocks), out_shape=[ja...  71.8 us
    pallas_call x2, Pallas kernels, attention(): pl.pallas_call(functools.partial(attend, head_dim), out_shape=jax.ShapeDt...  47.7 us
    dynamic_slice x2, local copies, waits for them, and re-layouts, piece_cols(): lax.dynamic_slice(w, (0, (col ^ shift) * span + start), (w.shape[0], size))  44.5 us
    ppermute x52, starting transfers between devices, partner(): return lax.ppermute(arr, 'col', [(i, i ^ shift) for i in range(col_size)])  44.3 us
  transfers between devices with their start and end apart: 62, of which 23 were waited for; matrix products, arithmetic and copies ran while one was open for 5% of the time, Pallas kernels for 52%

profile of v1, /device:TPU:0, one launch (start us, length us, event | category | flops | bytes accessed | tf_op | source)
XLA Modules:
  0.0 2190.7 jit_solution(2706296935370614602)
XLA Ops:
  25.9 180.9 %collective-permute-done.1.refs_2_ = bf16[3072,1536]{1,0:T(8,128)(2,1)} collective-permute-done((bf16[3072,1536]{1,0:T(8,128)(2,1)}, bf16[3072,1536]{1,0:T(8,128)(2,1)}, u32[]{:S(2)}, u32[]{:S(2)}) %collective-permute-start.1) | collective-permute-done | bytes 9437216 | tf_op jit(solution)/shard_map/ppermute | solution.py:229
  216.7 19.2 constant_dynamic-slice_fusion.24
  235.9 11.6 constant_dynamic-slice_fusion.4
  252.7 25.3 %constant_dynamic-slice_fusion.8 = (bf16[1536,768]{1,0:T(8,128)(2,1)}, bf16[1536,768]{1,0:T(8,128)(2,1)}, bf16[1536,768]{1,0:T(8,128)(2,1)}, bf16[1536,768]{1,0:...) fusion(bf16[1536,12288]{1,0:T(8,128)(2,1)} %param.16, ...), kind=kLoop, calls=%fused_computation.18 | loop fusion | bytes 75497536 | tf_op jit(solution)/shard_map/dynamic_slice | solution.py:241
  297.6 35.9 %shard_map.100 = (bf16[3072,1536]{1,0:T(8,128)(2,1)}, bf16[3072,1536]{1,0:T(8,128)(2,1)}, bf16[3072,1536]{1,0:T(8,128)(2,1)}, bf16[3072,1536]{1,0:T(8,128)(2,1)}) custom-call(bf16[3072,1536]{1,0:T(8,128)(2,1)} %bitcast.6, bf16[3072,1536]{1,0:T(8,128)(2,1)} %collective-permute-done.refs_1_, bf16[3072,1536]{1,0:T(8,128)(2,1)} %collective-permute-done.1.refs_2_, ...), custom_call_target="tpu_custom_call" | custom-call | flops 11324620800 | bytes 75497472 | tf_op jit(solution)/shard_map/pallas_call | solution.py:50
  337.9 49.3 %collective-permute-done.14.refs_7_ = bf16[1536,768]{1,0:T(8,128)(2,1)} collective-permute-done((bf16[1536,768]{1,0:T(8,128)(2,1)}, bf16[1536,768]{1,0:T(8,128)(2,1)}, u32[]{:S(2)}, u32[]{:S(2)}) %collective-permute-start.14) | collective-permute-done | bytes 2359328 | tf_op jit(solution)/shard_map/ppermute | solution.py:229
  387.8 37.5 %shard_map.103.refs_2_ = bf16[3072,768]{1,0:T(8,128)(2,1)} custom-call(bf16[3072,1536]{1,0:T(8,128)(2,1)} %get-tuple-element.13.refs_0_, bf16[3072,1536]{1,0:T(8,128)(2,1)} %get-tuple-element.14.refs_1_, bf16[3072,1536]{1,0:T(8,128)(2,1)} %get-tuple-element.15.refs_2_, bf16[3072,1536]{1,0:T(8,128)(2,1)} %get-tuple-element.16.refs_3_, ...), custom_call_target="tpu_custom_call" | custom-call | flops 28991029248 | bytes 94371840 | tf_op jit(solution)/shard_map/pallas_call | solution.py:86
  425.2 13.3 collective-permute-done.25.refs_6_
  440.3 48.0 %collective-permute-done.26.refs_7_ = bf16[1536,768]{1,0:T(8,128)(2,1)} collective-permute-done((bf16[1536,768]{1,0:T(8,128)(2,1)}, bf16[1536,768]{1,0:T(8,128)(2,1)}, u32[]{:S(2)}, u32[]{:S(2)}) %collective-permute-start.26) | collective-permute-done | bytes 2359328 | tf_op jit(solution)/shard_map/ppermute | solution.py:229
  489.2 50.4 %collective-permute-done.10.refs_6_ = bf16[1536,768]{1,0:T(8,128)(2,1)} collective-permute-done((bf16[1536,768]{1,0:T(8,128)(2,1)}, bf16[1536,768]{1,0:T(8,128)(2,1)}, u32[]{:S(2)}, u32[]{:S(2)}) %collective-permute-start.10) | collective-permute-done | bytes 2359328 | tf_op jit(solution)/shard_map/ppermute | solution.py:229
  541.4 48.1 %collective-permute-done.11.refs_7_ = bf16[1536,768]{1,0:T(8,128)(2,1)} collective-permute-done((bf16[1536,768]{1,0:T(8,128)(2,1)}, bf16[1536,768]{1,0:T(8,128)(2,1)}, u32[]{:S(2)}, u32[]{:S(2)}) %collective-permute-start.11) | collective-permute-done | bytes 2359328 | tf_op jit(solution)/shard_map/ppermute | solution.py:229
  593.2 37.6 %shard_map.102.refs_1_ = bf16[3072,768]{1,0:T(8,128)(2,1)} custom-call(bf16[3072,1536]{1,0:T(8,128)(2,1)} %get-tuple-element.13.refs_0_, bf16[3072,1536]{1,0:T(8,128)(2,1)} %get-tuple-element.14.refs_1_, bf16[3072,1536]{1,0:T(8,128)(2,1)} %get-tuple-element.15.refs_2_, bf16[3072,1536]{1,0:T(8,128)(2,1)} %get-tuple-element.16.refs_3_, ...), custom_call_target="tpu_custom_call" | custom-call | flops 28991029248 | bytes 94371840 | tf_op jit(solution)/shard_map/pallas_call | solution.py:86
  630.8 10.0 collective-permute-done.7.refs_6_
  642.5 48.0 %collective-permute-done.8.refs_7_ = bf16[1536,768]{1,0:T(8,128)(2,1)} collective-permute-done((bf16[1536,768]{1,0:T(8,128)(2,1)S(1)}, bf16[1536,768]{1,0:T(8,128)(2,1)}, u32[]{:S(2)}, u32[]{:S(2)}) %collective-permute-start.8) | collective-permute-done | bytes 2359328 | tf_op jit(solution)/shard_map/ppermute | solution.py:229
  692.8 37.3 %shard_map.101.refs_0_ = bf16[3072,768]{1,0:T(8,128)(2,1)} custom-call(bf16[3072,1536]{1,0:T(8,128)(2,1)} %get-tuple-element.13.refs_0_, bf16[3072,1536]{1,0:T(8,128)(2,1)} %get-tuple-element.14.refs_1_, bf16[3072,1536]{1,0:T(8,128)(2,1)} %get-tuple-element.15.refs_2_, bf16[3072,1536]{1,0:T(8,128)(2,1)} %get-tuple-element.16.refs_3_, ...), custom_call_target="tpu_custom_call" | custom-call | flops 28991029248 | bytes 94371840 | tf_op jit(solution)/shard_map/pallas_call | solution.py:86
  730.1 11.8 collective-permute-done.22.refs_6_
  743.6 48.1 %collective-permute-done.23.refs_7_ = bf16[1536,768]{1,0:T(8,128)(2,1)S(1)} collective-permute-done((bf16[1536,768]{1,0:T(8,128)(2,1)}, bf16[1536,768]{1,0:T(8,128)(2,1)S(1)}, u32[]{:S(2)}, u32[]{:S(2)}) %collective-permute-start.23) | collective-permute-done | bytes 2359328 | tf_op jit(solution)/shard_map/ppermute | solution.py:229
  793.1 39.7 %shard_map.108.refs_4_ = bf16[3072,768]{1,0:T(8,128)(2,1)} custom-call(bf16[3072,1536]{1,0:T(8,128)(2,1)} %get-tuple-element.13.refs_0_, bf16[3072,1536]{1,0:T(8,128)(2,1)} %get-tuple-element.14.refs_1_, bf16[3072,1536]{1,0:T(8,128)(2,1)} %get-tuple-element.15.refs_2_, bf16[3072,1536]{1,0:T(8,128)(2,1)} %get-tuple-element.16.refs_3_, ...), custom_call_target="tpu_custom_call" | custom-call | flops 28991029248 | bytes 94371840 | tf_op jit(solution)/shard_map/pallas_call | solution.py:86
  843.0 39.9 %shard_map.107.refs_3_ = bf16[3072,768]{1,0:T(8,128)(2,1)} custom-call(bf16[3072,1536]{1,0:T(8,128)(2,1)} %get-tuple-element.13.refs_0_, bf16[3072,1536]{1,0:T(8,128)(2,1)} %get-tuple-element.14.refs_1_, bf16[3072,1536]{1,0:T(8,128)(2,1)} %get-tuple-element.15.refs_2_, bf16[3072,1536]{1,0:T(8,128)(2,1)} %get-tuple-element.16.refs_3_, ...), custom_call_target="tpu_custom_call" | custom-call | flops 28991029248 | bytes 94371840 | tf_op jit(solution)/shard_map/pallas_call | solution.py:86
  882.9 9.7 collective-permute-done.20.refs_7_
  894.9 39.6 %shard_map.106.refs_2_ = bf16[3072,768]{1,0:T(8,128)(2,1)} custom-call(bf16[3072,1536]{1,0:T(8,128)(2,1)} %get-tuple-element.13.refs_0_, bf16[3072,1536]{1,0:T(8,128)(2,1)} %get-tuple-element.14.refs_1_, bf16[3072,1536]{1,0:T(8,128)(2,1)} %get-tuple-element.15.refs_2_, bf16[3072,1536]{1,0:T(8,128)(2,1)} %get-tuple-element.16.refs_3_, ...), custom_call_target="tpu_custom_call" | custom-call | flops 28991029248 | bytes 94371840 | tf_op jit(solution)/shard_map/pallas_call | solution.py:86
  934.4 12.6 collective-permute-done.16.refs_6_
  947.1 23.8 %shard_map.104.refs_0_ = bf16[3072,768]{1,0:T(8,128)(2,1)} custom-call(f32[1,128]{1,0:T(1,128)} %bitcast.9, f32[1,128]{1,0:T(1,128)} %bitcast.11, bf16[3072,768]{1,0:T(8,128)(2,1)} %shard_map.101.refs_0_, bf16[3072,768]{1,0:T(8,128)(2,1)} %shard_map.102.refs_1_, bf16[3072,768]{1,0:T(8,128)(2,1)} %shard_map.103.refs_2_), custom_call_target="tpu_custom_call" | custom-call | flops 19327352832 | bytes 14155776 | tf_op jit(solution)/shard_map/pallas_call | solution.py:213
  971.0 25.9 %collective-permute-done.17.refs_7_ = bf16[1536,768]{1,0:T(8,128)(2,1)} collective-permute-done((bf16[1536,768]{1,0:T(8,128)(2,1)}, bf16[1536,768]{1,0:T(8,128)(2,1)}, u32[]{:S(2)}, u32[]{:S(2)}) %collective-permute-start.17) | collective-permute-done | bytes 2359328 | tf_op jit(solution)/shard_map/ppermute | solution.py:229
  999.0 39.6 %shard_map.105.refs_1_ = bf16[3072,768]{1,0:T(8,128)(2,1)} custom-call(bf16[3072,1536]{1,0:T(8,128)(2,1)} %get-tuple-element.13.refs_0_, bf16[3072,1536]{1,0:T(8,128)(2,1)} %get-tuple-element.14.refs_1_, bf16[3072,1536]{1,0:T(8,128)(2,1)} %get-tuple-element.15.refs_2_, bf16[3072,1536]{1,0:T(8,128)(2,1)} %get-tuple-element.16.refs_3_, ...), custom_call_target="tpu_custom_call" | custom-call | flops 28991029248 | bytes 94371840 | tf_op jit(solution)/shard_map/pallas_call | solution.py:86
  1038.6 42.4 %collective-permute-done.51.refs_5_ = bf16[3840,512]{1,0:T(8,128)(2,1)} collective-permute-done((bf16[3840,512]{1,0:T(8,128)(2,1)S(1)}, bf16[3840,512]{1,0:T(8,128)(2,1)}, u32[]{:S(2)}, u32[]{:S(2)}) %collective-permute-start.51) | collective-permute-done | bytes 3932192 | tf_op jit(solution)/shard_map/ppermute | solution.py:229
  1082.2 18.0 shard_map.133
  1101.0 44.9 %shard_map.109 = bf16[3072,1536]{1,0:T(8,128)(2,1)} custom-call(bf16[3072,768]{1,0:T(8,128)(2,1)} %shard_map.104.refs_0_, bf16[3072,768]{1,0:T(8,128)(2,1)} %shard_map.105.refs_1_, bf16[3072,768]{1,0:T(8,128)(2,1)} %shard_map.106.refs_2_, bf16[3072,768]{1,0:T(8,128)(2,1)} %shard_map.107.refs_3_, bf16[3072,768]{1,0:T(8,128)(2,1)} %shard_map.108.refs_4_, ...), custom_call_target="tpu_custom_call" | custom-call | flops 36238786560 | bytes 35389440 | tf_op jit(solution)/shard_map/pallas_call | solution.py:136
  1147.7 35.8 %shard_map.110 = (bf16[3072,1536]{1,0:T(8,128)(2,1)}, bf16[3072,1536]{1,0:T(8,128)(2,1)}, bf16[3072,1536]{1,0:T(8,128)(2,1)}, bf16[3072,1536]{1,0:T(8,128)(2,1)}) custom-call(bf16[3072,1536]{1,0:T(8,128)(2,1)} %collective-permute-done.29.refs_0_, bf16[3072,1536]{1,0:T(8,128)(2,1)} %collective-permute-done.30.refs_1_, ...), custom_call_target="tpu_custom_call" | custom-call | flops 11324620800 | bytes 75497472 | tf_op jit(solution)/shard_map/pallas_call | solution.py:50
  1183.5 39.8 %shard_map.118.refs_4_ = bf16[3072,768]{1,0:T(8,128)(2,1)} custom-call(bf16[3072,1536]{1,0:T(8,128)(2,1)} %get-tuple-element.17.refs_0_, bf16[3072,1536]{1,0:T(8,128)(2,1)} %get-tuple-element.18.refs_1_, bf16[3072,1536]{1,0:T(8,128)(2,1)} %get-tuple-element.19.refs_2_, bf16[3072,1536]{1,0:T(8,128)(2,1)} %get-tuple-element.20.refs_3_, ...), custom_call_target="tpu_custom_call" | custom-call | flops 28991029248 | bytes 94371840 | tf_op jit(solution)/shard_map/pallas_call | solution.py:86
  1223.3 39.5 %shard_map.117.refs_3_ = bf16[3072,768]{1,0:T(8,128)(2,1)} custom-call(bf16[3072,1536]{1,0:T(8,128)(2,1)} %get-tuple-element.17.refs_0_, bf16[3072,1536]{1,0:T(8,128)(2,1)} %get-tuple-element.18.refs_1_, bf16[3072,1536]{1,0:T(8,128)(2,1)} %get-tuple-element.19.refs_2_, bf16[3072,1536]{1,0:T(8,128)(2,1)} %get-tuple-element.20.refs_3_, ...), custom_call_target="tpu_custom_call" | custom-call | flops 28991029248 | bytes 94371840 | tf_op jit(solution)/shard_map/pallas_call | solution.py:86
  1262.8 39.5 %shard_map.116.refs_2_ = bf16[3072,768]{1,0:T(8,128)(2,1)} custom-call(bf16[3072,1536]{1,0:T(8,128)(2,1)} %get-tuple-element.17.refs_0_, bf16[3072,1536]{1,0:T(8,128)(2,1)} %get-tuple-element.18.refs_1_, bf16[3072,1536]{1,0:T(8,128)(2,1)} %get-tuple-element.19.refs_2_, bf16[3072,1536]{1,0:T(8,128)(2,1)} %get-tuple-element.20.refs_3_, ...), custom_call_target="tpu_custom_call" | custom-call | flops 28991029248 | bytes 94371840 | tf_op jit(solution)/shard_map/pallas_call | solution.py:86
  1302.3 39.8 %shard_map.115.refs_1_ = bf16[3072,768]{1,0:T(8,128)(2,1)} custom-call(bf16[3072,1536]{1,0:T(8,128)(2,1)} %get-tuple-element.17.refs_0_, bf16[3072,1536]{1,0:T(8,128)(2,1)} %get-tuple-element.18.refs_1_, bf16[3072,1536]{1,0:T(8,128)(2,1)} %get-tuple-element.19.refs_2_, bf16[3072,1536]{1,0:T(8,128)(2,1)} %get-tuple-element.20.refs_3_, ...), custom_call_target="tpu_custom_call" | custom-call | flops 28991029248 | bytes 94371840 | tf_op jit(solution)/shard_map/pallas_call | solution.py:86
  1342.1 37.4 %shard_map.113.refs_2_ = bf16[3072,768]{1,0:T(8,128)(2,1)} custom-call(bf16[3072,1536]{1,0:T(8,128)(2,1)} %get-tuple-element.17.refs_0_, bf16[3072,1536]{1,0:T(8,128)(2,1)} %get-tuple-element.18.refs_1_, bf16[3072,1536]{1,0:T(8,128)(2,1)} %get-tuple-element.19.refs_2_, bf16[3072,1536]{1,0:T(8,128)(2,1)} %get-tuple-element.20.refs_3_, ...), custom_call_target="tpu_custom_call" | custom-call | flops 28991029248 | bytes 94371840 | tf_op jit(solution)/shard_map/pallas_call | solution.py:86
  1379.6 37.3 %shard_map.112.refs_1_ = bf16[3072,768]{1,0:T(8,128)(2,1)} custom-call(bf16[3072,1536]{1,0:T(8,128)(2,1)} %get-tuple-element.17.refs_0_, bf16[3072,1536]{1,0:T(8,128)(2,1)} %get-tuple-element.18.refs_1_, bf16[3072,1536]{1,0:T(8,128)(2,1)} %get-tuple-element.19.refs_2_, bf16[3072,1536]{1,0:T(8,128)(2,1)} %get-tuple-element.20.refs_3_, ...), custom_call_target="tpu_custom_call" | custom-call | flops 28991029248 | bytes 94371840 | tf_op jit(solution)/shard_map/pallas_call | solution.py:86
  1416.9 37.5 %shard_map.111.refs_0_ = bf16[3072,768]{1,0:T(8,128)(2,1)} custom-call(bf16[3072,1536]{1,0:T(8,128)(2,1)} %get-tuple-element.17.refs_0_, bf16[3072,1536]{1,0:T(8,128)(2,1)} %get-tuple-element.18.refs_1_, bf16[3072,1536]{1,0:T(8,128)(2,1)} %get-tuple-element.19.refs_2_, bf16[3072,1536]{1,0:T(8,128)(2,1)} %get-tuple-element.20.refs_3_, ...), custom_call_target="tpu_custom_call" | custom-call | flops 28991029248 | bytes 94371840 | tf_op jit(solution)/shard_map/pallas_call | solution.py:86
  1454.4 23.8 %shard_map.114.refs_0_ = bf16[3072,768]{1,0:T(8,128)(2,1)} custom-call(f32[1,128]{1,0:T(1,128)} %bitcast.10, f32[1,128]{1,0:T(1,128)} %bitcast.12, bf16[3072,768]{1,0:T(8,128)(2,1)} %shard_map.111.refs_0_, bf16[3072,768]{1,0:T(8,128)(2,1)} %shard_map.112.refs_1_, bf16[3072,768]{1,0:T(8,128)(2,1)} %shard_map.113.refs_2_), custom_call_target="tpu_custom_call" | custom-call | flops 19327352832 | bytes 14155776 | tf_op jit(solution)/shard_map/pallas_call | solution.py:213
  1478.3 45.0 %shard_map.119 = bf16[3072,1536]{1,0:T(8,128)(2,1)} custom-call(bf16[3072,768]{1,0:T(8,128)(2,1)} %shard_map.114.refs_0_, bf16[3072,768]{1,0:T(8,128)(2,1)} %shard_map.115.refs_1_, bf16[3072,768]{1,0:T(8,128)(2,1)} %shard_map.116.refs_2_, bf16[3072,768]{1,0:T(8,128)(2,1)} %shard_map.117.refs_3_, bf16[3072,768]{1,0:T(8,128)(2,1)} %shard_map.118.refs_4_, ...), custom_call_target="tpu_custom_call" | custom-call | flops 36238786560 | bytes 35389440 | tf_op jit(solution)/shard_map/pallas_call | solution.py:136
  1523.6 18.1 shard_map.129
  1543.3 13.6 shard_map.137
  1557.4 18.0 shard_map.134
  1575.4 13.5 shard_map.138
  1589.4 13.7 shard_map.126
  1603.6 18.0 shard_map.130
  1621.6 13.5 shard_map.125
  1635.1 14.1 shard_map.139
  1649.2 21.7 collective-permute-done.44.refs_5_
  1673.1 14.0 shard_map.127
  1687.1 18.8 shard_map.135
  1708.1 14.4 shard_map.140
  1723.0 18.7 shard_map.131
  1743.8 18.0 shard_map.123
  1761.8 18.1 shard_map.122
  1781.6 18.2 shard_map.121
  1799.8 18.1 shard_map.120
  1818.3 95.8 %collective-permute-done.42.refs_7_ = bf16[3072,256]{1,0:T(8,128)(2,1)} collective-permute-done((bf16[3072,256]{1,0:T(8,128)(2,1)S(1)}, bf16[3072,256]{1,0:T(8,128)(2,1)}, u32[]{:S(2)}, u32[]{:S(2)}) %collective-permute-start.42) | collective-permute-done | bytes 1572896 | tf_op jit(solution)/shard_map/ppermute | solution.py:232
  1917.9 14.3 shard_map.128
  1932.2 19.5 shard_map.136
  1951.7 19.5 shard_map.132
  1973.2 42.0 %collective-permute-done.36.refs_9_ = bf16[3072,384]{1,0:T(8,128)(2,1)} collective-permute-done((bf16[3072,384]{1,0:T(8,128)(2,1)S(1)}, bf16[3072,384]{1,0:T(8,128)(2,1)}, u32[]{:S(2)}, u32[]{:S(2)}) %collective-permute-start.36) | collective-permute-done | bytes 2359328 | tf_op jit(solution)/shard_map/ppermute | solution.py:232
  2016.9 48.9 %collective-permute-done.35.refs_8_ = bf16[3072,384]{1,0:T(8,128)(2,1)} collective-permute-done((bf16[3072,384]{1,0:T(8,128)(2,1)}, bf16[3072,384]{1,0:T(8,128)(2,1)}, u32[]{:S(2)}, u32[]{:S(2)}) %collective-permute-start.35) | collective-permute-done | bytes 2359328 | tf_op jit(solution)/shard_map/ppermute | solution.py:232
  2067.5 48.0 %collective-permute-done.34.refs_7_ = bf16[3072,384]{1,0:T(8,128)(2,1)} collective-permute-done((bf16[3072,384]{1,0:T(8,128)(2,1)}, bf16[3072,384]{1,0:T(8,128)(2,1)}, u32[]{:S(2)}, u32[]{:S(2)}) %collective-permute-start.34) | collective-permute-done | bytes 2359328 | tf_op jit(solution)/shard_map/ppermute | solution.py:232
  2115.5 49.6 %shard_map.124.main_ref = f32[3072,1536]{1,0:T(8,128)} custom-call(bf16[3072,768]{1,0:T(8,128)(2,1)} %shard_map.104.refs_0_, bf16[3072,768]{1,0:T(8,128)(2,1)} %shard_map.105.refs_1_, bf16[3072,768]{1,0:T(8,128)(2,1)} %shard_map.106.refs_2_, bf16[3072,768]{1,0:T(8,128)(2,1)} %shard_map.107.refs_3_, bf16[3072,768]{1,0:T(8,128)(2,1)} %shard_map.108.refs_4_, ...), custom_call_target="tpu_custom_call" | custom-call | flops 36238786560 | bytes 35389440 | tf_op jit(solution)/shard_map/pallas_call | solution.py:136
  2173.8 12.3 shard_map.141.held_ref
  (163 shorter events, 134.0 us)
Async XLA Ops:
  0.0 206.7 %collective-permute-start.1 = (bf16[3072,1536]{1,0:T(8,128)(2,1)}, bf16[3072,1536]{1,0:T(8,128)(2,1)}, u32[]{:S(2)}, u32[]{:S(2)}) collective-permute-start(bf16[3072,1536]{1,0:T(8,128)(2,1)} %bitcast.4), channel_id=1, source_target_pairs={{0,2},{1,3},{2,0},{3,1},{4,6},{5,7},{6,4},{7,5}} | collective-permute-start | bytes 28311560 | tf_op jit(solution)/shard_map/ppermute | solution.py:229
  3.3 279.1 %collective-permute-start.3 = (f32[1536]{0:T(1024)}, f32[1536]{0:T(1024)S(1)}, u32[]{:S(2)}, u32[]{:S(2)}) collective-permute-start(f32[1536]{0:T(1024)} %param.11), channel_id=1, source_target_pairs={{0,1},{1,0},{2,3},{3,2},{4,5},{5,4},{6,7},{7,6}} | collective-permute-start | bytes 18440 | tf_op jit(solution)/shard_map/ppermute | solution.py:229
  3.3 279.6 %collective-permute-start.4 = (f32[1536]{0:T(1024)}, f32[1536]{0:T(1024)S(1)}, u32[]{:S(2)}, u32[]{:S(2)}) collective-permute-start(f32[1536]{0:T(1024)} %param.11), channel_id=1, source_target_pairs={{0,2},{1,3},{2,0},{3,1},{4,6},{5,7},{6,4},{7,5}} | collective-permute-start | bytes 18440 | tf_op jit(solution)/shard_map/ppermute | solution.py:229
  3.3 279.6 %collective-permute-start.5 = (f32[1536]{0:T(1024)}, f32[1536]{0:T(1024)S(1)}, u32[]{:S(2)}, u32[]{:S(2)}) collective-permute-start(f32[1536]{0:T(1024)} %param.11), channel_id=1, source_target_pairs={{0,3},{1,2},{2,1},{3,0},{4,7},{5,6},{6,5},{7,4}} | collective-permute-start | bytes 18440 | tf_op jit(solution)/shard_map/ppermute | solution.py:229
  5.2 279.5 %collective-permute-start = (bf16[3072,1536]{1,0:T(8,128)(2,1)}, bf16[3072,1536]{1,0:T(8,128)(2,1)}, u32[]{:S(2)}, u32[]{:S(2)}) collective-permute-start(bf16[3072,1536]{1,0:T(8,128)(2,1)} %bitcast.5), channel_id=1, source_target_pairs={{0,1},{1,0},{2,3},{3,2},{4,5},{5,4},{6,7},{7,6}} | collective-permute-start | bytes 28311560 | tf_op jit(solution)/shard_map/ppermute | solution.py:229
  206.7 89.2 %collective-permute-start.2 = (bf16[3072,1536]{1,0:T(8,128)(2,1)}, bf16[3072,1536]{1,0:T(8,128)(2,1)}, u32[]{:S(2)}, u32[]{:S(2)}) collective-permute-start(bf16[3072,1536]{1,0:T(8,128)(2,1)} %collective-permute-done.1.refs_2_), channel_id=1, source_target_pairs={{0,1},{1,0},{2,3},{3,2},{4,5},{5,4},{6,7},{7,6}} | collective-permute-start | bytes 28311560 | tf_op jit(solution)/shard_map/ppermute | solution.py:229
  282.4 51.1 %collective-permute-start.24 = (bf16[1536,768]{1,0:T(8,128)(2,1)}, bf16[1536,768]{1,0:T(8,128)(2,1)}, u32[]{:S(2)}, u32[]{:S(2)}) collective-permute-start(bf16[1536,768]{1,0:T(8,128)(2,1)} %get-tuple-element.32), channel_id=1, source_target_pairs={{0,1},{1,0},{2,3},{3,2},{4,5},{5,4},{6,7},{7,6}} | collective-permute-start | bytes 7077896 | tf_op jit(solution)/shard_map/ppermute | solution.py:229
  282.9 50.7 %collective-permute-start.12 = (bf16[1536,768]{1,0:T(8,128)(2,1)}, bf16[1536,768]{1,0:T(8,128)(2,1)}, u32[]{:S(2)}, u32[]{:S(2)}) collective-permute-start(bf16[1536,768]{1,0:T(8,128)(2,1)} %get-tuple-element.48), channel_id=1, source_target_pairs={{0,1},{1,0},{2,3},{3,2},{4,5},{5,4},{6,7},{7,6}} | collective-permute-start | bytes 7077896 | tf_op jit(solution)/shard_map/ppermute | solution.py:229
  283.0 54.4 %collective-permute-start.13 = (bf16[1536,768]{1,0:T(8,128)(2,1)}, bf16[1536,768]{1,0:T(8,128)(2,1)}, u32[]{:S(2)}, u32[]{:S(2)}) collective-permute-start(bf16[1536,768]{1,0:T(8,128)(2,1)} %get-tuple-element.58), channel_id=1, source_target_pairs={{0,2},{1,3},{2,0},{3,1},{4,6},{5,7},{6,4},{7,5}} | collective-permute-start | bytes 7077896 | tf_op jit(solution)/shard_map/ppermute | solution.py:229
  284.7 102.5 %collective-permute-start.14 = (bf16[1536,768]{1,0:T(8,128)(2,1)}, bf16[1536,768]{1,0:T(8,128)(2,1)}, u32[]{:S(2)}, u32[]{:S(2)}) collective-permute-start(bf16[1536,768]{1,0:T(8,128)(2,1)} %get-tuple-element.47), channel_id=1, source_target_pairs={{0,3},{1,2},{2,1},{3,0},{4,7},{5,6},{6,5},{7,4}} | collective-permute-start | bytes 7077896 | tf_op jit(solution)/shard_map/ppermute | solution.py:229
  295.9 142.6 %collective-permute-start.25 = (bf16[1536,768]{1,0:T(8,128)(2,1)}, bf16[1536,768]{1,0:T(8,128)(2,1)}, u32[]{:S(2)}, u32[]{:S(2)}) collective-permute-start(bf16[1536,768]{1,0:T(8,128)(2,1)} %get-tuple-element.46), channel_id=1, source_target_pairs={{0,2},{1,3},{2,0},{3,1},{4,6},{5,7},{6,4},{7,5}} | collective-permute-start | bytes 7077896 | tf_op jit(solution)/shard_map/ppermute | solution.py:229
  333.5 154.8 %collective-permute-start.26 = (bf16[1536,768]{1,0:T(8,128)(2,1)}, bf16[1536,768]{1,0:T(8,128)(2,1)}, u32[]{:S(2)}, u32[]{:S(2)}) collective-permute-start(bf16[1536,768]{1,0:T(8,128)(2,1)} %get-tuple-element.31), channel_id=1, source_target_pairs={{0,3},{1,2},{2,1},{3,0},{4,7},{5,6},{6,5},{7,4}} | collective-permute-start | bytes 7077896 | tf_op jit(solution)/shard_map/ppermute | solution.py:229
  333.6 206.0 %collective-permute-start.10 = (bf16[1536,768]{1,0:T(8,128)(2,1)}, bf16[1536,768]{1,0:T(8,128)(2,1)}, u32[]{:S(2)}, u32[]{:S(2)}) collective-permute-start(bf16[1536,768]{1,0:T(8,128)(2,1)} %get-tuple-element.51), channel_id=1, source_target_pairs={{0,2},{1,3},{2,0},{3,1},{4,6},{5,7},{6,4},{7,5}} | collective-permute-start | bytes 7077896 | tf_op jit(solution)/shard_map/ppermute | solution.py:229
  337.4 252.0 %collective-permute-start.11 = (bf16[1536,768]{1,0:T(8,128)(2,1)}, bf16[1536,768]{1,0:T(8,128)(2,1)}, u32[]{:S(2)}, u32[]{:S(2)}) collective-permute-start(bf16[1536,768]{1,0:T(8,128)(2,1)} %get-tuple-element.50), channel_id=1, source_target_pairs={{0,3},{1,2},{2,1},{3,0},{4,7},{5,6},{6,5},{7,4}} | collective-permute-start | bytes 7077896 | tf_op jit(solution)/shard_map/ppermute | solution.py:229
  387.2 204.4 %collective-permute-start.9 = (bf16[1536,768]{1,0:T(8,128)(2,1)}, bf16[1536,768]{1,0:T(8,128)(2,1)}, u32[]{:S(2)}, u32[]{:S(2)}) collective-permute-start(bf16[1536,768]{1,0:T(8,128)(2,1)} %get-tuple-element.52), channel_id=1, source_target_pairs={{0,1},{1,0},{2,3},{3,2},{4,5},{5,4},{6,7},{7,6}} | collective-permute-start | bytes 7077896 | tf_op jit(solution)/shard_map/ppermute | solution.py:229
  387.8 201.7 %copy-start.5 = (bf16[1536,768]{1,0:T(8,128)(2,1)S(1)}, bf16[1536,768]{1,0:T(8,128)(2,1)}, u32[]{:S(2)}) copy-start(bf16[1536,768]{1,0:T(8,128)(2,1)} %get-tuple-element.54) | copy-start | bytes 7077892
  438.5 455.8 %collective-permute-start.29 = (bf16[3072,1536]{1,0:T(8,128)(2,1)}, bf16[3072,1536]{1,0:T(8,128)(2,1)}, u32[]{:S(2)}, u32[]{:S(2)}) collective-permute-start(bf16[3072,1536]{1,0:T(8,128)(2,1)} %bitcast.7), channel_id=1, source_target_pairs={{0,4},{4,0},{1,5},{5,1},{2,6},{6,2},{3,7},{7,3}} | collective-permute-start | bytes 28311560 | tf_op jit(solution)/shard_map/ppermute | solution.py:232
  488.3 142.4 %collective-permute-start.6 = (bf16[1536,768]{1,0:T(8,128)(2,1)}, bf16[1536,768]{1,0:T(8,128)(2,1)}, u32[]{:S(2)}, u32[]{:S(2)}) collective-permute-start(bf16[1536,768]{1,0:T(8,128)(2,1)} %get-tuple-element.56), channel_id=1, source_target_pairs={{0,1},{1,0},{2,3},{3,2},{4,5},{5,4},{6,7},{7,6}} | collective-permute-start | bytes 7077896 | tf_op jit(solution)/shard_map/ppermute | solution.py:229
  539.6 101.1 %collective-permute-start.7 = (bf16[1536,768]{1,0:T(8,128)(2,1)}, bf16[1536,768]{1,0:T(8,128)(2,1)}, u32[]{:S(2)}, u32[]{:S(2)}) collective-permute-start(bf16[1536,768]{1,0:T(8,128)(2,1)} %get-tuple-element.55), channel_id=1, source_target_pairs={{0,2},{1,3},{2,0},{3,1},{4,6},{5,7},{6,4},{7,5}} | collective-permute-start | bytes 7077896 | tf_op jit(solution)/shard_map/ppermute | solution.py:229
  589.4 101.0 %collective-permute-start.8 = (bf16[1536,768]{1,0:T(8,128)(2,1)S(1)}, bf16[1536,768]{1,0:T(8,128)(2,1)}, u32[]{:S(2)}, u32[]{:S(2)}) collective-permute-start(bf16[1536,768]{1,0:T(8,128)(2,1)S(1)} %copy-done.5), channel_id=1, source_target_pairs={{0,3},{1,2},{2,1},{3,0},{4,7},{5,6},{6,5},{7,4}} | collective-permute-start | bytes 7077896 | tf_op jit(solution)/shard_map/ppermute | solution.py:229
  591.6 303.1 %collective-permute-start.31 = (bf16[3072,1536]{1,0:T(8,128)(2,1)}, bf16[3072,1536]{1,0:T(8,128)(2,1)}, u32[]{:S(2)}, u32[]{:S(2)}) collective-permute-start(bf16[3072,1536]{1,0:T(8,128)(2,1)} %collective-permute-done.1.refs_2_), channel_id=1, source_target_pairs={{0,4},{4,0},{1,5},{5,1},{2,6},{6,2},{3,7},{7,3}} | collective-permute-start | bytes 28311560 | tf_op jit(solution)/shard_map/ppermute | solution.py:232
  630.7 99.3 %collective-permute-start.21 = (bf16[1536,768]{1,0:T(8,128)(2,1)}, bf16[1536,768]{1,0:T(8,128)(2,1)}, u32[]{:S(2)}, u32[]{:S(2)}) collective-permute-start(bf16[1536,768]{1,0:T(8,128)(2,1)} %get-tuple-element.36), channel_id=1, source_target_pairs={{0,1},{1,0},{2,3},{3,2},{4,5},{5,4},{6,7},{7,6}} | collective-permute-start | bytes 7077896 | tf_op jit(solution)/shard_map/ppermute | solution.py:229
  640.7 101.1 %collective-permute-start.22 = (bf16[1536,768]{1,0:T(8,128)(2,1)}, bf16[1536,768]{1,0:T(8,128)(2,1)}, u32[]{:S(2)}, u32[]{:S(2)}) collective-permute-start(bf16[1536,768]{1,0:T(8,128)(2,1)} %get-tuple-element.35), channel_id=1, source_target_pairs={{0,2},{1,3},{2,0},{3,1},{4,6},{5,7},{6,4},{7,5}} | collective-permute-start | bytes 7077896 | tf_op jit(solution)/shard_map/ppermute | solution.py:229
  690.5 101.2 %collective-permute-start.23 = (bf16[1536,768]{1,0:T(8,128)(2,1)}, bf16[1536,768]{1,0:T(8,128)(2,1)S(1)}, u32[]{:S(2)}, u32[]{:S(2)}) collective-permute-start(bf16[1536,768]{1,0:T(8,128)(2,1)} %get-tuple-element.34), channel_id=1, source_target_pairs={{0,3},{1,2},{2,1},{3,0},{4,7},{5,6},{6,5},{7,4}} | collective-permute-start | bytes 7077896 | tf_op jit(solution)/shard_map/ppermute | solution.py:229
  730.1 102.7 %collective-permute-start.18 = (bf16[1536,768]{1,0:T(8,128)(2,1)}, bf16[1536,768]{1,0:T(8,128)(2,1)}, u32[]{:S(2)}, u32[]{:S(2)}) collective-permute-start(bf16[1536,768]{1,0:T(8,128)(2,1)} %get-tuple-element.40), channel_id=1, source_target_pairs={{0,1},{1,0},{2,3},{3,2},{4,5},{5,4},{6,7},{7,6}} | collective-permute-start | bytes 7077896 | tf_op jit(solution)/shard_map/ppermute | solution.py:229
  741.9 101.1 %collective-permute-start.19 = (bf16[1536,768]{1,0:T(8,128)(2,1)}, bf16[1536,768]{1,0:T(8,128)(2,1)}, u32[]{:S(2)}, u32[]{:S(2)}) collective-permute-start(bf16[1536,768]{1,0:T(8,128)(2,1)} %get-tuple-element.39), channel_id=1, source_target_pairs={{0,2},{1,3},{2,0},{3,1},{4,6},{5,7},{6,4},{7,5}} | collective-permute-start | bytes 7077896 | tf_op jit(solution)/shard_map/ppermute | solution.py:229
  791.7 308.5 %collective-permute-start.27 = (bf16[3840,1536]{1,0:T(8,128)(2,1)}, bf16[3840,1536]{1,0:T(8,128)(2,1)}, u32[]{:S(2)}, u32[]{:S(2)}) collective-permute-start(bf16[3840,1536]{1,0:T(8,128)(2,1)} %pad_maximum_fusion.1), channel_id=1, source_target_pairs={{0,1},{1,0},{2,3},{3,2},{4,5},{5,4},{6,7},{7,6}} | collective-permute-start | bytes 35389448 | tf_op jit(solution)/shard_map/ppermute | solution.py:229
  832.8 59.8 %collective-permute-start.20 = (bf16[1536,768]{1,0:T(8,128)(2,1)}, bf16[1536,768]{1,0:T(8,128)(2,1)}, u32[]{:S(2)}, u32[]{:S(2)}) collective-permute-start(bf16[1536,768]{1,0:T(8,128)(2,1)} %get-tuple-element.38), channel_id=1, source_target_pairs={{0,3},{1,2},{2,1},{3,0},{4,7},{5,6},{6,5},{7,4}} | collective-permute-start | bytes 7077896 | tf_op jit(solution)/shard_map/ppermute | solution.py:229
  843.0 51.3 %collective-permute-start.15 = (bf16[1536,768]{1,0:T(8,128)(2,1)S(1)}, bf16[1536,768]{1,0:T(8,128)(2,1)}, u32[]{:S(2)}, u32[]{:S(2)}) collective-permute-start(bf16[1536,768]{1,0:T(8,128)(2,1)S(1)} %copy-done.4), channel_id=1, source_target_pairs={{0,1},{1,0},{2,3},{3,2},{4,5},{5,4},{6,7},{7,6}} | collective-permute-start | bytes 7077896 | tf_op jit(solution)/shard_map/ppermute | solution.py:229
  892.6 54.4 %collective-permute-start.16 = (bf16[1536,768]{1,0:T(8,128)(2,1)}, bf16[1536,768]{1,0:T(8,128)(2,1)}, u32[]{:S(2)}, u32[]{:S(2)}) collective-permute-start(bf16[1536,768]{1,0:T(8,128)(2,1)} %get-tuple-element.43), channel_id=1, source_target_pairs={{0,2},{1,3},{2,0},{3,1},{4,6},{5,7},{6,4},{7,5}} | collective-permute-start | bytes 7077896 | tf_op jit(solution)/shard_map/ppermute | solution.py:229
  894.3 102.5 %collective-permute-start.17 = (bf16[1536,768]{1,0:T(8,128)(2,1)}, bf16[1536,768]{1,0:T(8,128)(2,1)}, u32[]{:S(2)}, u32[]{:S(2)}) collective-permute-start(bf16[1536,768]{1,0:T(8,128)(2,1)} %get-tuple-element.42), channel_id=1, source_target_pairs={{0,3},{1,2},{2,1},{3,0},{4,7},{5,6},{6,5},{7,4}} | collective-permute-start | bytes 7077896 | tf_op jit(solution)/shard_map/ppermute | solution.py:229
  894.3 251.6 %collective-permute-start.30 = (bf16[3072,1536]{1,0:T(8,128)(2,1)}, bf16[3072,1536]{1,0:T(8,128)(2,1)}, u32[]{:S(2)}, u32[]{:S(2)}) collective-permute-start(bf16[3072,1536]{1,0:T(8,128)(2,1)} %collective-permute-done.29.refs_0_), channel_id=1, source_target_pairs={{0,1},{1,0},{2,3},{3,2},{4,5},{5,4},{6,7},{7,6}} | collective-permute-start | bytes 28311560 | tf_op jit(solution)/shard_map/ppermute | solution.py:229
  894.7 252.9 %collective-permute-start.32 = (bf16[3072,1536]{1,0:T(8,128)(2,1)}, bf16[3072,1536]{1,0:T(8,128)(2,1)}, u32[]{:S(2)}, u32[]{:S(2)}) collective-permute-start(bf16[3072,1536]{1,0:T(8,128)(2,1)} %collective-permute-done.31.refs_2_), channel_id=1, source_target_pairs={{0,1},{1,0},{2,3},{3,2},{4,5},{5,4},{6,7},{7,6}} | collective-permute-start | bytes 28311560 | tf_op jit(solution)/shard_map/ppermute | solution.py:229
  947.0 134.0 %collective-permute-start.51 = (bf16[3840,512]{1,0:T(8,128)(2,1)S(1)}, bf16[3840,512]{1,0:T(8,128)(2,1)}, u32[]{:S(2)}, u32[]{:S(2)}) collective-permute-start(bf16[3840,512]{1,0:T(8,128)(2,1)S(1)} %copy-done.2), channel_id=1, source_target_pairs={{0,3},{1,2},{2,1},{3,0},{4,7},{5,6},{6,5},{7,4}} | collective-permute-start | bytes 11796488 | tf_op jit(solution)/shard_map/ppermute | solution.py:229
  996.8 544.9 %collective-permute-start.57 = (bf16[3840,256]{1,0:T(8,128)(2,1)}, bf16[3840,256]{1,0:T(8,128)(2,1)}, u32[]{:S(2)}, u32[]{:S(2)}) collective-permute-start(bf16[3840,256]{1,0:T(8,128)(2,1)} %pad_maximum_fusion.9), channel_id=1, source_target_pairs={{0,3},{1,2},{2,1},{3,0},{4,7},{5,6},{6,5},{7,4}} | collective-permute-start | bytes 5898248 | tf_op jit(solution)/shard_map/ppermute | solution.py:229
  1081.0 475.9 %collective-permute-start.56 = (bf16[3840,256]{1,0:T(8,128)(2,1)}, bf16[3840,256]{1,0:T(8,128)(2,1)}, u32[]{:S(2)}, u32[]{:S(2)}) collective-permute-start(bf16[3840,256]{1,0:T(8,128)(2,1)} %pad_maximum_fusion.8), channel_id=1, source_target_pairs={{0,2},{1,3},{2,0},{3,1},{4,6},{5,7},{6,4},{7,5}} | collective-permute-start | bytes 5898248 | tf_op jit(solution)/shard_map/ppermute | solution.py:229
  1100.2 502.9 %collective-permute-start.50 = (bf16[3840,512]{1,0:T(8,128)(2,1)}, bf16[3840,512]{1,0:T(8,128)(2,1)}, u32[]{:S(2)}, u32[]{:S(2)}) collective-permute-start(bf16[3840,512]{1,0:T(8,128)(2,1)} %pad_maximum_fusion.4), channel_id=1, source_target_pairs={{0,2},{1,3},{2,0},{3,1},{4,6},{5,7},{6,4},{7,5}} | collective-permute-start | bytes 11796488 | tf_op jit(solution)/shard_map/ppermute | solution.py:229
  1145.9 377.3 %collective-permute-start.45 = (bf16[3840,512]{1,0:T(8,128)(2,1)}, bf16[3840,512]{1,0:T(8,128)(2,1)}, u32[]{:S(2)}, u32[]{:S(2)}) collective-permute-start(bf16[3840,512]{1,0:T(8,128)(2,1)} %pad_maximum_fusion.3), channel_id=1, source_target_pairs={{0,3},{1,2},{2,1},{3,0},{4,7},{5,6},{6,5},{7,4}} | collective-permute-start | bytes 11796488 | tf_op jit(solution)/shard_map/ppermute | solution.py:229
  1147.6 427.7 %collective-permute-start.39 = (bf16[3840,256]{1,0:T(8,128)(2,1)}, bf16[3840,256]{1,0:T(8,128)(2,1)}, u32[]{:S(2)}, u32[]{:S(2)}) collective-permute-start(bf16[3840,256]{1,0:T(8,128)(2,1)} %pad_maximum_fusion.7), channel_id=1, source_target_pairs={{0,3},{1,2},{2,1},{3,0},{4,7},{5,6},{6,5},{7,4}} | collective-permute-start | bytes 5898248 | tf_op jit(solution)/shard_map/ppermute | solution.py:229
  1523.2 220.2 %collective-permute-start.33 = (bf16[3072,1536]{1,0:T(8,128)(2,1)}, bf16[3072,1536]{1,0:T(8,128)(2,1)}, u32[]{:S(2)}, u32[]{:S(2)}) collective-permute-start(bf16[3072,1536]{1,0:T(8,128)(2,1)} %shard_map.119), channel_id=1, source_target_pairs={{0,1},{1,0},{2,3},{3,2},{4,5},{5,4},{6,7},{7,6}} | collective-permute-start | bytes 28311560 | tf_op jit(solution)/shard_map/ppermute | solution.py:229
  1541.8 47.1 %collective-permute-start.38 = (bf16[3840,256]{1,0:T(8,128)(2,1)S(1)}, bf16[3840,256]{1,0:T(8,128)(2,1)S(1)}, u32[]{:S(2)}, u32[]{:S(2)}) collective-permute-start(bf16[3840,256]{1,0:T(8,128)(2,1)S(1)} %copy-done.7), channel_id=1, source_target_pairs={{0,2},{1,3},{2,0},{3,1},{4,6},{5,7},{6,4},{7,5}} | collective-permute-start | bytes 5898248 | tf_op jit(solution)/shard_map/ppermute | solution.py:229
  1556.9 114.0 %collective-permute-start.44 = (bf16[3840,512]{1,0:T(8,128)(2,1)}, bf16[3840,512]{1,0:T(8,128)(2,1)}, u32[]{:S(2)}, u32[]{:S(2)}) collective-permute-start(bf16[3840,512]{1,0:T(8,128)(2,1)} %pad_maximum_fusion.2), channel_id=1, source_target_pairs={{0,2},{1,3},{2,0},{3,1},{4,6},{5,7},{6,4},{7,5}} | collective-permute-start | bytes 11796488 | tf_op jit(solution)/shard_map/ppermute | solution.py:229
  1575.4 96.1 %collective-permute-start.53 = (bf16[3072,512]{1,0:T(8,128)(2,1)}, bf16[3072,512]{1,0:T(8,128)(2,1)}, u32[]{:S(2)}, u32[]{:S(2)}) collective-permute-start(bf16[3072,512]{1,0:T(8,128)(2,1)} %shard_map.134), channel_id=1, source_target_pairs={{0,1},{1,0},{2,3},{3,2},{4,5},{5,4},{6,7},{7,6}} | collective-permute-start | bytes 9437192 | tf_op jit(solution)/shard_map/ppermute | solution.py:229
  1588.9 32.6 %collective-permute-start.59 = (bf16[3072,256]{1,0:T(8,128)(2,1)}, bf16[3072,256]{1,0:T(8,128)(2,1)}, u32[]{:S(2)}, u32[]{:S(2)}) collective-permute-start(bf16[3072,256]{1,0:T(8,128)(2,1)} %shard_map.138), channel_id=1, source_target_pairs={{0,1},{1,0},{2,3},{3,2},{4,5},{5,4},{6,7},{7,6}} | collective-permute-start | bytes 4718600 | tf_op jit(solution)/shard_map/ppermute | solution.py:229
  1603.1 67.8 %collective-permute-start.41 = (bf16[3072,256]{1,0:T(8,128)(2,1)}, bf16[3072,256]{1,0:T(8,128)(2,1)S(1)}, u32[]{:S(2)}, u32[]{:S(2)}) collective-permute-start(bf16[3072,256]{1,0:T(8,128)(2,1)} %shard_map.126), channel_id=1, source_target_pairs={{0,1},{1,0},{2,3},{3,2},{4,5},{5,4},{6,7},{7,6}} | collective-permute-start | bytes 4718600 | tf_op jit(solution)/shard_map/ppermute | solution.py:229
  1621.6 100.9 %collective-permute-start.47 = (bf16[3072,512]{1,0:T(8,128)(2,1)}, bf16[3072,512]{1,0:T(8,128)(2,1)}, u32[]{:S(2)}, u32[]{:S(2)}) collective-permute-start(bf16[3072,512]{1,0:T(8,128)(2,1)} %shard_map.130), channel_id=1, source_target_pairs={{0,1},{1,0},{2,3},{3,2},{4,5},{5,4},{6,7},{7,6}} | collective-permute-start | bytes 9437192 | tf_op jit(solution)/shard_map/ppermute | solution.py:229
  1670.9 35.0 %collective-permute-start.58 = (bf16[3072,256]{1,0:T(8,128)(2,1)S(1)}, bf16[3072,256]{1,0:T(8,128)(2,1)}, u32[]{:S(2)}, u32[]{:S(2)}) collective-permute-start(bf16[3072,256]{1,0:T(8,128)(2,1)S(1)} %copy-done.8), channel_id=1, source_target_pairs={{0,1},{1,0},{2,3},{3,2},{4,5},{5,4},{6,7},{7,6}} | collective-permute-start | bytes 4718600 | tf_op jit(solution)/shard_map/ppermute | solution.py:229
  1671.0 300.2 %collective-permute-start.28 = (bf16[3072,1536]{1,0:T(8,128)(2,1)}, bf16[3072,1536]{1,0:T(8,128)(2,1)}, u32[]{:S(2)}, u32[]{:S(2)}) collective-permute-start(bf16[3072,1536]{1,0:T(8,128)(2,1)} %shard_map.109), channel_id=1, source_target_pairs={{0,1},{1,0},{2,3},{3,2},{4,5},{5,4},{6,7},{7,6}} | collective-permute-start | bytes 28311560 | tf_op jit(solution)/shard_map/ppermute | solution.py:229
  1671.5 36.6 %collective-permute-start.60 = (bf16[3072,256]{1,0:T(8,128)(2,1)}, bf16[3072,256]{1,0:T(8,128)(2,1)}, u32[]{:S(2)}, u32[]{:S(2)}) collective-permute-start(bf16[3072,256]{1,0:T(8,128)(2,1)} %shard_map.139), channel_id=1, source_target_pairs={{0,4},{4,0},{1,5},{5,1},{2,6},{6,2},{3,7},{7,3}} | collective-permute-start | bytes 4718600 | tf_op jit(solution)/shard_map/ppermute | solution.py:232
  1706.0 73.9 %collective-permute-start.52 = (bf16[3072,512]{1,0:T(8,128)(2,1)}, bf16[3072,512]{1,0:T(8,128)(2,1)}, u32[]{:S(2)}, u32[]{:S(2)}) collective-permute-start(bf16[3072,512]{1,0:T(8,128)(2,1)} %shard_map.133), channel_id=1, source_target_pairs={{0,1},{1,0},{2,3},{3,2},{4,5},{5,4},{6,7},{7,6}} | collective-permute-start | bytes 9437192 | tf_op jit(solution)/shard_map/ppermute | solution.py:229
  1708.1 33.6 %collective-permute-start.40 = (bf16[3072,256]{1,0:T(8,128)(2,1)S(1)}, bf16[3072,256]{1,0:T(8,128)(2,1)S(1)}, u32[]{:S(2)}, u32[]{:S(2)}) collective-permute-start(bf16[3072,256]{1,0:T(8,128)(2,1)S(1)} %copy-done.10), channel_id=1, source_target_pairs={{0,1},{1,0},{2,3},{3,2},{4,5},{5,4},{6,7},{7,6}} | collective-permute-start | bytes 4718600 | tf_op jit(solution)/shard_map/ppermute | solution.py:229
  1722.5 95.5 %collective-permute-start.46 = (bf16[3072,512]{1,0:T(8,128)(2,1)}, bf16[3072,512]{1,0:T(8,128)(2,1)}, u32[]{:S(2)}, u32[]{:S(2)}) collective-permute-start(bf16[3072,512]{1,0:T(8,128)(2,1)} %shard_map.129), channel_id=1, source_target_pairs={{0,1},{1,0},{2,3},{3,2},{4,5},{5,4},{6,7},{7,6}} | collective-permute-start | bytes 9437192 | tf_op jit(solution)/shard_map/ppermute | solution.py:229
  1741.7 174.1 %collective-permute-start.54 = (bf16[3072,512]{1,0:T(8,128)(2,1)}, bf16[3072,512]{1,0:T(8,128)(2,1)}, u32[]{:S(2)}, u32[]{:S(2)}) collective-permute-start(bf16[3072,512]{1,0:T(8,128)(2,1)} %shard_map.135), channel_id=1, source_target_pairs={{0,4},{4,0},{1,5},{5,1},{2,6},{6,2},{3,7},{7,3}} | collective-permute-start | bytes 9437192 | tf_op jit(solution)/shard_map/ppermute | solution.py:232
  1743.4 172.8 %collective-permute-start.48 = (bf16[3072,512]{1,0:T(8,128)(2,1)}, bf16[3072,512]{1,0:T(8,128)(2,1)}, u32[]{:S(2)}, u32[]{:S(2)}) collective-permute-start(bf16[3072,512]{1,0:T(8,128)(2,1)} %shard_map.131), channel_id=1, source_target_pairs={{0,4},{4,0},{1,5},{5,1},{2,6},{6,2},{3,7},{7,3}} | collective-permute-start | bytes 9437192 | tf_op jit(solution)/shard_map/ppermute | solution.py:232
  1779.9 134.3 %collective-permute-start.42 = (bf16[3072,256]{1,0:T(8,128)(2,1)S(1)}, bf16[3072,256]{1,0:T(8,128)(2,1)}, u32[]{:S(2)}, u32[]{:S(2)}) collective-permute-start(bf16[3072,256]{1,0:T(8,128)(2,1)S(1)} %copy-done.9), channel_id=1, source_target_pairs={{0,4},{4,0},{1,5},{5,1},{2,6},{6,2},{3,7},{7,3}} | collective-permute-start | bytes 4718600 | tf_op jit(solution)/shard_map/ppermute | solution.py:232
  1799.8 114.3 %copy-start.6 = (bf16[3072,384]{1,0:T(8,128)(2,1)S(1)}, bf16[3072,384]{1,0:T(8,128)(2,1)}, u32[]{:S(2)}) copy-start(bf16[3072,384]{1,0:T(8,128)(2,1)} %shard_map.122) | copy-start | bytes 7077892
  1818.0 154.7 %collective-permute-start.37 = (bf16[3072,384]{1,0:T(8,128)(2,1)}, bf16[3072,384]{1,0:T(8,128)(2,1)}, u32[]{:S(2)}, u32[]{:S(2)}) collective-permute-start(bf16[3072,384]{1,0:T(8,128)(2,1)} %shard_map.123), channel_id=1, source_target_pairs={{0,4},{4,0},{1,5},{5,1},{2,6},{6,2},{3,7},{7,3}} | collective-permute-start | bytes 7077896 | tf_op jit(solution)/shard_map/ppermute | solution.py:232
  1914.2 101.1 %collective-permute-start.36 = (bf16[3072,384]{1,0:T(8,128)(2,1)S(1)}, bf16[3072,384]{1,0:T(8,128)(2,1)}, u32[]{:S(2)}, u32[]{:S(2)}) collective-permute-start(bf16[3072,384]{1,0:T(8,128)(2,1)S(1)} %copy-done.6), channel_id=1, source_target_pairs={{0,4},{4,0},{1,5},{5,1},{2,6},{6,2},{3,7},{7,3}} | collective-permute-start | bytes 7077896 | tf_op jit(solution)/shard_map/ppermute | solution.py:232
  1915.8 150.0 %collective-permute-start.35 = (bf16[3072,384]{1,0:T(8,128)(2,1)}, bf16[3072,384]{1,0:T(8,128)(2,1)}, u32[]{:S(2)}, u32[]{:S(2)}) collective-permute-start(bf16[3072,384]{1,0:T(8,128)(2,1)} %shard_map.121), channel_id=1, source_target_pairs={{0,4},{4,0},{1,5},{5,1},{2,6},{6,2},{3,7},{7,3}} | collective-permute-start | bytes 7077896 | tf_op jit(solution)/shard_map/ppermute | solution.py:232
  1916.2 199.3 %collective-permute-start.34 = (bf16[3072,384]{1,0:T(8,128)(2,1)}, bf16[3072,384]{1,0:T(8,128)(2,1)}, u32[]{:S(2)}, u32[]{:S(2)}) collective-permute-start(bf16[3072,384]{1,0:T(8,128)(2,1)} %shard_map.120), channel_id=1, source_target_pairs={{0,4},{4,0},{1,5},{5,1},{2,6},{6,2},{3,7},{7,3}} | collective-permute-start | bytes 7077896 | tf_op jit(solution)/shard_map/ppermute | solution.py:232
  1971.2 193.8 %collective-permute-start.61 = (bf16[3072,256]{1,0:T(8,128)(2,1)}, bf16[3072,256]{1,0:T(8,128)(2,1)}, u32[]{:S(2)}, u32[]{:S(2)}) collective-permute-start(bf16[3072,256]{1,0:T(8,128)(2,1)} %shard_map.140), channel_id=1, source_target_pairs={{0,2},{1,3},{2,0},{3,1},{4,6},{5,7},{6,4},{7,5}} | collective-permute-start | bytes 4718600 | tf_op jit(solution)/shard_map/ppermute | solution.py:229
  1972.7 213.4 %collective-permute-start.43 = (bf16[3072,256]{1,0:T(8,128)(2,1)}, bf16[3072,256]{1,0:T(8,128)(2,1)}, u32[]{:S(2)}, u32[]{:S(2)}) collective-permute-start(bf16[3072,256]{1,0:T(8,128)(2,1)} %shard_map.128), channel_id=1, source_target_pairs={{0,2},{1,3},{2,0},{3,1},{4,6},{5,7},{6,4},{7,5}} | collective-permute-start | bytes 4718600 | tf_op jit(solution)/shard_map/ppermute | solution.py:229
  2015.3 149.8 %collective-permute-start.55 = (bf16[3072,512]{1,0:T(8,128)(2,1)}, bf16[3072,512]{1,0:T(8,128)(2,1)S(1)}, u32[]{:S(2)}, u32[]{:S(2)}) collective-permute-start(bf16[3072,512]{1,0:T(8,128)(2,1)} %shard_map.136), channel_id=1, source_target_pairs={{0,2},{1,3},{2,0},{3,1},{4,6},{5,7},{6,4},{7,5}} | collective-permute-start | bytes 9437192 | tf_op jit(solution)/shard_map/ppermute | solution.py:229
  2065.8 107.9 %collective-permute-start.49 = (bf16[3072,512]{1,0:T(8,128)(2,1)}, bf16[3072,512]{1,0:T(8,128)(2,1)}, u32[]{:S(2)}, u32[]{:S(2)}) collective-permute-start(bf16[3072,512]{1,0:T(8,128)(2,1)} %shard_map.132), channel_id=1, source_target_pairs={{0,2},{1,3},{2,0},{3,1},{4,6},{5,7},{6,4},{7,5}} | collective-permute-start | bytes 9437192 | tf_op jit(solution)/shard_map/ppermute | solution.py:229
  (14 other events, 308.9 us)

commit v2 on v1

--- a/solution.py
+++ b/solution.py
@@ -11,7 +11,8 @@
 VMEM_LIMIT = 60 * 1024 * 1024
 UP_PIECES = 4
 OUT_PIECES = (512, 512, 256, 256)
-Y_PIECES = 4
+Y_PIECES = 3
+EARLY = 2
 
 
 def layer_norm_rows(values, gain_vec):
@@ -28,7 +29,7 @@
 
 
 def normalise_tile(n_blocks, *refs):
-    x_refs, gain_refs, out_refs = refs[:n_blocks], refs[n_blocks:2 * n_blocks], refs[2 * n_blocks:]
+    x_refs, gain_refs, out_refs = refs[:n_blocks], refs[n_blocks:2 * n_blocks], refs[-n_blocks:]
     full_width = n_blocks * x_refs[0].shape[1]
     total, squares = 0.0, 0.0
     for x_ref in x_refs:
@@ -42,53 +43,77 @@
         out_ref[...] = ((x_ref[...].astype(jnp.float32) - row_mean) * inv * gain_ref[...]).astype(jnp.bfloat16)
 
 
-def normalise(x_list, gain_list):
+def normalise(x_list, gain_list, held):
     rows, depth = x_list[0].shape
     n_blocks = len(x_list)
-    bm = tile_of(rows, 256)
+    bm = tile_of(rows, 64)
+    steps = rows // bm
+    shift = steps if held else 0
     row_block = pl.BlockSpec((bm, depth), lambda i: (i, 0))
+    held = list(held or [])
     return pl.pallas_call(
         functools.partial(normalise_tile, n_blocks),
-        out_shape=[jax.ShapeDtypeStruct((rows, depth), jnp.bfloat16)] * n_blocks,
-        grid=(rows // bm,),
-        in_specs=[row_block] * n_blocks + [pl.BlockSpec((1, depth), lambda i: (0, 0))] * n_blocks,
-        out_specs=[row_block] * n_blocks,
+        out_shape=[jax.ShapeDtypeStruct((2 * rows, depth), jnp.bfloat16)] * n_blocks,
+        grid=(steps,),
+        in_specs=[row_block] * n_blocks + [pl.BlockSpec((1, depth), lambda i: (0, 0))] * n_blocks
+        + [pl.BlockSpec(memory_space=pl.ANY)] * len(held),
+        out_specs=[pl.BlockSpec((bm, depth), lambda i: (i + shift, 0))] * n_blocks,
+        input_output_aliases={2 * n_blocks + k: k for k in range(len(held))},
         compiler_params=pltpu.CompilerParams(vmem_limit_bytes=VMEM_LIMIT),
         cost_estimate=pl.CostEstimate(flops=600 * rows * depth * n_blocks, bytes_accessed=4 * rows * depth * n_blocks, transcendentals=0),
-    )(*x_list, *[g.reshape(1, depth) for g in gain_list])
+    )(*x_list, *[g.reshape(1, depth) for g in gain_list], *held)
+
+
+def lane_tile(cols):
+    return 256 if cols % 256 == 0 else 128
 
 
 def block_matmul(n_blocks, with_gelu, *refs):
     n_refs, w_refs = refs[:n_blocks], refs[n_blocks:2 * n_blocks]
     out_ref = refs[-1]
-    acc = jnp.dot(n_refs[0][...], w_refs[0][...], preferred_element_type=jnp.float32)
-    for n_ref, w_ref in zip(n_refs[1:], w_refs[1:]):
-        acc = acc + jnp.dot(n_ref[...], w_ref[...], preferred_element_type=jnp.float32)
-    out = acc.astype(jnp.bfloat16)
-    if with_gelu:
-        bias_ref = refs[2 * n_blocks]
-        out = jax.nn.gelu(out.astype(jnp.float32) + bias_ref[...], approximate=True).astype(jnp.bfloat16)
-    out_ref[...] = out
-
-
-def project_in(n_list, w_list, bias):
+    tile = lane_tile(out_ref.shape[1])
+
+    def step(t, carry):
+        cols = pl.ds(pl.multiple_of(t * tile, tile), tile)
+        acc = jnp.dot(n_refs[0][...], w_refs[0][:, cols], preferred_element_type=jnp.float32)
+        for n_ref, w_ref in zip(n_refs[1:], w_refs[1:]):
+            acc = acc + jnp.dot(n_ref[...], w_ref[:, cols], preferred_element_type=jnp.float32)
+        out = acc.astype(jnp.bfloat16)
+        if with_gelu:
+            bias = refs[2 * n_blocks][:, cols]
+            out = jax.nn.gelu(out.astype(jnp.float32) + bias, approximate=True).astype(jnp.bfloat16)
+        out_ref[:, cols] = out
+        return carry
+
+    lax.fori_loop(0, out_ref.shape[1] // tile, step, 0)
+
+
+def project_in(n_list, w_list, bias, half=None, held=None):
     rows, depth = n_list[0].shape
     cols = w_list[0].shape[1]
     n_blocks = len(n_list)
-    bm, bn = tile_of(rows, 512), 768 if cols % 768 == 0 else tile_of(cols, 512)
-    in_specs = [pl.BlockSpec((bm, depth), lambda j, i: (i, 0))] * n_blocks
+    bm, bn = tile_of(rows // 2, 256), 768 if cols % 768 == 0 else tile_of(cols, 512)
+    steps = rows // bm if half is None else rows // bm // 2
+    shift = steps if half else 0
+    in_specs = [pl.BlockSpec((bm, depth), lambda j, i: (i + shift, 0))] * n_blocks
     in_specs += [pl.BlockSpec((depth, bn), lambda j, i: (0, j))] * n_blocks
     operands = [*n_list, *w_list]
     if bias is not None:
         in_specs.append(pl.BlockSpec((1, bn), lambda j, i: (0, j)))
         operands.append(bias.reshape(1, cols))
-    flops = 2 * rows * depth * n_blocks * cols
+    aliases = {}
+    if held is not None:
+        in_specs.append(pl.BlockSpec(memory_space=pl.ANY))
+        aliases = {len(operands): 0}
+        operands.append(held)
+    flops = 2 * bm * steps * depth * n_blocks * cols
     return pl.pallas_call(
         functools.partial(block_matmul, n_blocks, bias is not None),
         out_shape=jax.ShapeDtypeStruct((rows, cols), jnp.bfloat16),
-        grid=(cols // bn, rows // bm),
+        grid=(cols // bn, steps),
         in_specs=in_specs,
-        out_specs=pl.BlockSpec((bm, bn), lambda j, i: (i, j)),
+        out_specs=pl.BlockSpec((bm, bn), lambda j, i: (i + shift, j)),
+        input_output_aliases=aliases,
         compiler_params=pltpu.CompilerParams(vmem_limit_bytes=VMEM_LIMIT),
         cost_estimate=pl.CostEstimate(flops=flops, bytes_accessed=4 * n_blocks * depth * (rows + cols), transcendentals=0),
     )(*operands)
@@ -98,39 +123,49 @@
     out_ref = refs[-1]
     hidden_refs, w_ref = refs[:n_hidden], refs[n_hidden]
     rest = refs[n_hidden + 1:-1]
-    acc, start = None, 0
-    for h_ref in hidden_refs:
-        stop = start + h_ref.shape[1]
-        term = jnp.dot(h_ref[...], w_ref[start:stop], preferred_element_type=jnp.float32)
-        acc = term if acc is None else acc + term
+    tile = lane_tile(out_ref.shape[1])
+
+    def step(t, carry):
+        cols = pl.ds(pl.multiple_of(t * tile, tile), tile)
+        acc, start = None, 0
+        for h_ref in hidden_refs:
+            stop = start + h_ref.shape[1]
+            term = jnp.dot(h_ref[...], w_ref[start:stop, cols], preferred_element_type=jnp.float32)
+            acc = term if acc is None else acc + term
+            start = stop
+        for add_ref in rest[:n_adds]:
+            acc = acc + add_ref[:, cols].astype(jnp.float32)
+        if has_res:
+            acc = rest[n_adds + n_parts][:, cols].astype(jnp.float32) + acc + rest[n_adds + n_parts + 1][:, cols]
+        out_ref[:, cols] = acc.astype(out_ref.dtype)
+        return carry
+
+    lax.fori_loop(0, out_ref.shape[1] // tile, step, 0)
+    start = 0
+    for part_ref in rest[n_adds:n_adds + n_parts]:
+        stop = start + part_ref.shape[1]
+        out_ref[:, start:stop] = out_ref[:, start:stop] + part_ref[...].astype(jnp.float32)
         start = stop
-    for add_ref in rest[:n_adds]:
-        acc = acc + add_ref[...].astype(jnp.float32)
-    rest = rest[n_adds:]
-    if has_res:
-        acc = rest[n_parts][...].astype(jnp.float32) + acc + rest[n_parts + 1][...]
-    if not n_parts:
-        out_ref[...] = acc.astype(out_ref.dtype)
-    start = 0
-    for part_ref in rest[:n_parts]:
-        stop = start + part_ref.shape[1]
-        out_ref[:, start:stop] = (acc[:, start:stop] + part_ref[...].astype(jnp.float32)).astype(out_ref.dtype)
-        start = stop
-
-
-def project_out(hidden, w, adds, parts=(), residual=None, bias=None, window=(0, 1)):
-    rows = hidden[0].shape[0]
+
+
+def project_out(hidden, w, adds, half=None, parts=(), residual=None, bias=None, window=(0, 1)):
+    all_rows = hidden[0].shape[0]
+    rows = all_rows if half is None else all_rows // 2
     index, count = window
     depth, cols = w.shape[0], w.shape[1] // count
     bm = tile_of(rows, 512)
-    row_block = lambda width: pl.BlockSpec((bm, width), lambda i: (i, 0))
-    in_specs = [row_block(h.shape[1]) for h in hidden] + [pl.BlockSpec((depth, cols), lambda i: (0, index))]
-    in_specs += [pl.BlockSpec((bm, cols), lambda i: (i, index))] * len(adds)
-    in_specs += [row_block(p.shape[1]) for p in parts]
+
+    def row_block(arr, width, col_index=0):
+        shift = rows // bm if half and arr.shape[0] == all_rows else 0
+        return pl.BlockSpec((bm, width), lambda i: (i + shift, col_index))
+
+    in_specs = [row_block(h, h.shape[1]) for h in hidden] + [pl.BlockSpec((depth, cols), lambda i: (0, index))]
+    in_specs += [row_block(a, cols, index) for a in adds]
+    in_specs += [row_block(p, p.shape[1]) for p in parts]
     operands = [*hidden, w, *adds, *parts]
     out_type = jnp.bfloat16
     if residual is not None:
-        in_specs += [row_block(cols), pl.BlockSpec((1, cols), lambda i: (0, 0))]
+        in_specs += [row_block(residual, cols), pl.BlockSpec((1, cols), lambda i: (0, 0))]
         operands += [residual, bias.reshape(1, cols)]
         out_type = jnp.float32
     return pl.pallas_call(
@@ -138,7 +173,7 @@
         out_shape=jax.ShapeDtypeStruct((rows, cols), out_type),
         grid=(rows // bm,),
         in_specs=in_specs,
-        out_specs=row_block(cols),
+        out_specs=pl.BlockSpec((bm, cols), lambda i: (i, 0)),
         compiler_params=pltpu.CompilerParams(vmem_limit_bytes=VMEM_LIMIT),
         cost_estimate=pl.CostEstimate(flops=2 * rows * depth * cols, bytes_accessed=2 * (rows + cols) * depth, transcendentals=0),
     )(*operands)
@@ -158,7 +193,7 @@
 
 def join_parts(main, parts):
     rows, cols = main.shape
-    bm = tile_of(rows, 512)
+    bm = tile_of(rows, 128)
     row_block = lambda width: pl.BlockSpec((bm, width), lambda i: (i, 0))
     return pl.pallas_call(
         add_parts,
@@ -259,43 +294,46 @@
         z2 = over_row(x2)
         z1 = partner(z0, 1)
         z3 = partner(z2, 1)
-        own = normalise([x_rows, x1, x2, x3], gains)
-        oth = normalise([z0, z1, z2, z3], gains)
+        first = normalise([x_rows, x1, x2, x3], gains, None)
+        both = normalise([z0, z1, z2, z3], gains, first)
 
         head_cols = 3 * q_scale.shape[0]
         qkv_cols = w_qkv.shape[1] // col_size
         up_cols = w_up.shape[1] // col_size
         qkv_step, up_step = 2 * head_cols, up_cols // UP_PIECES
-        qkv_own, qkv_oth, g_own, g_oth = [], [], [], []
+        qkv, hidden = [], []
         for i in range(qkv_cols // qkv_step):
             w = in_weights(w_qkv, i * qkv_step, qkv_step)
-            qkv_own.append(project_in(own, w, None))
-            qkv_oth.append(project_in(oth, w, None))
-        attn_own = attention(qkv_own, q_scale, k_scale, seq_len)
-        attn_oth = attention(qkv_oth, q_scale, k_scale, seq_len)
+            if i < EARLY:
+                part = project_in(first, w, None, half=0)
+                qkv.append(project_in(both, w, None, half=1, held=part))
+            else:
+                qkv.append(project_in(both, w, None))
+        hidden.append(attention(qkv, q_scale, k_scale, seq_len))
         for i in range(UP_PIECES):
             w = in_weights(w_up, i * up_step, up_step)
             bias = lax.dynamic_slice(b_up, (col * up_cols + i * up_step,), (up_step,))
-            g_own.append(project_in(own, w, bias))
-            g_oth.append(project_in(oth, w, bias))
-        hid_own, hid_oth = [attn_own, *g_own], [attn_oth, *g_oth]
+            if i < UP_PIECES - 1:
+                hidden.append(project_in(both, w, bias))
+        up_oth = project_in(both, w, bias, half=1)
+        up_both = project_in(both, w, bias, half=0, held=up_oth)
+        hid_oth, hid = [*hidden, up_oth], [*hidden, up_both]
 
         out_cols = w_out.shape[1]
         wo_0 = out_piece(0, 0, out_cols)
         wo_1 = partner(out_piece(1, 0, out_cols), 1)
-        d1_oth = partner(project_out(hid_oth, wo_1, []), 1)
-        d1_own = partner(project_out(hid_own, wo_1, []), 1)
-        y0 = [over_row(project_out(hid_oth, wo_0, [d1_oth], window=(i, Y_PIECES))) for i in range(Y_PIECES)]
+        d1_oth = partner(project_out(hid_oth, wo_1, [], half=1), 1)
+        d1_own = partner(project_out(hid, wo_1, [], half=0), 1)
+        y0 = [over_row(project_out(hid, wo_0, [d1_oth], half=1, window=(i, Y_PIECES))) for i in range(Y_PIECES)]
         x_parts, start = [], 0
         for size in OUT_PIECES:
             wo_3 = partner(out_piece(3, start, size), 3)
             wo_2 = partner(out_piece(2, start, size), 2)
-            d3_oth = partner(project_out(hid_oth, wo_3, []), 1)
-            d3_own = partner(project_out(hid_own, wo_3, []), 1)
-            y2 = over_row(project_out(hid_oth, wo_2, [d3_oth]))
-            x_parts.append(partner(project_out(hid_own, wo_2, [d3_own, y2]), 2))
+            d3 = partner(project_out(hid, wo_3, []), 1)
+            y2 = over_row(project_out(hid, wo_2, [d3], half=1))
+            x_parts.append(partner(project_out(hid, wo_2, [d3, y2], half=0), 2))
             start += size
-        main = project_out(hid_own, wo_0, [d1_own], parts=y0, residual=x_rows, bias=b_down)
+        main = project_out(hid, wo_0, [d1_own], half=0, parts=y0, residual=x_rows, bias=b_down)
         out = join_last(main, x_parts[-1], join_parts(main, x_parts[:-1]))
         return out.reshape(imgs, seq_len, width)
 

time: 2200 us -> 2250 us (1.023)
  Pallas kernels: 1150 us -> 1200 us
    ppermute x10 -> x9, waiting for transfers between devices: 237 us -> 344 us  [over_row(): return lax.ppermute(arr, 'row', [(i, i ^ 1) for i in range(row_size)])]
    ppermute x52 -> x48, waiting for transfers between devices: 639 us -> 537 us  [partner(): return lax.ppermute(arr, 'col', [(i, i ^ shift) for i in range(col_size)])]
    pallas_call x14 -> x10, Pallas kernels: 542 us -> 574 us  [project_in(): pl.pallas_call(functools.partial(block_matmul, n_blocks, bias is not None...]
    pallas_call x23 -> x18, Pallas kernels: 471 us -> 462 us  [project_out(): pl.pallas_call(functools.partial(out_matmul, len(hidden), len(adds), len(...]
    pallas_call x2 -> x1, Pallas kernels: 47.7 us -> 45.7 us  [attention(): pl.pallas_call(functools.partial(attend, head_dim), out_shape=jax.ShapeDt...]
  transfers between devices with their start and end apart: 62 -> 57, of which waited for: 23 -> 18; matrix products, arithmetic and copies ran while one was open for 5% -> 5% of each run, Pallas kernels for 52% -> 53%
where the time goes in v2:
time: 2250 us; the launch traced here: 2240 us
  Pallas kernels  1200 us (53%)
  waiting for transfers between devices  881 us (39%)
  local copies, waits for them, and re-layouts  81.2 us (4%)
  starting transfers between devices  50.7 us (2%)
  other arithmetic  30 us (1%)
    pallas_call x10, Pallas kernels, project_in(): pl.pallas_call(functools.partial(block_matmul, n_blocks, bias is not None...  574 us
    ppermute x48, waiting for transfers between devices, partner(): return lax.ppermute(arr, 'col', [(i, i ^ shift) for i in range(col_size)])  537 us
    pallas_call x18, Pallas kernels, project_out(): pl.pallas_call(functools.partial(out_matmul, len(hidden), len(adds), len(...  462 us
    ppermute x9, waiting for transfers between devices, over_row(): return lax.ppermute(arr, 'row', [(i, i ^ 1) for i in range(row_size)])  344 us
    pallas_call x2, Pallas kernels, normalise(): pl.pallas_call(functools.partial(normalise_tile, n_blocks), out_shape=[ja...  93.8 us
    pallas_call x1, Pallas kernels, attention(): pl.pallas_call(functools.partial(attend, head_dim), out_shape=jax.ShapeDt...  45.7 us
  transfers between devices with their start and end apart: 57, of which 18 were waited for; matrix products, arithmetic and copies ran while one was open for 5% of the time, Pallas kernels for 53%

profile of v2, /device:TPU:0, one launch (start us, length us, event | category | flops | bytes accessed | tf_op | source)
XLA Modules:
  0.0 2242.5 jit_solution(16320116408852414401)
XLA Ops:
  0.0 3.3 collective-permute-start.2
  4.8 201.7 %collective-permute-done.2.refs_2_ = bf16[3072,1536]{1,0:T(8,128)(2,1)} collective-permute-done((bf16[3072,1536]{1,0:T(8,128)(2,1)}, bf16[3072,1536]{1,0:T(8,128)(2,1)}, u32[]{:S(2)}, u32[]{:S(2)}) %collective-permute-start.2) | collective-permute-done | bytes 9437216 | tf_op jit(solution)/shard_map/ppermute | solution.py:264
  208.8 2.2 constant_dynamic-slice_fusion.37
  213.1 5.7 constant_dynamic-slice_fusion.36
  218.8 5.4 constant_dynamic-slice_fusion.40
  224.2 2.2 pad_maximum_fusion.2
  228.2 2.1 pad_maximum_fusion.3
  230.3 2.3 pad_maximum_fusion.4
  232.5 2.1 pad_maximum_fusion.5
  234.7 19.2 constant_dynamic-slice_fusion.24
  253.9 11.6 constant_dynamic-slice_fusion.4
  265.4 5.3 pad_maximum_fusion.1
  270.8 25.4 %constant_dynamic-slice_fusion.8 = (bf16[1536,768]{1,0:T(8,128)(2,1)}, bf16[1536,768]{1,0:T(8,128)(2,1)}, bf16[1536,768]{1,0:T(8,128)(2,1)}, bf16[1536,768]{1,0:...) fusion(bf16[1536,12288]{1,0:T(8,128)(2,1)} %param.16, ...), kind=kLoop, calls=%fused_computation.18 | loop fusion | bytes 75497536 | tf_op jit(solution)/shard_map/dynamic_slice | solution.py:276
  296.7 114.2 %collective-permute-done.3.refs_2_ = bf16[3072,1536]{1,0:T(8,128)(2,1)} collective-permute-done((bf16[3072,1536]{1,0:T(8,128)(2,1)}, bf16[3072,1536]{1,0:T(8,128)(2,1)}, u32[]{:S(2)}, u32[]{:S(2)}) %collective-permute-start.3) | collective-permute-done | bytes 9437216 | tf_op jit(solution)/shard_map/ppermute | solution.py:267
  411.0 2.5 pad_maximum_fusion.6
  427.3 9.3 pad_maximum_fusion.refs_5_
  438.4 46.9 %shard_map.100 = (bf16[6144,1536]{1,0:T(8,128)(2,1)}, bf16[6144,1536]{1,0:T(8,128)(2,1)}, bf16[6144,1536]{1,0:T(8,128)(2,1)}, bf16[6144,1536]{1,0:T(8,128)(2,1)}) custom-call(bf16[3072,1536]{1,0:T(8,128)(2,1)} %bitcast.9, bf16[3072,1536]{1,0:T(8,128)(2,1)} %collective-permute-done.8.refs_1_, bf16[3072,1536]{1,0:T(8,128)(2,1)} %collective-permute-done.2.refs_2_, ...), custom_call_target="tpu_custom_call" | custom-call | flops 11324620800 | bytes 75497472 | tf_op jit(solution)/shard_map/pallas_call | solution.py:54
  486.7 42.4 %collective-permute-done.15.refs_7_ = bf16[1536,768]{1,0:T(8,128)(2,1)} collective-permute-done((bf16[1536,768]{1,0:T(8,128)(2,1)}, bf16[1536,768]{1,0:T(8,128)(2,1)}, u32[]{:S(2)}, u32[]{:S(2)}) %collective-permute-start.15) | collective-permute-done | bytes 2359328 | tf_op jit(solution)/shard_map/ppermute | solution.py:264
  530.9 41.4 %shard_map.104.refs_8_ = bf16[6144,768]{1,0:T(8,128)(2,1)} custom-call(bf16[6144,1536]{1,0:T(8,128)(2,1)} %get-tuple-element.13.refs_8_.refs_0_, bf16[6144,1536]{1,0:T(8,128)(2,1)} %get-tuple-element.14.refs_9_.refs_1_, bf16[6144,1536]{1,0:T(8,128)(2,1)} %get-tuple-element.15.refs_10_.refs_2_, bf16[6144,1536]{1,0:T(8,128)(2,1)} %get-tuple-element.16.refs_11_.refs_3_, ...), custom_call_target="tpu_custom_call" | custom-call | flops 28991029248 | bytes 169869312 | tf_op jit(solution)/shard_map/pallas_call | solution.py:110
  572.4 9.1 collective-permute-done.11.refs_6_
  582.1 48.1 %collective-permute-done.12.refs_7_ = bf16[1536,768]{1,0:T(8,128)(2,1)} collective-permute-done((bf16[1536,768]{1,0:T(8,128)(2,1)S(1)}, bf16[1536,768]{1,0:T(8,128)(2,1)}, u32[]{:S(2)}, u32[]{:S(2)}) %collective-permute-start.12) | collective-permute-done | bytes 2359328 | tf_op jit(solution)/shard_map/ppermute | solution.py:264
  632.0 41.4 %shard_map.102.refs_8_ = bf16[6144,768]{1,0:T(8,128)(2,1)} custom-call(bf16[6144,1536]{1,0:T(8,128)(2,1)} %get-tuple-element.13.refs_8_.refs_0_, bf16[6144,1536]{1,0:T(8,128)(2,1)} %get-tuple-element.14.refs_9_.refs_1_, bf16[6144,1536]{1,0:T(8,128)(2,1)} %get-tuple-element.15.refs_10_.refs_2_, bf16[6144,1536]{1,0:T(8,128)(2,1)} %get-tuple-element.16.refs_11_.refs_3_, ...), custom_call_target="tpu_custom_call" | custom-call | flops 28991029248 | bytes 169869312 | tf_op jit(solution)/shard_map/pallas_call | solution.py:110
  675.0 46.9 %shard_map.101 = (bf16[6144,1536]{1,0:T(8,128)(2,1)}, bf16[6144,1536]{1,0:T(8,128)(2,1)}, bf16[6144,1536]{1,0:T(8,128)(2,1)}, bf16[6144,1536]{1,0:T(8,128)(2,1)}) custom-call(bf16[3072,1536]{1,0:T(8,128)(2,1)} %collective-permute-done.refs_0_, ...), custom_call_target="tpu_custom_call", output_to_operand_aliasing={{0}: (8, {}), {1}: (9, {}), {2}: (10, {}), {3}: (11, {})} | custom-call | flops 11324620800 | bytes 75497472 | tf_op jit(solution)/shard_map/pallas_call | solution.py:54
  722.7 8.6 collective-permute-done.18.refs_7_
  732.7 77.3 %shard_map.106.refs_2_ = bf16[6144,768]{1,0:T(8,128)(2,1)} custom-call(bf16[6144,1536]{1,0:T(8,128)(2,1)} %get-tuple-element.17.refs_0_, bf16[6144,1536]{1,0:T(8,128)(2,1)} %get-tuple-element.18.refs_1_, bf16[6144,1536]{1,0:T(8,128)(2,1)} %get-tuple-element.19.refs_2_, bf16[6144,1536]{1,0:T(8,128)(2,1)} %get-tuple-element.20.refs_3_, ...), custom_call_target="tpu_custom_call" | custom-call | flops 57982058496 | bytes 169869312 | tf_op jit(solution)/shard_map/pallas_call | solution.py:110
  811.6 20.8 collective-permute-done.21.refs_7_
  834.1 81.3 %shard_map.108.refs_1_ = bf16[6144,768]{1,0:T(8,128)(2,1)} custom-call(bf16[6144,1536]{1,0:T(8,128)(2,1)} %get-tuple-element.17.refs_0_, bf16[6144,1536]{1,0:T(8,128)(2,1)} %get-tuple-element.18.refs_1_, bf16[6144,1536]{1,0:T(8,128)(2,1)} %get-tuple-element.19.refs_2_, bf16[6144,1536]{1,0:T(8,128)(2,1)} %get-tuple-element.20.refs_3_, ...), custom_call_target="tpu_custom_call" | custom-call | flops 57982058496 | bytes 169869312 | tf_op jit(solution)/shard_map/pallas_call | solution.py:110
  915.4 41.6 %shard_map.103.refs_0_ = bf16[6144,768]{1,0:T(8,128)(2,1)} custom-call(bf16[6144,1536]{1,0:T(8,128)(2,1)} %get-tuple-element.17.refs_0_, bf16[6144,1536]{1,0:T(8,128)(2,1)} %get-tuple-element.18.refs_1_, bf16[6144,1536]{1,0:T(8,128)(2,1)} %get-tuple-element.19.refs_2_, bf16[6144,1536]{1,0:T(8,128)(2,1)} %get-tuple-element.20.refs_3_, ...), custom_call_target="tpu_custom_call", output_to_operand_aliasing={{}: (8, {})} | custom-call | flops 28991029248 | bytes 169869312 | tf_op jit(solution)/shard_map/pallas_call | solution.py:110
  959.2 81.3 %shard_map.109.refs_2_ = bf16[6144,768]{1,0:T(8,128)(2,1)} custom-call(bf16[6144,1536]{1,0:T(8,128)(2,1)} %get-tuple-element.17.refs_0_, bf16[6144,1536]{1,0:T(8,128)(2,1)} %get-tuple-element.18.refs_1_, bf16[6144,1536]{1,0:T(8,128)(2,1)} %get-tuple-element.19.refs_2_, bf16[6144,1536]{1,0:T(8,128)(2,1)} %get-tuple-element.20.refs_3_, ...), custom_call_target="tpu_custom_call" | custom-call | flops 57982058496 | bytes 169869312 | tf_op jit(solution)/shard_map/pallas_call | solution.py:110
  1040.4 41.5 %shard_map.105.refs_1_ = bf16[6144,768]{1,0:T(8,128)(2,1)} custom-call(bf16[6144,1536]{1,0:T(8,128)(2,1)} %get-tuple-element.17.refs_0_, bf16[6144,1536]{1,0:T(8,128)(2,1)} %get-tuple-element.18.refs_1_, bf16[6144,1536]{1,0:T(8,128)(2,1)} %get-tuple-element.19.refs_2_, bf16[6144,1536]{1,0:T(8,128)(2,1)} %get-tuple-element.20.refs_3_, ...), custom_call_target="tpu_custom_call", output_to_operand_aliasing={{}: (8, {})} | custom-call | flops 28991029248 | bytes 169869312 | tf_op jit(solution)/shard_map/pallas_call | solution.py:110
  1081.9 45.7 %shard_map.107.refs_0_ = bf16[6144,768]{1,0:T(8,128)(2,1)} custom-call(f32[1,128]{1,0:T(1,128)} %bitcast.11, f32[1,128]{1,0:T(1,128)} %bitcast.12, bf16[6144,768]{1,0:T(8,128)(2,1)} %shard_map.103.refs_0_, bf16[6144,768]{1,0:T(8,128)(2,1)} %shard_map.105.refs_1_, bf16[6144,768]{1,0:T(8,128)(2,1)} %shard_map.106.refs_2_), custom_call_target="tpu_custom_call" | custom-call | flops 38654705664 | bytes 28311552 | tf_op jit(solution)/shard_map/pallas_call | solution.py:248
  1129.7 43.6 %shard_map.111.refs_9_.refs_4_ = bf16[6144,768]{1,0:T(8,128)(2,1)} custom-call(bf16[6144,1536]{1,0:T(8,128)(2,1)} %get-tuple-element.17.refs_0_, bf16[6144,1536]{1,0:T(8,128)(2,1)} %get-tuple-element.18.refs_1_, bf16[6144,1536]{1,0:T(8,128)(2,1)} %get-tuple-element.19.refs_2_, bf16[6144,1536]{1,0:T(8,128)(2,1)} %get-tuple-element.20.refs_3_, ...), custom_call_target="tpu_custom_call" | custom-call | flops 28991029248 | bytes 169869312 | tf_op jit(solution)/shard_map/pallas_call | solution.py:110
  1174.8 7.3 collective-permute-done.26.refs_6_
  1182.6 48.4 %collective-permute-done.27.refs_7_ = bf16[1536,768]{1,0:T(8,128)(2,1)} collective-permute-done((bf16[1536,768]{1,0:T(8,128)(2,1)}, bf16[1536,768]{1,0:T(8,128)(2,1)}, u32[]{:S(2)}, u32[]{:S(2)}) %collective-permute-start.27) | collective-permute-done | bytes 2359328 | tf_op jit(solution)/shard_map/ppermute | solution.py:264
  1232.6 81.3 %shard_map.110.refs_3_ = bf16[6144,768]{1,0:T(8,128)(2,1)} custom-call(bf16[6144,1536]{1,0:T(8,128)(2,1)} %get-tuple-element.17.refs_0_, bf16[6144,1536]{1,0:T(8,128)(2,1)} %get-tuple-element.18.refs_1_, bf16[6144,1536]{1,0:T(8,128)(2,1)} %get-tuple-element.19.refs_2_, bf16[6144,1536]{1,0:T(8,128)(2,1)} %get-tuple-element.20.refs_3_, ...), custom_call_target="tpu_custom_call" | custom-call | flops 57982058496 | bytes 169869312 | tf_op jit(solution)/shard_map/pallas_call | solution.py:110
  1314.1 50.0 %shard_map.114 = bf16[3072,1536]{1,0:T(8,128)(2,1)} custom-call(bf16[6144,768]{1,0:T(8,128)(2,1)} %shard_map.107.refs_0_, bf16[6144,768]{1,0:T(8,128)(2,1)} %shard_map.108.refs_1_, bf16[6144,768]{1,0:T(8,128)(2,1)} %shard_map.109.refs_2_, bf16[6144,768]{1,0:T(8,128)(2,1)} %shard_map.110.refs_3_, bf16[6144,768]{1,0:T(8,128)(2,1)} %shard_map.111.refs_9_.refs_4_, ...), custom_call_target="tpu_custom_call" | custom-call | flops 36238786560 | bytes 35389440 | tf_op jit(solution)/shard_map/pallas_call | solution.py:171
  1364.1 43.5 %shard_map.112.refs_4_ = bf16[6144,768]{1,0:T(8,128)(2,1)} custom-call(bf16[6144,1536]{1,0:T(8,128)(2,1)} %get-tuple-element.17.refs_0_, bf16[6144,1536]{1,0:T(8,128)(2,1)} %get-tuple-element.18.refs_1_, bf16[6144,1536]{1,0:T(8,128)(2,1)} %get-tuple-element.19.refs_2_, bf16[6144,1536]{1,0:T(8,128)(2,1)} %get-tuple-element.20.refs_3_, ...), custom_call_target="tpu_custom_call", output_to_operand_aliasing={{}: (9, {})} | custom-call | flops 28991029248 | bytes 169869312 | tf_op jit(solution)/shard_map/pallas_call | solution.py:110
  1407.6 76.2 %collective-permute-done.43.refs_5_ = bf16[3840,512]{1,0:T(8,128)(2,1)} collective-permute-done((bf16[3840,512]{1,0:T(8,128)(2,1)S(1)}, bf16[3840,512]{1,0:T(8,128)(2,1)}, u32[]{:S(2)}, u32[]{:S(2)}) %collective-permute-start.43) | collective-permute-done | bytes 3932192 | tf_op jit(solution)/shard_map/ppermute | solution.py:264
  1484.8 33.4 %shard_map.122 = bf16[6144,512]{1,0:T(8,128)(2,1)} custom-call(bf16[6144,768]{1,0:T(8,128)(2,1)} %shard_map.107.refs_0_, bf16[6144,768]{1,0:T(8,128)(2,1)} %shard_map.108.refs_1_, bf16[6144,768]{1,0:T(8,128)(2,1)} %shard_map.109.refs_2_, bf16[6144,768]{1,0:T(8,128)(2,1)} %shard_map.110.refs_3_, bf16[6144,768]{1,0:T(8,128)(2,1)} %shard_map.112.refs_4_, ...), custom_call_target="tpu_custom_call" | custom-call | flops 24159191040 | bytes 51118080 | tf_op jit(solution)/shard_map/pallas_call | solution.py:171
  1520.3 24.1 %shard_map.119 = bf16[6144,256]{1,0:T(8,128)(2,1)} custom-call(bf16[6144,768]{1,0:T(8,128)(2,1)} %shard_map.107.refs_0_, bf16[6144,768]{1,0:T(8,128)(2,1)} %shard_map.108.refs_1_, bf16[6144,768]{1,0:T(8,128)(2,1)} %shard_map.109.refs_2_, bf16[6144,768]{1,0:T(8,128)(2,1)} %shard_map.110.refs_3_, bf16[6144,768]{1,0:T(8,128)(2,1)} %shard_map.112.refs_4_, ...), custom_call_target="tpu_custom_call" | custom-call | flops 12079595520 | bytes 49152000 | tf_op jit(solution)/shard_map/pallas_call | solution.py:171
  1544.4 67.3 %collective-permute-done.52.refs_5_ = bf16[3840,256]{1,0:T(8,128)(2,1)S(1)} collective-permute-done((bf16[3840,256]{1,0:T(8,128)(2,1)}, bf16[3840,256]{1,0:T(8,128)(2,1)S(1)}, u32[]{:S(2)}, u32[]{:S(2)}) %collective-permute-start.52) | collective-permute-done | bytes 1966112 | tf_op jit(solution)/shard_map/ppermute | solution.py:264
  1612.2 33.6 %shard_map.125 = bf16[6144,512]{1,0:T(8,128)(2,1)} custom-call(bf16[6144,768]{1,0:T(8,128)(2,1)} %shard_map.107.refs_0_, bf16[6144,768]{1,0:T(8,128)(2,1)} %shard_map.108.refs_1_, bf16[6144,768]{1,0:T(8,128)(2,1)} %shard_map.109.refs_2_, bf16[6144,768]{1,0:T(8,128)(2,1)} %shard_map.110.refs_3_, bf16[6144,768]{1,0:T(8,128)(2,1)} %shard_map.112.refs_4_, ...), custom_call_target="tpu_custom_call" | custom-call | flops 24159191040 | bytes 51118080 | tf_op jit(solution)/shard_map/pallas_call | solution.py:171
  1645.8 6.6 collective-permute-done.53.refs_5_
  1653.0 24.1 %shard_map.128 = bf16[6144,256]{1,0:T(8,128)(2,1)} custom-call(bf16[6144,768]{1,0:T(8,128)(2,1)} %shard_map.107.refs_0_, bf16[6144,768]{1,0:T(8,128)(2,1)} %shard_map.108.refs_1_, bf16[6144,768]{1,0:T(8,128)(2,1)} %shard_map.109.refs_2_, bf16[6144,768]{1,0:T(8,128)(2,1)} %shard_map.110.refs_3_, bf16[6144,768]{1,0:T(8,128)(2,1)} %shard_map.112.refs_4_, ...), custom_call_target="tpu_custom_call" | custom-call | flops 12079595520 | bytes 49152000 | tf_op jit(solution)/shard_map/pallas_call | solution.py:171
  1677.6 50.0 %shard_map.113 = bf16[3072,1536]{1,0:T(8,128)(2,1)} custom-call(bf16[6144,768]{1,0:T(8,128)(2,1)} %shard_map.107.refs_0_, bf16[6144,768]{1,0:T(8,128)(2,1)} %shard_map.108.refs_1_, bf16[6144,768]{1,0:T(8,128)(2,1)} %shard_map.109.refs_2_, bf16[6144,768]{1,0:T(8,128)(2,1)} %shard_map.110.refs_3_, bf16[6144,768]{1,0:T(8,128)(2,1)} %shard_map.112.refs_4_, ...), custom_call_target="tpu_custom_call" | custom-call | flops 36238786560 | bytes 35389440 | tf_op jit(solution)/shard_map/pallas_call | solution.py:171
  1727.6 13.7 shard_map.120
  1741.9 13.8 shard_map.129
  1757.2 19.2 shard_map.123
  1778.5 19.3 shard_map.126
  1798.3 19.2 shard_map.115
  1817.5 19.2 shard_map.116
  1836.8 19.3 shard_map.117
  1858.2 36.2 %collective-permute-done.45.refs_7_ = bf16[3072,512]{1,0:T(8,128)(2,1)} collective-permute-done((bf16[3072,512]{1,0:T(8,128)(2,1)}, bf16[3072,512]{1,0:T(8,128)(2,1)}, u32[]{:S(2)}, u32[]{:S(2)}) %collective-permute-start.45) | collective-permute-done | bytes 3145760 | tf_op jit(solution)/shard_map/ppermute | solution.py:267
  1895.9 14.3 shard_map.121
  1910.2 14.4 shard_map.130
  1924.6 20.1 shard_map.124
  1944.6 17.2 collective-permute-done.50.refs_7_
  1963.3 20.1 shard_map.127
  1983.9 45.3 %collective-permute-done.34.refs_7_ = bf16[3072,512]{1,0:T(8,128)(2,1)} collective-permute-done((bf16[3072,512]{1,0:T(8,128)(2,1)}, bf16[3072,512]{1,0:T(8,128)(2,1)}, u32[]{:S(2)}, u32[]{:S(2)}) %collective-permute-start.34) | collective-permute-done | bytes 3145760 | tf_op jit(solution)/shard_map/ppermute | solution.py:267
  2030.7 65.9 %collective-permute-done.35.refs_8_ = bf16[3072,512]{1,0:T(8,128)(2,1)} collective-permute-done((bf16[3072,512]{1,0:T(8,128)(2,1)S(1)}, bf16[3072,512]{1,0:T(8,128)(2,1)}, u32[]{:S(2)}, u32[]{:S(2)}) %collective-permute-start.35) | collective-permute-done | bytes 3145760 | tf_op jit(solution)/shard_map/ppermute | solution.py:267
  2098.1 65.2 %collective-permute-done.36.refs_9_ = bf16[3072,512]{1,0:T(8,128)(2,1)} collective-permute-done((bf16[3072,512]{1,0:T(8,128)(2,1)}, bf16[3072,512]{1,0:T(8,128)(2,1)}, u32[]{:S(2)}, u32[]{:S(2)}) %collective-permute-start.36) | collective-permute-done | bytes 3145760 | tf_op jit(solution)/shard_map/ppermute | solution.py:267
  2163.3 54.2 %shard_map.118.main_ref = f32[3072,1536]{1,0:T(8,128)} custom-call(bf16[6144,768]{1,0:T(8,128)(2,1)} %shard_map.107.refs_0_, bf16[6144,768]{1,0:T(8,128)(2,1)} %shard_map.108.refs_1_, bf16[6144,768]{1,0:T(8,128)(2,1)} %shard_map.109.refs_2_, bf16[6144,768]{1,0:T(8,128)(2,1)} %shard_map.110.refs_3_, bf16[6144,768]{1,0:T(8,128)(2,1)} %shard_map.112.refs_4_, ...), custom_call_target="tpu_custom_call" | custom-call | flops 36238786560 | bytes 35389440 | tf_op jit(solution)/shard_map/pallas_call | solution.py:171
  2219.2 19.1 shard_map.131.held_ref
  2238.3 4.2 shard_map.132
  (150 shorter events, 64.2 us)
Async XLA Ops:
  0.0 206.5 %collective-permute-start.2 = (bf16[3072,1536]{1,0:T(8,128)(2,1)}, bf16[3072,1536]{1,0:T(8,128)(2,1)}, u32[]{:S(2)}, u32[]{:S(2)}) collective-permute-start(bf16[3072,1536]{1,0:T(8,128)(2,1)} %bitcast.6), channel_id=1, source_target_pairs={{0,2},{1,3},{2,0},{3,1},{4,6},{5,7},{6,4},{7,5}} | collective-permute-start | bytes 28311560 | tf_op jit(solution)/shard_map/ppermute | solution.py:264
  3.3 292.9 %collective-permute-start = (bf16[3072,1536]{1,0:T(8,128)(2,1)}, bf16[3072,1536]{1,0:T(8,128)(2,1)}, u32[]{:S(2)}, u32[]{:S(2)}) collective-permute-start(bf16[3072,1536]{1,0:T(8,128)(2,1)} %bitcast.7), channel_id=1, source_target_pairs={{0,4},{4,0},{1,5},{5,1},{2,6},{6,2},{3,7},{7,3}} | collective-permute-start | bytes 28311560 | tf_op jit(solution)/shard_map/ppermute | solution.py:267
  206.5 204.4 %collective-permute-start.3 = (bf16[3072,1536]{1,0:T(8,128)(2,1)}, bf16[3072,1536]{1,0:T(8,128)(2,1)}, u32[]{:S(2)}, u32[]{:S(2)}) collective-permute-start(bf16[3072,1536]{1,0:T(8,128)(2,1)} %collective-permute-done.2.refs_2_), channel_id=1, source_target_pairs={{0,4},{4,0},{1,5},{5,1},{2,6},{6,2},{3,7},{7,3}} | collective-permute-start | bytes 28311560 | tf_op jit(solution)/shard_map/ppermute | solution.py:267
  208.3 217.6 %collective-permute-start.8 = (bf16[3072,1536]{1,0:T(8,128)(2,1)}, bf16[3072,1536]{1,0:T(8,128)(2,1)}, u32[]{:S(2)}, u32[]{:S(2)}) collective-permute-start(bf16[3072,1536]{1,0:T(8,128)(2,1)} %bitcast.8), channel_id=1, source_target_pairs={{0,1},{1,0},{2,3},{3,2},{4,5},{5,4},{6,7},{7,6}} | collective-permute-start | bytes 28311560 | tf_op jit(solution)/shard_map/ppermute | solution.py:264
  208.3 208.0 %collective-permute-start.5 = (f32[1536]{0:T(1024)}, f32[1536]{0:T(1024)S(1)}, u32[]{:S(2)}, u32[]{:S(2)}) collective-permute-start(f32[1536]{0:T(1024)} %param.11), channel_id=1, source_target_pairs={{0,1},{1,0},{2,3},{3,2},{4,5},{5,4},{6,7},{7,6}} | collective-permute-start | bytes 18440 | tf_op jit(solution)/shard_map/ppermute | solution.py:264
  226.4 200.1 %collective-permute-start.9 = (bf16[3072,1536]{1,0:T(8,128)(2,1)}, bf16[3072,1536]{1,0:T(8,128)(2,1)}, u32[]{:S(2)}, u32[]{:S(2)}) collective-permute-start(bf16[3072,1536]{1,0:T(8,128)(2,1)} %collective-permute-done.2.refs_2_), channel_id=1, source_target_pairs={{0,1},{1,0},{2,3},{3,2},{4,5},{5,4},{6,7},{7,6}} | collective-permute-start | bytes 28311560 | tf_op jit(solution)/shard_map/ppermute | solution.py:264
  270.8 140.2 %copy-start.6 = (bf16[3072,256]{1,0:T(8,128)(2,1)S(1)}, bf16[3072,256]{1,0:T(8,128)(2,1)}, u32[]{:S(2)}) copy-start(bf16[3072,256]{1,0:T(8,128)(2,1)} %get-tuple-element.23) | copy-start | bytes 4718596
  296.2 117.3 %copy-start.5 = (bf16[3072,256]{1,0:T(8,128)(2,1)S(1)}, bf16[3072,256]{1,0:T(8,128)(2,1)}, u32[]{:S(2)}) copy-start(bf16[3072,256]{1,0:T(8,128)(2,1)} %get-tuple-element.22) | copy-start | bytes 4718596
  296.2 377.2 %collective-permute-start.1 = (bf16[3072,1536]{1,0:T(8,128)(2,1)}, bf16[3072,1536]{1,0:T(8,128)(2,1)}, u32[]{:S(2)}, u32[]{:S(2)}) collective-permute-start(bf16[3072,1536]{1,0:T(8,128)(2,1)} %collective-permute-done.refs_0_), channel_id=1, source_target_pairs={{0,1},{1,0},{2,3},{3,2},{4,5},{5,4},{6,7},{7,6}} | collective-permute-start | bytes 28311560 | tf_op jit(solution)/shard_map/ppermute | solution.py:264
  411.0 262.5 %collective-permute-start.4 = (bf16[3072,1536]{1,0:T(8,128)(2,1)}, bf16[3072,1536]{1,0:T(8,128)(2,1)}, u32[]{:S(2)}, u32[]{:S(2)}) collective-permute-start(bf16[3072,1536]{1,0:T(8,128)(2,1)} %collective-permute-done.3.refs_2_), channel_id=1, source_target_pairs={{0,1},{1,0},{2,3},{3,2},{4,5},{5,4},{6,7},{7,6}} | collective-permute-start | bytes 28311560 | tf_op jit(solution)/shard_map/ppermute | solution.py:264
  416.3 3.7 collective-permute-start.6
  419.9 4.8 collective-permute-start.7
  424.8 60.5 %collective-permute-start.13 = (bf16[1536,768]{1,0:T(8,128)(2,1)}, bf16[1536,768]{1,0:T(8,128)(2,1)}, u32[]{:S(2)}, u32[]{:S(2)}) collective-permute-start(bf16[1536,768]{1,0:T(8,128)(2,1)} %get-tuple-element.52), channel_id=1, source_target_pairs={{0,1},{1,0},{2,3},{3,2},{4,5},{5,4},{6,7},{7,6}} | collective-permute-start | bytes 7077896 | tf_op jit(solution)/shard_map/ppermute | solution.py:264
  425.9 60.2 %collective-permute-start.14 = (bf16[1536,768]{1,0:T(8,128)(2,1)}, bf16[1536,768]{1,0:T(8,128)(2,1)}, u32[]{:S(2)}, u32[]{:S(2)}) collective-permute-start(bf16[1536,768]{1,0:T(8,128)(2,1)} %get-tuple-element.51), channel_id=1, source_target_pairs={{0,2},{1,3},{2,0},{3,1},{4,6},{5,7},{6,4},{7,5}} | collective-permute-start | bytes 7077896 | tf_op jit(solution)/shard_map/ppermute | solution.py:264
  426.5 102.5 %collective-permute-start.15 = (bf16[1536,768]{1,0:T(8,128)(2,1)}, bf16[1536,768]{1,0:T(8,128)(2,1)}, u32[]{:S(2)}, u32[]{:S(2)}) collective-permute-start(bf16[1536,768]{1,0:T(8,128)(2,1)} %get-tuple-element.50), channel_id=1, source_target_pairs={{0,3},{1,2},{2,1},{3,0},{4,7},{5,6},{6,5},{7,4}} | collective-permute-start | bytes 7077896 | tf_op jit(solution)/shard_map/ppermute | solution.py:264
  438.4 90.7 %copy-start.12 = (bf16[1536,768]{1,0:T(8,128)(2,1)S(1)}, bf16[1536,768]{1,0:T(8,128)(2,1)}, u32[]{:S(2)}) copy-start(bf16[1536,768]{1,0:T(8,128)(2,1)} %get-tuple-element.54) | copy-start | bytes 7077892
  485.3 87.0 %collective-permute-start.10 = (bf16[1536,768]{1,0:T(8,128)(2,1)}, bf16[1536,768]{1,0:T(8,128)(2,1)}, u32[]{:S(2)}, u32[]{:S(2)}) collective-permute-start(bf16[1536,768]{1,0:T(8,128)(2,1)} %get-tuple-element.56), channel_id=1, source_target_pairs={{0,1},{1,0},{2,3},{3,2},{4,5},{5,4},{6,7},{7,6}} | collective-permute-start | bytes 7077896 | tf_op jit(solution)/shard_map/ppermute | solution.py:264
  486.1 95.4 %collective-permute-start.11 = (bf16[1536,768]{1,0:T(8,128)(2,1)}, bf16[1536,768]{1,0:T(8,128)(2,1)}, u32[]{:S(2)}, u32[]{:S(2)}) collective-permute-start(bf16[1536,768]{1,0:T(8,128)(2,1)} %get-tuple-element.55), channel_id=1, source_target_pairs={{0,2},{1,3},{2,0},{3,1},{4,6},{5,7},{6,4},{7,5}} | collective-permute-start | bytes 7077896 | tf_op jit(solution)/shard_map/ppermute | solution.py:264
  529.0 101.1 %collective-permute-start.12 = (bf16[1536,768]{1,0:T(8,128)(2,1)S(1)}, bf16[1536,768]{1,0:T(8,128)(2,1)}, u32[]{:S(2)}, u32[]{:S(2)}) collective-permute-start(bf16[1536,768]{1,0:T(8,128)(2,1)S(1)} %copy-done.12), channel_id=1, source_target_pairs={{0,3},{1,2},{2,1},{3,0},{4,7},{5,6},{6,5},{7,4}} | collective-permute-start | bytes 7077896 | tf_op jit(solution)/shard_map/ppermute | solution.py:264
  572.4 149.6 %collective-permute-start.16 = (bf16[1536,768]{1,0:T(8,128)(2,1)}, bf16[1536,768]{1,0:T(8,128)(2,1)}, u32[]{:S(2)}, u32[]{:S(2)}) collective-permute-start(bf16[1536,768]{1,0:T(8,128)(2,1)} %get-tuple-element.48), channel_id=1, source_target_pairs={{0,1},{1,0},{2,3},{3,2},{4,5},{5,4},{6,7},{7,6}} | collective-permute-start | bytes 7077896 | tf_op jit(solution)/shard_map/ppermute | solution.py:264
  581.5 140.9 %collective-permute-start.17 = (bf16[1536,768]{1,0:T(8,128)(2,1)}, bf16[1536,768]{1,0:T(8,128)(2,1)}, u32[]{:S(2)}, u32[]{:S(2)}) collective-permute-start(bf16[1536,768]{1,0:T(8,128)(2,1)} %get-tuple-element.58), channel_id=1, source_target_pairs={{0,2},{1,3},{2,0},{3,1},{4,6},{5,7},{6,4},{7,5}} | collective-permute-start | bytes 7077896 | tf_op jit(solution)/shard_map/ppermute | solution.py:264
  630.2 101.1 %collective-permute-start.18 = (bf16[1536,768]{1,0:T(8,128)(2,1)}, bf16[1536,768]{1,0:T(8,128)(2,1)}, u32[]{:S(2)}, u32[]{:S(2)}) collective-permute-start(bf16[1536,768]{1,0:T(8,128)(2,1)} %get-tuple-element.47), channel_id=1, source_target_pairs={{0,3},{1,2},{2,1},{3,0},{4,7},{5,6},{6,5},{7,4}} | collective-permute-start | bytes 7077896 | tf_op jit(solution)/shard_map/ppermute | solution.py:264
  673.5 136.5 %collective-permute-start.19 = (bf16[1536,768]{1,0:T(8,128)(2,1)}, bf16[1536,768]{1,0:T(8,128)(2,1)}, u32[]{:S(2)}, u32[]{:S(2)}) collective-permute-start(bf16[1536,768]{1,0:T(8,128)(2,1)} %get-tuple-element.44), channel_id=1, source_target_pairs={{0,1},{1,0},{2,3},{3,2},{4,5},{5,4},{6,7},{7,6}} | collective-permute-start | bytes 7077896 | tf_op jit(solution)/shard_map/ppermute | solution.py:264
  673.5 48.4 %copy-start.11 = (bf16[1536,768]{1,0:T(8,128)(2,1)S(1)}, bf16[1536,768]{1,0:T(8,128)(2,1)}, u32[]{:S(2)}) copy-start(bf16[1536,768]{1,0:T(8,128)(2,1)} %get-tuple-element.42) | copy-start | bytes 7077892
  673.5 138.1 %collective-permute-start.20 = (bf16[1536,768]{1,0:T(8,128)(2,1)}, bf16[1536,768]{1,0:T(8,128)(2,1)}, u32[]{:S(2)}, u32[]{:S(2)}) collective-permute-start(bf16[1536,768]{1,0:T(8,128)(2,1)} %get-tuple-element.43), channel_id=1, source_target_pairs={{0,2},{1,3},{2,0},{3,1},{4,6},{5,7},{6,4},{7,5}} | collective-permute-start | bytes 7077896 | tf_op jit(solution)/shard_map/ppermute | solution.py:264
  721.9 110.5 %collective-permute-start.21 = (bf16[1536,768]{1,0:T(8,128)(2,1)S(1)}, bf16[1536,768]{1,0:T(8,128)(2,1)}, u32[]{:S(2)}, u32[]{:S(2)}) collective-permute-start(bf16[1536,768]{1,0:T(8,128)(2,1)S(1)} %copy-done.11), channel_id=1, source_target_pairs={{0,3},{1,2},{2,1},{3,0},{4,7},{5,6},{6,5},{7,4}} | collective-permute-start | bytes 7077896 | tf_op jit(solution)/shard_map/ppermute | solution.py:264
  722.4 234.5 %collective-permute-start.22 = (bf16[1536,768]{1,0:T(8,128)(2,1)}, bf16[1536,768]{1,0:T(8,128)(2,1)}, u32[]{:S(2)}, u32[]{:S(2)}) collective-permute-start(bf16[1536,768]{1,0:T(8,128)(2,1)} %get-tuple-element.40), channel_id=1, source_target_pairs={{0,1},{1,0},{2,3},{3,2},{4,5},{5,4},{6,7},{7,6}} | collective-permute-start | bytes 7077896 | tf_op jit(solution)/shard_map/ppermute | solution.py:264
  731.3 226.3 %collective-permute-start.23 = (bf16[1536,768]{1,0:T(8,128)(2,1)}, bf16[1536,768]{1,0:T(8,128)(2,1)}, u32[]{:S(2)}, u32[]{:S(2)}) collective-permute-start(bf16[1536,768]{1,0:T(8,128)(2,1)} %get-tuple-element.39), channel_id=1, source_target_pairs={{0,2},{1,3},{2,0},{3,1},{4,6},{5,7},{6,4},{7,5}} | collective-permute-start | bytes 7077896 | tf_op jit(solution)/shard_map/ppermute | solution.py:264
  810.0 148.4 %collective-permute-start.24 = (bf16[1536,768]{1,0:T(8,128)(2,1)}, bf16[1536,768]{1,0:T(8,128)(2,1)}, u32[]{:S(2)}, u32[]{:S(2)}) collective-permute-start(bf16[1536,768]{1,0:T(8,128)(2,1)} %get-tuple-element.38), channel_id=1, source_target_pairs={{0,3},{1,2},{2,1},{3,0},{4,7},{5,6},{6,5},{7,4}} | collective-permute-start | bytes 7077896 | tf_op jit(solution)/shard_map/ppermute | solution.py:264
  811.6 361.7 %collective-permute-start.25 = (bf16[1536,768]{1,0:T(8,128)(2,1)}, bf16[1536,768]{1,0:T(8,128)(2,1)}, u32[]{:S(2)}, u32[]{:S(2)}) collective-permute-start(bf16[1536,768]{1,0:T(8,128)(2,1)} %get-tuple-element.36), channel_id=1, source_target_pairs={{0,1},{1,0},{2,3},{3,2},{4,5},{5,4},{6,7},{7,6}} | collective-permute-start | bytes 7077896 | tf_op jit(solution)/shard_map/ppermute | solution.py:264
  832.4 295.2 %collective-permute-start.28 = (bf16[1536,768]{1,0:T(8,128)(2,1)}, bf16[1536,768]{1,0:T(8,128)(2,1)}, u32[]{:S(2)}, u32[]{:S(2)}) collective-permute-start(bf16[1536,768]{1,0:T(8,128)(2,1)} %get-tuple-element.32), channel_id=1, source_target_pairs={{0,1},{1,0},{2,3},{3,2},{4,5},{5,4},{6,7},{7,6}} | collective-permute-start | bytes 7077896 | tf_op jit(solution)/shard_map/ppermute | solution.py:264
  915.4 42.2 %copy-start.10 = (bf16[1536,768]{1,0:T(8,128)(2,1)S(1)}, bf16[1536,768]{1,0:T(8,128)(2,1)}, u32[]{:S(2)}) copy-start(bf16[1536,768]{1,0:T(8,128)(2,1)} %get-tuple-element.31) | copy-start | bytes 7077892
  957.0 171.2 %collective-permute-start.29 = (bf16[1536,768]{1,0:T(8,128)(2,1)}, bf16[1536,768]{1,0:T(8,128)(2,1)}, u32[]{:S(2)}, u32[]{:S(2)}) collective-permute-start(bf16[1536,768]{1,0:T(8,128)(2,1)} %get-tuple-element.46), channel_id=1, source_target_pairs={{0,2},{1,3},{2,0},{3,1},{4,6},{5,7},{6,4},{7,5}} | collective-permute-start | bytes 7077896 | tf_op jit(solution)/shard_map/ppermute | solution.py:264
  957.6 171.6 %collective-permute-start.30 = (bf16[1536,768]{1,0:T(8,128)(2,1)S(1)}, bf16[1536,768]{1,0:T(8,128)(2,1)}, u32[]{:S(2)}, u32[]{:S(2)}) collective-permute-start(bf16[1536,768]{1,0:T(8,128)(2,1)S(1)} %copy-done.10), channel_id=1, source_target_pairs={{0,3},{1,2},{2,1},{3,0},{4,7},{5,6},{6,5},{7,4}} | collective-permute-start | bytes 7077896 | tf_op jit(solution)/shard_map/ppermute | solution.py:264
  958.4 355.5 %collective-permute-start.31 = (bf16[3840,1536]{1,0:T(8,128)(2,1)}, bf16[3840,1536]{1,0:T(8,128)(2,1)}, u32[]{:S(2)}, u32[]{:S(2)}) collective-permute-start(bf16[3840,1536]{1,0:T(8,128)(2,1)} %pad_maximum_fusion.1), channel_id=1, source_target_pairs={{0,1},{1,0},{2,3},{3,2},{4,5},{5,4},{6,7},{7,6}} | collective-permute-start | bytes 35389448 | tf_op jit(solution)/shard_map/ppermute | solution.py:264
  1127.6 54.4 %collective-permute-start.26 = (bf16[1536,768]{1,0:T(8,128)(2,1)}, bf16[1536,768]{1,0:T(8,128)(2,1)}, u32[]{:S(2)}, u32[]{:S(2)}) collective-permute-start(bf16[1536,768]{1,0:T(8,128)(2,1)} %get-tuple-element.35), channel_id=1, source_target_pairs={{0,2},{1,3},{2,0},{3,1},{4,6},{5,7},{6,4},{7,5}} | collective-permute-start | bytes 7077896 | tf_op jit(solution)/shard_map/ppermute | solution.py:264
  1128.2 102.9 %collective-permute-start.27 = (bf16[1536,768]{1,0:T(8,128)(2,1)}, bf16[1536,768]{1,0:T(8,128)(2,1)}, u32[]{:S(2)}, u32[]{:S(2)}) collective-permute-start(bf16[1536,768]{1,0:T(8,128)(2,1)} %get-tuple-element.34), channel_id=1, source_target_pairs={{0,3},{1,2},{2,1},{3,0},{4,7},{5,6},{6,5},{7,4}} | collective-permute-start | bytes 7077896 | tf_op jit(solution)/shard_map/ppermute | solution.py:264
  1129.2 415.2 %collective-permute-start.37 = (bf16[3840,256]{1,0:T(8,128)(2,1)}, bf16[3840,256]{1,0:T(8,128)(2,1)}, u32[]{:S(2)}, u32[]{:S(2)}) collective-permute-start(bf16[3840,256]{1,0:T(8,128)(2,1)} %pad_maximum_fusion.6), channel_id=1, source_target_pairs={{0,2},{1,3},{2,0},{3,1},{4,6},{5,7},{6,4},{7,5}} | collective-permute-start | bytes 5898248 | tf_op jit(solution)/shard_map/ppermute | solution.py:264
  1129.7 101.3 %copy-start.7 = (bf16[3840,512]{1,0:T(8,128)(2,1)S(1)}, bf16[3840,512]{1,0:T(8,128)(2,1)}, u32[]{:S(2)}) copy-start(bf16[3840,512]{1,0:T(8,128)(2,1)} %pad_maximum_fusion.3) | copy-start | bytes 11796484
  1173.4 344.9 %collective-permute-start.38 = (bf16[3840,256]{1,0:T(8,128)(2,1)}, bf16[3840,256]{1,0:T(8,128)(2,1)}, u32[]{:S(2)}, u32[]{:S(2)}) collective-permute-start(bf16[3840,256]{1,0:T(8,128)(2,1)} %pad_maximum_fusion.7), channel_id=1, source_target_pairs={{0,3},{1,2},{2,1},{3,0},{4,7},{5,6},{6,5},{7,4}} | collective-permute-start | bytes 5898248 | tf_op jit(solution)/shard_map/ppermute | solution.py:264
  1182.0 495.0 %collective-permute-start.42 = (bf16[3840,512]{1,0:T(8,128)(2,1)}, bf16[3840,512]{1,0:T(8,128)(2,1)}, u32[]{:S(2)}, u32[]{:S(2)}) collective-permute-start(bf16[3840,512]{1,0:T(8,128)(2,1)} %pad_maximum_fusion.2), channel_id=1, source_target_pairs={{0,2},{1,3},{2,0},{3,1},{4,6},{5,7},{6,4},{7,5}} | collective-permute-start | bytes 11796488 | tf_op jit(solution)/shard_map/ppermute | solution.py:264
  1231.0 252.8 %collective-permute-start.43 = (bf16[3840,512]{1,0:T(8,128)(2,1)S(1)}, bf16[3840,512]{1,0:T(8,128)(2,1)}, u32[]{:S(2)}, u32[]{:S(2)}) collective-permute-start(bf16[3840,512]{1,0:T(8,128)(2,1)S(1)} %copy-done.7), channel_id=1, source_target_pairs={{0,3},{1,2},{2,1},{3,0},{4,7},{5,6},{6,5},{7,4}} | collective-permute-start | bytes 11796488 | tf_op jit(solution)/shard_map/ppermute | solution.py:264
  1313.9 297.8 %collective-permute-start.48 = (bf16[3840,512]{1,0:T(8,128)(2,1)}, bf16[3840,512]{1,0:T(8,128)(2,1)}, u32[]{:S(2)}, u32[]{:S(2)}) collective-permute-start(bf16[3840,512]{1,0:T(8,128)(2,1)} %pad_maximum_fusion.5), channel_id=1, source_target_pairs={{0,3},{1,2},{2,1},{3,0},{4,7},{5,6},{6,5},{7,4}} | collective-permute-start | bytes 11796488 | tf_op jit(solution)/shard_map/ppermute | solution.py:264
  1483.8 34.4 %copy-start.13 = (bf16[3840,256]{1,0:T(8,128)(2,1)S(1)}, bf16[3840,256]{1,0:T(8,128)(2,1)}, u32[]{:S(2)}) copy-start(bf16[3840,256]{1,0:T(8,128)(2,1)} %pad_maximum_fusion.9) | copy-start | bytes 5898244
  1483.8 127.8 %collective-permute-start.52 = (bf16[3840,256]{1,0:T(8,128)(2,1)}, bf16[3840,256]{1,0:T(8,128)(2,1)S(1)}, u32[]{:S(2)}, u32[]{:S(2)}) collective-permute-start(bf16[3840,256]{1,0:T(8,128)(2,1)} %pad_maximum_fusion.8), channel_id=1, source_target_pairs={{0,2},{1,3},{2,0},{3,1},{4,6},{5,7},{6,4},{7,5}} | collective-permute-start | bytes 5898248 | tf_op jit(solution)/shard_map/ppermute | solution.py:264
  1518.3 134.1 %collective-permute-start.53 = (bf16[3840,256]{1,0:T(8,128)(2,1)S(1)}, bf16[3840,256]{1,0:T(8,128)(2,1)}, u32[]{:S(2)}, u32[]{:S(2)}) collective-permute-start(bf16[3840,256]{1,0:T(8,128)(2,1)S(1)} %copy-done.13), channel_id=1, source_target_pairs={{0,3},{1,2},{2,1},{3,0},{4,7},{5,6},{6,5},{7,4}} | collective-permute-start | bytes 5898248 | tf_op jit(solution)/shard_map/ppermute | solution.py:264
  1544.4 253.4 %collective-permute-start.33 = (bf16[3072,1536]{1,0:T(8,128)(2,1)}, bf16[3072,1536]{1,0:T(8,128)(2,1)}, u32[]{:S(2)}, u32[]{:S(2)}) collective-permute-start(bf16[3072,1536]{1,0:T(8,128)(2,1)} %shard_map.114), channel_id=1, source_target_pairs={{0,1},{1,0},{2,3},{3,2},{4,5},{5,4},{6,7},{7,6}} | collective-permute-start | bytes 28311560 | tf_op jit(solution)/shard_map/ppermute | solution.py:264
  1611.7 65.9 %collective-permute-start.39 = (bf16[6144,256]{1,0:T(8,128)(2,1)}, bf16[6144,256]{1,0:T(8,128)(2,1)}, u32[]{:S(2)}, u32[]{:S(2)}) collective-permute-start(bf16[6144,256]{1,0:T(8,128)(2,1)} %shard_map.119), channel_id=1, source_target_pairs={{0,1},{1,0},{2,3},{3,2},{4,5},{5,4},{6,7},{7,6}} | collective-permute-start | bytes 9437192 | tf_op jit(solution)/shard_map/ppermute | solution.py:264
  1611.7 144.0 %collective-permute-start.44 = (bf16[6144,512]{1,0:T(8,128)(2,1)}, bf16[6144,512]{1,0:T(8,128)(2,1)}, u32[]{:S(2)}, u32[]{:S(2)}) collective-permute-start(bf16[6144,512]{1,0:T(8,128)(2,1)} %shard_map.122), channel_id=1, source_target_pairs={{0,1},{1,0},{2,3},{3,2},{4,5},{5,4},{6,7},{7,6}} | collective-permute-start | bytes 18874376 | tf_op jit(solution)/shard_map/ppermute | solution.py:264
  1652.4 124.6 %collective-permute-start.49 = (bf16[6144,512]{1,0:T(8,128)(2,1)}, bf16[6144,512]{1,0:T(8,128)(2,1)}, u32[]{:S(2)}, u32[]{:S(2)}) collective-permute-start(bf16[6144,512]{1,0:T(8,128)(2,1)} %shard_map.125), channel_id=1, source_target_pairs={{0,1},{1,0},{2,3},{3,2},{4,5},{5,4},{6,7},{7,6}} | collective-permute-start | bytes 18874376 | tf_op jit(solution)/shard_map/ppermute | solution.py:264
  1677.0 99.4 %collective-permute-start.47 = (bf16[3840,512]{1,0:T(8,128)(2,1)}, bf16[3840,512]{1,0:T(8,128)(2,1)S(1)}, u32[]{:S(2)}, u32[]{:S(2)}) collective-permute-start(bf16[3840,512]{1,0:T(8,128)(2,1)} %pad_maximum_fusion.4), channel_id=1, source_target_pairs={{0,2},{1,3},{2,0},{3,1},{4,6},{5,7},{6,4},{7,5}} | collective-permute-start | bytes 11796488 | tf_op jit(solution)/shard_map/ppermute | solution.py:264
  1677.6 63.8 %collective-permute-start.54 = (bf16[6144,256]{1,0:T(8,128)(2,1)}, bf16[6144,256]{1,0:T(8,128)(2,1)}, u32[]{:S(2)}, u32[]{:S(2)}) collective-permute-start(bf16[6144,256]{1,0:T(8,128)(2,1)} %shard_map.128), channel_id=1, source_target_pairs={{0,1},{1,0},{2,3},{3,2},{4,5},{5,4},{6,7},{7,6}} | collective-permute-start | bytes 9437192 | tf_op jit(solution)/shard_map/ppermute | solution.py:264
  1741.4 242.0 %collective-permute-start.32 = (bf16[3072,1536]{1,0:T(8,128)(2,1)}, bf16[3072,1536]{1,0:T(8,128)(2,1)}, u32[]{:S(2)}, u32[]{:S(2)}) collective-permute-start(bf16[3072,1536]{1,0:T(8,128)(2,1)} %shard_map.113), channel_id=1, source_target_pairs={{0,1},{1,0},{2,3},{3,2},{4,5},{5,4},{6,7},{7,6}} | collective-permute-start | bytes 28311560 | tf_op jit(solution)/shard_map/ppermute | solution.py:264
  1755.7 100.4 %collective-permute-start.40 = (bf16[3072,256]{1,0:T(8,128)(2,1)}, bf16[3072,256]{1,0:T(8,128)(2,1)}, u32[]{:S(2)}, u32[]{:S(2)}) collective-permute-start(bf16[3072,256]{1,0:T(8,128)(2,1)} %shard_map.120), channel_id=1, source_target_pairs={{0,4},{4,0},{1,5},{5,1},{2,6},{6,2},{3,7},{7,3}} | collective-permute-start | bytes 4718600 | tf_op jit(solution)/shard_map/ppermute | solution.py:267
  1776.4 81.2 %collective-permute-start.55 = (bf16[3072,256]{1,0:T(8,128)(2,1)}, bf16[3072,256]{1,0:T(8,128)(2,1)}, u32[]{:S(2)}, u32[]{:S(2)}) collective-permute-start(bf16[3072,256]{1,0:T(8,128)(2,1)} %shard_map.129), channel_id=1, source_target_pairs={{0,4},{4,0},{1,5},{5,1},{2,6},{6,2},{3,7},{7,3}} | collective-permute-start | bytes 4718600 | tf_op jit(solution)/shard_map/ppermute | solution.py:267
  1777.0 117.4 %collective-permute-start.45 = (bf16[3072,512]{1,0:T(8,128)(2,1)}, bf16[3072,512]{1,0:T(8,128)(2,1)}, u32[]{:S(2)}, u32[]{:S(2)}) collective-permute-start(bf16[3072,512]{1,0:T(8,128)(2,1)} %shard_map.123), channel_id=1, source_target_pairs={{0,4},{4,0},{1,5},{5,1},{2,6},{6,2},{3,7},{7,3}} | collective-permute-start | bytes 9437192 | tf_op jit(solution)/shard_map/ppermute | solution.py:267
  1797.8 164.1 %collective-permute-start.50 = (bf16[3072,512]{1,0:T(8,128)(2,1)}, bf16[3072,512]{1,0:T(8,128)(2,1)}, u32[]{:S(2)}, u32[]{:S(2)}) collective-permute-start(bf16[3072,512]{1,0:T(8,128)(2,1)} %shard_map.126), channel_id=1, source_target_pairs={{0,4},{4,0},{1,5},{5,1},{2,6},{6,2},{3,7},{7,3}} | collective-permute-start | bytes 9437192 | tf_op jit(solution)/shard_map/ppermute | solution.py:267
  1856.1 173.1 %collective-permute-start.34 = (bf16[3072,512]{1,0:T(8,128)(2,1)}, bf16[3072,512]{1,0:T(8,128)(2,1)}, u32[]{:S(2)}, u32[]{:S(2)}) collective-permute-start(bf16[3072,512]{1,0:T(8,128)(2,1)} %shard_map.115), channel_id=1, source_target_pairs={{0,4},{4,0},{1,5},{5,1},{2,6},{6,2},{3,7},{7,3}} | collective-permute-start | bytes 9437192 | tf_op jit(solution)/shard_map/ppermute | solution.py:267
  1857.6 239.0 %collective-permute-start.35 = (bf16[3072,512]{1,0:T(8,128)(2,1)S(1)}, bf16[3072,512]{1,0:T(8,128)(2,1)}, u32[]{:S(2)}, u32[]{:S(2)}) collective-permute-start(bf16[3072,512]{1,0:T(8,128)(2,1)S(1)} %copy-done.8), channel_id=1, source_target_pairs={{0,4},{4,0},{1,5},{5,1},{2,6},{6,2},{3,7},{7,3}} | collective-permute-start | bytes 9437192 | tf_op jit(solution)/shard_map/ppermute | solution.py:267
  1894.4 268.9 %collective-permute-start.36 = (bf16[3072,512]{1,0:T(8,128)(2,1)}, bf16[3072,512]{1,0:T(8,128)(2,1)}, u32[]{:S(2)}, u32[]{:S(2)}) collective-permute-start(bf16[3072,512]{1,0:T(8,128)(2,1)} %shard_map.117), channel_id=1, source_target_pairs={{0,4},{4,0},{1,5},{5,1},{2,6},{6,2},{3,7},{7,3}} | collective-permute-start | bytes 9437192 | tf_op jit(solution)/shard_map/ppermute | solution.py:267
  1961.8 276.5 %collective-permute-start.41 = (bf16[3072,256]{1,0:T(8,128)(2,1)}, bf16[3072,256]{1,0:T(8,128)(2,1)}, u32[]{:S(2)}, u32[]{:S(2)}) collective-permute-start(bf16[3072,256]{1,0:T(8,128)(2,1)} %shard_map.121), channel_id=1, source_target_pairs={{0,2},{1,3},{2,0},{3,1},{4,6},{5,7},{6,4},{7,5}} | collective-permute-start | bytes 4718600 | tf_op jit(solution)/shard_map/ppermute | solution.py:264
  1983.3 234.2 %collective-permute-start.56 = (bf16[3072,256]{1,0:T(8,128)(2,1)}, bf16[3072,256]{1,0:T(8,128)(2,1)}, u32[]{:S(2)}, u32[]{:S(2)}) collective-permute-start(bf16[3072,256]{1,0:T(8,128)(2,1)} %shard_map.130), channel_id=1, source_target_pairs={{0,2},{1,3},{2,0},{3,1},{4,6},{5,7},{6,4},{7,5}} | collective-permute-start | bytes 4718600 | tf_op jit(solution)/shard_map/ppermute | solution.py:264
  2029.2 188.3 %collective-permute-start.46 = (bf16[3072,512]{1,0:T(8,128)(2,1)}, bf16[3072,512]{1,0:T(8,128)(2,1)}, u32[]{:S(2)}, u32[]{:S(2)}) collective-permute-start(bf16[3072,512]{1,0:T(8,128)(2,1)} %shard_map.124), channel_id=1, source_target_pairs={{0,2},{1,3},{2,0},{3,1},{4,6},{5,7},{6,4},{7,5}} | collective-permute-start | bytes 9437192 | tf_op jit(solution)/shard_map/ppermute | solution.py:264
  2096.6 120.9 %collective-permute-start.51 = (bf16[3072,512]{1,0:T(8,128)(2,1)}, bf16[3072,512]{1,0:T(8,128)(2,1)S(1)}, u32[]{:S(2)}, u32[]{:S(2)}) collective-permute-start(bf16[3072,512]{1,0:T(8,128)(2,1)} %shard_map.127), channel_id=1, source_target_pairs={{0,2},{1,3},{2,0},{3,1},{4,6},{5,7},{6,4},{7,5}} | collective-permute-start | bytes 9437192 | tf_op jit(solution)/shard_map/ppermute | solution.py:264
  (12 other events, 119.1 us)

commit v3 on v2

--- a/solution.py
+++ b/solution.py
@@ -9,6 +9,7 @@
 
 NORM_EPS = 1e-6
 VMEM_LIMIT = 60 * 1024 * 1024
+SMALL_LIMIT = 16 * 1024 * 1024
 UP_PIECES = 4
 OUT_PIECES = (512, 512, 256, 256)
 Y_PIECES = 3
@@ -201,7 +202,7 @@
         grid=(rows // bm,),
         in_specs=[row_block(cols)] + [row_block(p.shape[1]) for p in parts],
         out_specs=row_block(cols),
-        compiler_params=pltpu.CompilerParams(vmem_limit_bytes=VMEM_LIMIT),
+        compiler_params=pltpu.CompilerParams(vmem_limit_bytes=SMALL_LIMIT),
         cost_estimate=pl.CostEstimate(flops=2 * rows * cols, bytes_accessed=8 * rows * cols, transcendentals=0),
     )(main, *parts)
 
@@ -219,7 +220,7 @@
         in_specs=[tail_block, pl.BlockSpec((bm, size), lambda i: (i, 0)), pl.BlockSpec(memory_space=pl.ANY)],
         out_specs=tail_block,
         input_output_aliases={2: 0},
-        compiler_params=pltpu.CompilerParams(vmem_limit_bytes=VMEM_LIMIT),
+        compiler_params=pltpu.CompilerParams(vmem_limit_bytes=SMALL_LIMIT),
         cost_estimate=pl.CostEstimate(flops=2 * rows * size, bytes_accessed=8 * rows * size, transcendentals=0),
     )(main, part, held)
 

time: 2250 us -> 2250 us (level)
  no operation moved by 1% of the time
where the time goes in v3:
time: 2250 us; the launch traced here: 2240 us
  Pallas kernels  1190 us (53%)
  waiting for transfers between devices  881 us (39%)
  local copies, waits for them, and re-layouts  85.9 us (4%)
  starting transfers between devices  50.7 us (2%)
  other arithmetic  30 us (1%)
    pallas_call x10, Pallas kernels, project_in(): pl.pallas_call(functools.partial(block_matmul, n_blocks, bias is not None...  574 us
    ppermute x48, waiting for transfers between devices, partner(): return lax.ppermute(arr, 'col', [(i, i ^ shift) for i in range(col_size)])  537 us
    pallas_call x18, Pallas kernels, project_out(): pl.pallas_call(functools.partial(out_matmul, len(hidden), len(adds), len(...  462 us
    ppermute x9, waiting for transfers between devices, over_row(): return lax.ppermute(arr, 'row', [(i, i ^ 1) for i in range(row_size)])  344 us
    pallas_call x2, Pallas kernels, normalise(): pl.pallas_call(functools.partial(normalise_tile, n_blocks), out_shape=[ja...  93.8 us
    pallas_call x1, Pallas kernels, attention(): pl.pallas_call(functools.partial(attend, head_dim), out_shape=jax.ShapeDt...  45.7 us
  transfers between devices with their start and end apart: 57, of which 18 were waited for; matrix products, arithmetic and copies ran while one was open for 5% of the time, Pallas kernels for 53%

profile of v3, /device:TPU:0, one launch (start us, length us, event | category | flops | bytes accessed | tf_op | source)
XLA Modules:
  0.0 2242.4 jit_solution(16143733809125799914)
XLA Ops:
  0.0 3.3 collective-permute-start.2
  4.8 201.7 %collective-permute-done.2.refs_2_ = bf16[3072,1536]{1,0:T(8,128)(2,1)} collective-permute-done((bf16[3072,1536]{1,0:T(8,128)(2,1)}, bf16[3072,1536]{1,0:T(8,128)(2,1)}, u32[]{:S(2)}, u32[]{:S(2)}) %collective-permute-start.2) | collective-permute-done | bytes 9437216 | tf_op jit(solution)/shard_map/ppermute | solution.py:265
  208.8 2.2 constant_dynamic-slice_fusion.37
  213.1 5.7 constant_dynamic-slice_fusion.36
  218.8 5.4 constant_dynamic-slice_fusion.40
  224.2 2.2 pad_maximum_fusion.2
  230.3 2.3 pad_maximum_fusion.4
  232.5 2.1 pad_maximum_fusion.5
  234.7 19.2 constant_dynamic-slice_fusion.24
  253.9 11.6 constant_dynamic-slice_fusion.4
  265.4 5.3 pad_maximum_fusion.1
  270.8 25.4 %constant_dynamic-slice_fusion.8 = (bf16[1536,768]{1,0:T(8,128)(2,1)}, bf16[1536,768]{1,0:T(8,128)(2,1)}, bf16[1536,768]{1,0:T(8,128)(2,1)}, bf16[1536,768]{1,0:...) fusion(bf16[1536,12288]{1,0:T(8,128)(2,1)} %param.16, ...), kind=kLoop, calls=%fused_computation.18 | loop fusion | bytes 75497536 | tf_op jit(solution)/shard_map/dynamic_slice | solution.py:277
  296.7 114.2 %collective-permute-done.3.refs_2_ = bf16[3072,1536]{1,0:T(8,128)(2,1)} collective-permute-done((bf16[3072,1536]{1,0:T(8,128)(2,1)}, bf16[3072,1536]{1,0:T(8,128)(2,1)}, u32[]{:S(2)}, u32[]{:S(2)}) %collective-permute-start.3) | collective-permute-done | bytes 9437216 | tf_op jit(solution)/shard_map/ppermute | solution.py:268
  411.0 2.5 pad_maximum_fusion.6
  427.3 9.3 pad_maximum_fusion.refs_5_
  438.4 46.9 %shard_map.100 = (bf16[6144,1536]{1,0:T(8,128)(2,1)}, bf16[6144,1536]{1,0:T(8,128)(2,1)}, bf16[6144,1536]{1,0:T(8,128)(2,1)}, bf16[6144,1536]{1,0:T(8,128)(2,1)}) custom-call(bf16[3072,1536]{1,0:T(8,128)(2,1)} %bitcast.9, bf16[3072,1536]{1,0:T(8,128)(2,1)} %collective-permute-done.8.refs_1_, bf16[3072,1536]{1,0:T(8,128)(2,1)} %collective-permute-done.2.refs_2_, ...), custom_call_target="tpu_custom_call" | custom-call | flops 11324620800 | bytes 75497472 | tf_op jit(solution)/shard_map/pallas_call | solution.py:55
  486.7 42.4 %collective-permute-done.15.refs_7_ = bf16[1536,768]{1,0:T(8,128)(2,1)} collective-permute-done((bf16[1536,768]{1,0:T(8,128)(2,1)}, bf16[1536,768]{1,0:T(8,128)(2,1)}, u32[]{:S(2)}, u32[]{:S(2)}) %collective-permute-start.15) | collective-permute-done | bytes 2359328 | tf_op jit(solution)/shard_map/ppermute | solution.py:265
  530.9 41.4 %shard_map.104.refs_8_ = bf16[6144,768]{1,0:T(8,128)(2,1)} custom-call(bf16[6144,1536]{1,0:T(8,128)(2,1)} %get-tuple-element.13.refs_8_.refs_0_, bf16[6144,1536]{1,0:T(8,128)(2,1)} %get-tuple-element.14.refs_9_.refs_1_, bf16[6144,1536]{1,0:T(8,128)(2,1)} %get-tuple-element.15.refs_10_.refs_2_, bf16[6144,1536]{1,0:T(8,128)(2,1)} %get-tuple-element.16.refs_11_.refs_3_, ...), custom_call_target="tpu_custom_call" | custom-call | flops 28991029248 | bytes 169869312 | tf_op jit(solution)/shard_map/pallas_call | solution.py:111
  572.4 9.1 collective-permute-done.11.refs_6_
  582.1 48.1 %collective-permute-done.12.refs_7_ = bf16[1536,768]{1,0:T(8,128)(2,1)} collective-permute-done((bf16[1536,768]{1,0:T(8,128)(2,1)S(1)}, bf16[1536,768]{1,0:T(8,128)(2,1)}, u32[]{:S(2)}, u32[]{:S(2)}) %collective-permute-start.12) | collective-permute-done | bytes 2359328 | tf_op jit(solution)/shard_map/ppermute | solution.py:265
  632.0 41.4 %shard_map.102.refs_8_ = bf16[6144,768]{1,0:T(8,128)(2,1)} custom-call(bf16[6144,1536]{1,0:T(8,128)(2,1)} %get-tuple-element.13.refs_8_.refs_0_, bf16[6144,1536]{1,0:T(8,128)(2,1)} %get-tuple-element.14.refs_9_.refs_1_, bf16[6144,1536]{1,0:T(8,128)(2,1)} %get-tuple-element.15.refs_10_.refs_2_, bf16[6144,1536]{1,0:T(8,128)(2,1)} %get-tuple-element.16.refs_11_.refs_3_, ...), custom_call_target="tpu_custom_call" | custom-call | flops 28991029248 | bytes 169869312 | tf_op jit(solution)/shard_map/pallas_call | solution.py:111
  675.0 46.9 %shard_map.101 = (bf16[6144,1536]{1,0:T(8,128)(2,1)}, bf16[6144,1536]{1,0:T(8,128)(2,1)}, bf16[6144,1536]{1,0:T(8,128)(2,1)}, bf16[6144,1536]{1,0:T(8,128)(2,1)}) custom-call(bf16[3072,1536]{1,0:T(8,128)(2,1)} %collective-permute-done.refs_0_, ...), custom_call_target="tpu_custom_call", output_to_operand_aliasing={{0}: (8, {}), {1}: (9, {}), {2}: (10, {}), {3}: (11, {})} | custom-call | flops 11324620800 | bytes 75497472 | tf_op jit(solution)/shard_map/pallas_call | solution.py:55
  722.7 8.6 collective-permute-done.18.refs_7_
  732.7 77.3 %shard_map.106.refs_2_ = bf16[6144,768]{1,0:T(8,128)(2,1)} custom-call(bf16[6144,1536]{1,0:T(8,128)(2,1)} %get-tuple-element.17.refs_0_, bf16[6144,1536]{1,0:T(8,128)(2,1)} %get-tuple-element.18.refs_1_, bf16[6144,1536]{1,0:T(8,128)(2,1)} %get-tuple-element.19.refs_2_, bf16[6144,1536]{1,0:T(8,128)(2,1)} %get-tuple-element.20.refs_3_, ...), custom_call_target="tpu_custom_call" | custom-call | flops 57982058496 | bytes 169869312 | tf_op jit(solution)/shard_map/pallas_call | solution.py:111
  811.6 20.8 collective-permute-done.21.refs_7_
  834.1 81.3 %shard_map.108.refs_1_ = bf16[6144,768]{1,0:T(8,128)(2,1)} custom-call(bf16[6144,1536]{1,0:T(8,128)(2,1)} %get-tuple-element.17.refs_0_, bf16[6144,1536]{1,0:T(8,128)(2,1)} %get-tuple-element.18.refs_1_, bf16[6144,1536]{1,0:T(8,128)(2,1)} %get-tuple-element.19.refs_2_, bf16[6144,1536]{1,0:T(8,128)(2,1)} %get-tuple-element.20.refs_3_, ...), custom_call_target="tpu_custom_call" | custom-call | flops 57982058496 | bytes 169869312 | tf_op jit(solution)/shard_map/pallas_call | solution.py:111
  915.4 41.6 %shard_map.103.refs_0_ = bf16[6144,768]{1,0:T(8,128)(2,1)} custom-call(bf16[6144,1536]{1,0:T(8,128)(2,1)} %get-tuple-element.17.refs_0_, bf16[6144,1536]{1,0:T(8,128)(2,1)} %get-tuple-element.18.refs_1_, bf16[6144,1536]{1,0:T(8,128)(2,1)} %get-tuple-element.19.refs_2_, bf16[6144,1536]{1,0:T(8,128)(2,1)} %get-tuple-element.20.refs_3_, ...), custom_call_target="tpu_custom_call", output_to_operand_aliasing={{}: (8, {})} | custom-call | flops 28991029248 | bytes 169869312 | tf_op jit(solution)/shard_map/pallas_call | solution.py:111
  959.2 81.3 %shard_map.109.refs_2_ = bf16[6144,768]{1,0:T(8,128)(2,1)} custom-call(bf16[6144,1536]{1,0:T(8,128)(2,1)} %get-tuple-element.17.refs_0_, bf16[6144,1536]{1,0:T(8,128)(2,1)} %get-tuple-element.18.refs_1_, bf16[6144,1536]{1,0:T(8,128)(2,1)} %get-tuple-element.19.refs_2_, bf16[6144,1536]{1,0:T(8,128)(2,1)} %get-tuple-element.20.refs_3_, ...), custom_call_target="tpu_custom_call" | custom-call | flops 57982058496 | bytes 169869312 | tf_op jit(solution)/shard_map/pallas_call | solution.py:111
  1040.4 41.5 %shard_map.105.refs_1_ = bf16[6144,768]{1,0:T(8,128)(2,1)} custom-call(bf16[6144,1536]{1,0:T(8,128)(2,1)} %get-tuple-element.17.refs_0_, bf16[6144,1536]{1,0:T(8,128)(2,1)} %get-tuple-element.18.refs_1_, bf16[6144,1536]{1,0:T(8,128)(2,1)} %get-tuple-element.19.refs_2_, bf16[6144,1536]{1,0:T(8,128)(2,1)} %get-tuple-element.20.refs_3_, ...), custom_call_target="tpu_custom_call", output_to_operand_aliasing={{}: (8, {})} | custom-call | flops 28991029248 | bytes 169869312 | tf_op jit(solution)/shard_map/pallas_call | solution.py:111
  1081.9 45.7 %shard_map.107.refs_0_ = bf16[6144,768]{1,0:T(8,128)(2,1)} custom-call(f32[1,128]{1,0:T(1,128)} %bitcast.11, f32[1,128]{1,0:T(1,128)} %bitcast.12, bf16[6144,768]{1,0:T(8,128)(2,1)} %shard_map.103.refs_0_, bf16[6144,768]{1,0:T(8,128)(2,1)} %shard_map.105.refs_1_, bf16[6144,768]{1,0:T(8,128)(2,1)} %shard_map.106.refs_2_), custom_call_target="tpu_custom_call" | custom-call | flops 38654705664 | bytes 28311552 | tf_op jit(solution)/shard_map/pallas_call | solution.py:249
  1129.7 43.6 %shard_map.111.refs_9_.refs_4_ = bf16[6144,768]{1,0:T(8,128)(2,1)} custom-call(bf16[6144,1536]{1,0:T(8,128)(2,1)} %get-tuple-element.17.refs_0_, bf16[6144,1536]{1,0:T(8,128)(2,1)} %get-tuple-element.18.refs_1_, bf16[6144,1536]{1,0:T(8,128)(2,1)} %get-tuple-element.19.refs_2_, bf16[6144,1536]{1,0:T(8,128)(2,1)} %get-tuple-element.20.refs_3_, ...), custom_call_target="tpu_custom_call" | custom-call | flops 28991029248 | bytes 169869312 | tf_op jit(solution)/shard_map/pallas_call | solution.py:111
  1174.8 7.3 collective-permute-done.26.refs_6_
  1182.6 48.4 %collective-permute-done.27.refs_7_ = bf16[1536,768]{1,0:T(8,128)(2,1)} collective-permute-done((bf16[1536,768]{1,0:T(8,128)(2,1)}, bf16[1536,768]{1,0:T(8,128)(2,1)}, u32[]{:S(2)}, u32[]{:S(2)}) %collective-permute-start.27) | collective-permute-done | bytes 2359328 | tf_op jit(solution)/shard_map/ppermute | solution.py:265
  1232.6 81.3 %shard_map.110.refs_3_ = bf16[6144,768]{1,0:T(8,128)(2,1)} custom-call(bf16[6144,1536]{1,0:T(8,128)(2,1)} %get-tuple-element.17.refs_0_, bf16[6144,1536]{1,0:T(8,128)(2,1)} %get-tuple-element.18.refs_1_, bf16[6144,1536]{1,0:T(8,128)(2,1)} %get-tuple-element.19.refs_2_, bf16[6144,1536]{1,0:T(8,128)(2,1)} %get-tuple-element.20.refs_3_, ...), custom_call_target="tpu_custom_call" | custom-call | flops 57982058496 | bytes 169869312 | tf_op jit(solution)/shard_map/pallas_call | solution.py:111
  1314.1 50.0 %shard_map.114 = bf16[3072,1536]{1,0:T(8,128)(2,1)} custom-call(bf16[6144,768]{1,0:T(8,128)(2,1)} %shard_map.107.refs_0_, bf16[6144,768]{1,0:T(8,128)(2,1)} %shard_map.108.refs_1_, bf16[6144,768]{1,0:T(8,128)(2,1)} %shard_map.109.refs_2_, bf16[6144,768]{1,0:T(8,128)(2,1)} %shard_map.110.refs_3_, bf16[6144,768]{1,0:T(8,128)(2,1)} %shard_map.111.refs_9_.refs_4_, ...), custom_call_target="tpu_custom_call" | custom-call | flops 36238786560 | bytes 35389440 | tf_op jit(solution)/shard_map/pallas_call | solution.py:172
  1364.1 43.5 %shard_map.112.refs_4_ = bf16[6144,768]{1,0:T(8,128)(2,1)} custom-call(bf16[6144,1536]{1,0:T(8,128)(2,1)} %get-tuple-element.17.refs_0_, bf16[6144,1536]{1,0:T(8,128)(2,1)} %get-tuple-element.18.refs_1_, bf16[6144,1536]{1,0:T(8,128)(2,1)} %get-tuple-element.19.refs_2_, bf16[6144,1536]{1,0:T(8,128)(2,1)} %get-tuple-element.20.refs_3_, ...), custom_call_target="tpu_custom_call", output_to_operand_aliasing={{}: (9, {})} | custom-call | flops 28991029248 | bytes 169869312 | tf_op jit(solution)/shard_map/pallas_call | solution.py:111
  1407.6 76.2 %collective-permute-done.43.refs_5_ = bf16[3840,512]{1,0:T(8,128)(2,1)} collective-permute-done((bf16[3840,512]{1,0:T(8,128)(2,1)S(1)}, bf16[3840,512]{1,0:T(8,128)(2,1)}, u32[]{:S(2)}, u32[]{:S(2)}) %collective-permute-start.43) | collective-permute-done | bytes 3932192 | tf_op jit(solution)/shard_map/ppermute | solution.py:265
  1484.8 33.4 %shard_map.122 = bf16[6144,512]{1,0:T(8,128)(2,1)} custom-call(bf16[6144,768]{1,0:T(8,128)(2,1)} %shard_map.107.refs_0_, bf16[6144,768]{1,0:T(8,128)(2,1)} %shard_map.108.refs_1_, bf16[6144,768]{1,0:T(8,128)(2,1)} %shard_map.109.refs_2_, bf16[6144,768]{1,0:T(8,128)(2,1)} %shard_map.110.refs_3_, bf16[6144,768]{1,0:T(8,128)(2,1)} %shard_map.112.refs_4_, ...), custom_call_target="tpu_custom_call" | custom-call | flops 24159191040 | bytes 51118080 | tf_op jit(solution)/shard_map/pallas_call | solution.py:172
  1520.3 24.1 %shard_map.119 = bf16[6144,256]{1,0:T(8,128)(2,1)} custom-call(bf16[6144,768]{1,0:T(8,128)(2,1)} %shard_map.107.refs_0_, bf16[6144,768]{1,0:T(8,128)(2,1)} %shard_map.108.refs_1_, bf16[6144,768]{1,0:T(8,128)(2,1)} %shard_map.109.refs_2_, bf16[6144,768]{1,0:T(8,128)(2,1)} %shard_map.110.refs_3_, bf16[6144,768]{1,0:T(8,128)(2,1)} %shard_map.112.refs_4_, ...), custom_call_target="tpu_custom_call" | custom-call | flops 12079595520 | bytes 49152000 | tf_op jit(solution)/shard_map/pallas_call | solution.py:172
  1544.4 67.3 %collective-permute-done.52.refs_5_ = bf16[3840,256]{1,0:T(8,128)(2,1)S(1)} collective-permute-done((bf16[3840,256]{1,0:T(8,128)(2,1)}, bf16[3840,256]{1,0:T(8,128)(2,1)S(1)}, u32[]{:S(2)}, u32[]{:S(2)}) %collective-permute-start.52) | collective-permute-done | bytes 1966112 | tf_op jit(solution)/shard_map/ppermute | solution.py:265
  1612.2 33.6 %shard_map.125 = bf16[6144,512]{1,0:T(8,128)(2,1)} custom-call(bf16[6144,768]{1,0:T(8,128)(2,1)} %shard_map.107.refs_0_, bf16[6144,768]{1,0:T(8,128)(2,1)} %shard_map.108.refs_1_, bf16[6144,768]{1,0:T(8,128)(2,1)} %shard_map.109.refs_2_, bf16[6144,768]{1,0:T(8,128)(2,1)} %shard_map.110.refs_3_, bf16[6144,768]{1,0:T(8,128)(2,1)} %shard_map.112.refs_4_, ...), custom_call_target="tpu_custom_call" | custom-call | flops 24159191040 | bytes 51118080 | tf_op jit(solution)/shard_map/pallas_call | solution.py:172
  1645.8 6.6 collective-permute-done.53.refs_5_
  1653.0 24.1 %shard_map.128 = bf16[6144,256]{1,0:T(8,128)(2,1)} custom-call(bf16[6144,768]{1,0:T(8,128)(2,1)} %shard_map.107.refs_0_, bf16[6144,768]{1,0:T(8,128)(2,1)} %shard_map.108.refs_1_, bf16[6144,768]{1,0:T(8,128)(2,1)} %shard_map.109.refs_2_, bf16[6144,768]{1,0:T(8,128)(2,1)} %shard_map.110.refs_3_, bf16[6144,768]{1,0:T(8,128)(2,1)} %shard_map.112.refs_4_, ...), custom_call_target="tpu_custom_call" | custom-call | flops 12079595520 | bytes 49152000 | tf_op jit(solution)/shard_map/pallas_call | solution.py:172
  1677.6 50.0 %shard_map.113 = bf16[3072,1536]{1,0:T(8,128)(2,1)} custom-call(bf16[6144,768]{1,0:T(8,128)(2,1)} %shard_map.107.refs_0_, bf16[6144,768]{1,0:T(8,128)(2,1)} %shard_map.108.refs_1_, bf16[6144,768]{1,0:T(8,128)(2,1)} %shard_map.109.refs_2_, bf16[6144,768]{1,0:T(8,128)(2,1)} %shard_map.110.refs_3_, bf16[6144,768]{1,0:T(8,128)(2,1)} %shard_map.112.refs_4_, ...), custom_call_target="tpu_custom_call" | custom-call | flops 36238786560 | bytes 35389440 | tf_op jit(solution)/shard_map/pallas_call | solution.py:172
  1727.6 13.7 shard_map.120
  1741.9 13.8 shard_map.129
  1757.2 19.2 shard_map.123
  1778.5 19.3 shard_map.126
  1798.3 19.3 shard_map.115
  1817.6 19.2 shard_map.116
  1836.8 19.3 shard_map.117
  1858.2 36.2 %collective-permute-done.45.refs_7_ = bf16[3072,512]{1,0:T(8,128)(2,1)} collective-permute-done((bf16[3072,512]{1,0:T(8,128)(2,1)}, bf16[3072,512]{1,0:T(8,128)(2,1)}, u32[]{:S(2)}, u32[]{:S(2)}) %collective-permute-start.45) | collective-permute-done | bytes 3145760 | tf_op jit(solution)/shard_map/ppermute | solution.py:268
  1895.9 14.3 shard_map.121
  1910.2 14.4 shard_map.130
  1924.6 20.1 shard_map.124
  1944.6 17.2 collective-permute-done.50.refs_7_
  1963.3 20.1 shard_map.127
  1983.9 45.3 %collective-permute-done.34.refs_7_ = bf16[3072,512]{1,0:T(8,128)(2,1)} collective-permute-done((bf16[3072,512]{1,0:T(8,128)(2,1)S(1)}, bf16[3072,512]{1,0:T(8,128)(2,1)}, u32[]{:S(2)}, u32[]{:S(2)}) %collective-permute-start.34) | collective-permute-done | bytes 3145760 | tf_op jit(solution)/shard_map/ppermute | solution.py:268
  2030.7 65.9 %collective-permute-done.35.refs_8_ = bf16[3072,512]{1,0:T(8,128)(2,1)} collective-permute-done((bf16[3072,512]{1,0:T(8,128)(2,1)}, bf16[3072,512]{1,0:T(8,128)(2,1)}, u32[]{:S(2)}, u32[]{:S(2)}) %collective-permute-start.35) | collective-permute-done | bytes 3145760 | tf_op jit(solution)/shard_map/ppermute | solution.py:268
  2098.1 65.2 %collective-permute-done.36.refs_9_ = bf16[3072,512]{1,0:T(8,128)(2,1)} collective-permute-done((bf16[3072,512]{1,0:T(8,128)(2,1)}, bf16[3072,512]{1,0:T(8,128)(2,1)}, u32[]{:S(2)}, u32[]{:S(2)}) %collective-permute-start.36) | collective-permute-done | bytes 3145760 | tf_op jit(solution)/shard_map/ppermute | solution.py:268
  2163.3 54.2 %shard_map.118.main_ref = f32[3072,1536]{1,0:T(8,128)} custom-call(bf16[6144,768]{1,0:T(8,128)(2,1)} %shard_map.107.refs_0_, bf16[6144,768]{1,0:T(8,128)(2,1)} %shard_map.108.refs_1_, bf16[6144,768]{1,0:T(8,128)(2,1)} %shard_map.109.refs_2_, bf16[6144,768]{1,0:T(8,128)(2,1)} %shard_map.110.refs_3_, bf16[6144,768]{1,0:T(8,128)(2,1)} %shard_map.112.refs_4_, ...), custom_call_target="tpu_custom_call" | custom-call | flops 36238786560 | bytes 35389440 | tf_op jit(solution)/shard_map/pallas_call | solution.py:172
  2217.6 6.4 copy-done
  2223.9 15.0 shard_map.131.held_ref
  2238.9 3.5 shard_map.132
  (150 shorter events, 64.6 us)
Async XLA Ops:
  0.0 206.5 %collective-permute-start.2 = (bf16[3072,1536]{1,0:T(8,128)(2,1)}, bf16[3072,1536]{1,0:T(8,128)(2,1)}, u32[]{:S(2)}, u32[]{:S(2)}) collective-permute-start(bf16[3072,1536]{1,0:T(8,128)(2,1)} %bitcast.6), channel_id=1, source_target_pairs={{0,2},{1,3},{2,0},{3,1},{4,6},{5,7},{6,4},{7,5}} | collective-permute-start | bytes 28311560 | tf_op jit(solution)/shard_map/ppermute | solution.py:265
  3.3 292.9 %collective-permute-start = (bf16[3072,1536]{1,0:T(8,128)(2,1)}, bf16[3072,1536]{1,0:T(8,128)(2,1)}, u32[]{:S(2)}, u32[]{:S(2)}) collective-permute-start(bf16[3072,1536]{1,0:T(8,128)(2,1)} %bitcast.7), channel_id=1, source_target_pairs={{0,4},{4,0},{1,5},{5,1},{2,6},{6,2},{3,7},{7,3}} | collective-permute-start | bytes 28311560 | tf_op jit(solution)/shard_map/ppermute | solution.py:268
  206.5 204.4 %collective-permute-start.3 = (bf16[3072,1536]{1,0:T(8,128)(2,1)}, bf16[3072,1536]{1,0:T(8,128)(2,1)}, u32[]{:S(2)}, u32[]{:S(2)}) collective-permute-start(bf16[3072,1536]{1,0:T(8,128)(2,1)} %collective-permute-done.2.refs_2_), channel_id=1, source_target_pairs={{0,4},{4,0},{1,5},{5,1},{2,6},{6,2},{3,7},{7,3}} | collective-permute-start | bytes 28311560 | tf_op jit(solution)/shard_map/ppermute | solution.py:268
  208.3 217.6 %collective-permute-start.8 = (bf16[3072,1536]{1,0:T(8,128)(2,1)}, bf16[3072,1536]{1,0:T(8,128)(2,1)}, u32[]{:S(2)}, u32[]{:S(2)}) collective-permute-start(bf16[3072,1536]{1,0:T(8,128)(2,1)} %bitcast.8), channel_id=1, source_target_pairs={{0,1},{1,0},{2,3},{3,2},{4,5},{5,4},{6,7},{7,6}} | collective-permute-start | bytes 28311560 | tf_op jit(solution)/shard_map/ppermute | solution.py:265
  208.3 208.0 %collective-permute-start.5 = (f32[1536]{0:T(1024)}, f32[1536]{0:T(1024)S(1)}, u32[]{:S(2)}, u32[]{:S(2)}) collective-permute-start(f32[1536]{0:T(1024)} %param.11), channel_id=1, source_target_pairs={{0,1},{1,0},{2,3},{3,2},{4,5},{5,4},{6,7},{7,6}} | collective-permute-start | bytes 18440 | tf_op jit(solution)/shard_map/ppermute | solution.py:265
  226.4 200.1 %collective-permute-start.9 = (bf16[3072,1536]{1,0:T(8,128)(2,1)}, bf16[3072,1536]{1,0:T(8,128)(2,1)}, u32[]{:S(2)}, u32[]{:S(2)}) collective-permute-start(bf16[3072,1536]{1,0:T(8,128)(2,1)} %collective-permute-done.2.refs_2_), channel_id=1, source_target_pairs={{0,1},{1,0},{2,3},{3,2},{4,5},{5,4},{6,7},{7,6}} | collective-permute-start | bytes 28311560 | tf_op jit(solution)/shard_map/ppermute | solution.py:265
  270.8 140.2 %copy-start.7 = (bf16[3072,256]{1,0:T(8,128)(2,1)S(1)}, bf16[3072,256]{1,0:T(8,128)(2,1)}, u32[]{:S(2)}) copy-start(bf16[3072,256]{1,0:T(8,128)(2,1)} %get-tuple-element.23) | copy-start | bytes 4718596
  296.2 117.3 %copy-start.6 = (bf16[3072,256]{1,0:T(8,128)(2,1)S(1)}, bf16[3072,256]{1,0:T(8,128)(2,1)}, u32[]{:S(2)}) copy-start(bf16[3072,256]{1,0:T(8,128)(2,1)} %get-tuple-element.22) | copy-start | bytes 4718596
  296.2 377.2 %collective-permute-start.1 = (bf16[3072,1536]{1,0:T(8,128)(2,1)}, bf16[3072,1536]{1,0:T(8,128)(2,1)}, u32[]{:S(2)}, u32[]{:S(2)}) collective-permute-start(bf16[3072,1536]{1,0:T(8,128)(2,1)} %collective-permute-done.refs_0_), channel_id=1, source_target_pairs={{0,1},{1,0},{2,3},{3,2},{4,5},{5,4},{6,7},{7,6}} | collective-permute-start | bytes 28311560 | tf_op jit(solution)/shard_map/ppermute | solution.py:265
  411.0 262.5 %collective-permute-start.4 = (bf16[3072,1536]{1,0:T(8,128)(2,1)}, bf16[3072,1536]{1,0:T(8,128)(2,1)}, u32[]{:S(2)}, u32[]{:S(2)}) collective-permute-start(bf16[3072,1536]{1,0:T(8,128)(2,1)} %collective-permute-done.3.refs_2_), channel_id=1, source_target_pairs={{0,1},{1,0},{2,3},{3,2},{4,5},{5,4},{6,7},{7,6}} | collective-permute-start | bytes 28311560 | tf_op jit(solution)/shard_map/ppermute | solution.py:265
  416.3 3.7 collective-permute-start.6
  419.9 4.8 collective-permute-start.7
  424.8 60.5 %collective-permute-start.13 = (bf16[1536,768]{1,0:T(8,128)(2,1)}, bf16[1536,768]{1,0:T(8,128)(2,1)}, u32[]{:S(2)}, u32[]{:S(2)}) collective-permute-start(bf16[1536,768]{1,0:T(8,128)(2,1)} %get-tuple-element.52), channel_id=1, source_target_pairs={{0,1},{1,0},{2,3},{3,2},{4,5},{5,4},{6,7},{7,6}} | collective-permute-start | bytes 7077896 | tf_op jit(solution)/shard_map/ppermute | solution.py:265
  425.9 60.2 %collective-permute-start.14 = (bf16[1536,768]{1,0:T(8,128)(2,1)}, bf16[1536,768]{1,0:T(8,128)(2,1)}, u32[]{:S(2)}, u32[]{:S(2)}) collective-permute-start(bf16[1536,768]{1,0:T(8,128)(2,1)} %get-tuple-element.51), channel_id=1, source_target_pairs={{0,2},{1,3},{2,0},{3,1},{4,6},{5,7},{6,4},{7,5}} | collective-permute-start | bytes 7077896 | tf_op jit(solution)/shard_map/ppermute | solution.py:265
  426.5 102.5 %collective-permute-start.15 = (bf16[1536,768]{1,0:T(8,128)(2,1)}, bf16[1536,768]{1,0:T(8,128)(2,1)}, u32[]{:S(2)}, u32[]{:S(2)}) collective-permute-start(bf16[1536,768]{1,0:T(8,128)(2,1)} %get-tuple-element.50), channel_id=1, source_target_pairs={{0,3},{1,2},{2,1},{3,0},{4,7},{5,6},{6,5},{7,4}} | collective-permute-start | bytes 7077896 | tf_op jit(solution)/shard_map/ppermute | solution.py:265
  438.4 90.7 %copy-start.12 = (bf16[1536,768]{1,0:T(8,128)(2,1)S(1)}, bf16[1536,768]{1,0:T(8,128)(2,1)}, u32[]{:S(2)}) copy-start(bf16[1536,768]{1,0:T(8,128)(2,1)} %get-tuple-element.54) | copy-start | bytes 7077892
  485.3 87.0 %collective-permute-start.10 = (bf16[1536,768]{1,0:T(8,128)(2,1)}, bf16[1536,768]{1,0:T(8,128)(2,1)}, u32[]{:S(2)}, u32[]{:S(2)}) collective-permute-start(bf16[1536,768]{1,0:T(8,128)(2,1)} %get-tuple-element.56), channel_id=1, source_target_pairs={{0,1},{1,0},{2,3},{3,2},{4,5},{5,4},{6,7},{7,6}} | collective-permute-start | bytes 7077896 | tf_op jit(solution)/shard_map/ppermute | solution.py:265
  486.1 95.4 %collective-permute-start.11 = (bf16[1536,768]{1,0:T(8,128)(2,1)}, bf16[1536,768]{1,0:T(8,128)(2,1)}, u32[]{:S(2)}, u32[]{:S(2)}) collective-permute-start(bf16[1536,768]{1,0:T(8,128)(2,1)} %get-tuple-element.55), channel_id=1, source_target_pairs={{0,2},{1,3},{2,0},{3,1},{4,6},{5,7},{6,4},{7,5}} | collective-permute-start | bytes 7077896 | tf_op jit(solution)/shard_map/ppermute | solution.py:265
  529.0 101.1 %collective-permute-start.12 = (bf16[1536,768]{1,0:T(8,128)(2,1)S(1)}, bf16[1536,768]{1,0:T(8,128)(2,1)}, u32[]{:S(2)}, u32[]{:S(2)}) collective-permute-start(bf16[1536,768]{1,0:T(8,128)(2,1)S(1)} %copy-done.12), channel_id=1, source_target_pairs={{0,3},{1,2},{2,1},{3,0},{4,7},{5,6},{6,5},{7,4}} | collective-permute-start | bytes 7077896 | tf_op jit(solution)/shard_map/ppermute | solution.py:265
  572.4 149.6 %collective-permute-start.16 = (bf16[1536,768]{1,0:T(8,128)(2,1)}, bf16[1536,768]{1,0:T(8,128)(2,1)}, u32[]{:S(2)}, u32[]{:S(2)}) collective-permute-start(bf16[1536,768]{1,0:T(8,128)(2,1)} %get-tuple-element.48), channel_id=1, source_target_pairs={{0,1},{1,0},{2,3},{3,2},{4,5},{5,4},{6,7},{7,6}} | collective-permute-start | bytes 7077896 | tf_op jit(solution)/shard_map/ppermute | solution.py:265
  581.5 140.9 %collective-permute-start.17 = (bf16[1536,768]{1,0:T(8,128)(2,1)}, bf16[1536,768]{1,0:T(8,128)(2,1)}, u32[]{:S(2)}, u32[]{:S(2)}) collective-permute-start(bf16[1536,768]{1,0:T(8,128)(2,1)} %get-tuple-element.58), channel_id=1, source_target_pairs={{0,2},{1,3},{2,0},{3,1},{4,6},{5,7},{6,4},{7,5}} | collective-permute-start | bytes 7077896 | tf_op jit(solution)/shard_map/ppermute | solution.py:265
  630.2 101.1 %collective-permute-start.18 = (bf16[1536,768]{1,0:T(8,128)(2,1)}, bf16[1536,768]{1,0:T(8,128)(2,1)}, u32[]{:S(2)}, u32[]{:S(2)}) collective-permute-start(bf16[1536,768]{1,0:T(8,128)(2,1)} %get-tuple-element.47), channel_id=1, source_target_pairs={{0,3},{1,2},{2,1},{3,0},{4,7},{5,6},{6,5},{7,4}} | collective-permute-start | bytes 7077896 | tf_op jit(solution)/shard_map/ppermute | solution.py:265
  673.5 136.5 %collective-permute-start.19 = (bf16[1536,768]{1,0:T(8,128)(2,1)}, bf16[1536,768]{1,0:T(8,128)(2,1)}, u32[]{:S(2)}, u32[]{:S(2)}) collective-permute-start(bf16[1536,768]{1,0:T(8,128)(2,1)} %get-tuple-element.44), channel_id=1, source_target_pairs={{0,1},{1,0},{2,3},{3,2},{4,5},{5,4},{6,7},{7,6}} | collective-permute-start | bytes 7077896 | tf_op jit(solution)/shard_map/ppermute | solution.py:265
  673.5 48.4 %copy-start.11 = (bf16[1536,768]{1,0:T(8,128)(2,1)S(1)}, bf16[1536,768]{1,0:T(8,128)(2,1)}, u32[]{:S(2)}) copy-start(bf16[1536,768]{1,0:T(8,128)(2,1)} %get-tuple-element.42) | copy-start | bytes 7077892
  673.5 138.1 %collective-permute-start.20 = (bf16[1536,768]{1,0:T(8,128)(2,1)}, bf16[1536,768]{1,0:T(8,128)(2,1)}, u32[]{:S(2)}, u32[]{:S(2)}) collective-permute-start(bf16[1536,768]{1,0:T(8,128)(2,1)} %get-tuple-element.43), channel_id=1, source_target_pairs={{0,2},{1,3},{2,0},{3,1},{4,6},{5,7},{6,4},{7,5}} | collective-permute-start | bytes 7077896 | tf_op jit(solution)/shard_map/ppermute | solution.py:265
  721.9 110.5 %collective-permute-start.21 = (bf16[1536,768]{1,0:T(8,128)(2,1)S(1)}, bf16[1536,768]{1,0:T(8,128)(2,1)}, u32[]{:S(2)}, u32[]{:S(2)}) collective-permute-start(bf16[1536,768]{1,0:T(8,128)(2,1)S(1)} %copy-done.11), channel_id=1, source_target_pairs={{0,3},{1,2},{2,1},{3,0},{4,7},{5,6},{6,5},{7,4}} | collective-permute-start | bytes 7077896 | tf_op jit(solution)/shard_map/ppermute | solution.py:265
  722.4 234.5 %collective-permute-start.22 = (bf16[1536,768]{1,0:T(8,128)(2,1)}, bf16[1536,768]{1,0:T(8,128)(2,1)}, u32[]{:S(2)}, u32[]{:S(2)}) collective-permute-start(bf16[1536,768]{1,0:T(8,128)(2,1)} %get-tuple-element.40), channel_id=1, source_target_pairs={{0,1},{1,0},{2,3},{3,2},{4,5},{5,4},{6,7},{7,6}} | collective-permute-start | bytes 7077896 | tf_op jit(solution)/shard_map/ppermute | solution.py:265
  731.3 226.3 %collective-permute-start.23 = (bf16[1536,768]{1,0:T(8,128)(2,1)}, bf16[1536,768]{1,0:T(8,128)(2,1)}, u32[]{:S(2)}, u32[]{:S(2)}) collective-permute-start(bf16[1536,768]{1,0:T(8,128)(2,1)} %get-tuple-element.39), channel_id=1, source_target_pairs={{0,2},{1,3},{2,0},{3,1},{4,6},{5,7},{6,4},{7,5}} | collective-permute-start | bytes 7077896 | tf_op jit(solution)/shard_map/ppermute | solution.py:265
  810.0 148.4 %collective-permute-start.24 = (bf16[1536,768]{1,0:T(8,128)(2,1)}, bf16[1536,768]{1,0:T(8,128)(2,1)}, u32[]{:S(2)}, u32[]{:S(2)}) collective-permute-start(bf16[1536,768]{1,0:T(8,128)(2,1)} %get-tuple-element.38), channel_id=1, source_target_pairs={{0,3},{1,2},{2,1},{3,0},{4,7},{5,6},{6,5},{7,4}} | collective-permute-start | bytes 7077896 | tf_op jit(solution)/shard_map/ppermute | solution.py:265
  811.6 361.7 %collective-permute-start.25 = (bf16[1536,768]{1,0:T(8,128)(2,1)}, bf16[1536,768]{1,0:T(8,128)(2,1)}, u32[]{:S(2)}, u32[]{:S(2)}) collective-permute-start(bf16[1536,768]{1,0:T(8,128)(2,1)} %get-tuple-element.36), channel_id=1, source_target_pairs={{0,1},{1,0},{2,3},{3,2},{4,5},{5,4},{6,7},{7,6}} | collective-permute-start | bytes 7077896 | tf_op jit(solution)/shard_map/ppermute | solution.py:265
  832.4 295.2 %collective-permute-start.28 = (bf16[1536,768]{1,0:T(8,128)(2,1)}, bf16[1536,768]{1,0:T(8,128)(2,1)}, u32[]{:S(2)}, u32[]{:S(2)}) collective-permute-start(bf16[1536,768]{1,0:T(8,128)(2,1)} %get-tuple-element.32), channel_id=1, source_target_pairs={{0,1},{1,0},{2,3},{3,2},{4,5},{5,4},{6,7},{7,6}} | collective-permute-start | bytes 7077896 | tf_op jit(solution)/shard_map/ppermute | solution.py:265
  915.4 42.2 %copy-start.10 = (bf16[1536,768]{1,0:T(8,128)(2,1)S(1)}, bf16[1536,768]{1,0:T(8,128)(2,1)}, u32[]{:S(2)}) copy-start(bf16[1536,768]{1,0:T(8,128)(2,1)} %get-tuple-element.31) | copy-start | bytes 7077892
  957.0 171.2 %collective-permute-start.29 = (bf16[1536,768]{1,0:T(8,128)(2,1)}, bf16[1536,768]{1,0:T(8,128)(2,1)}, u32[]{:S(2)}, u32[]{:S(2)}) collective-permute-start(bf16[1536,768]{1,0:T(8,128)(2,1)} %get-tuple-element.46), channel_id=1, source_target_pairs={{0,2},{1,3},{2,0},{3,1},{4,6},{5,7},{6,4},{7,5}} | collective-permute-start | bytes 7077896 | tf_op jit(solution)/shard_map/ppermute | solution.py:265
  957.6 171.6 %collective-permute-start.30 = (bf16[1536,768]{1,0:T(8,128)(2,1)S(1)}, bf16[1536,768]{1,0:T(8,128)(2,1)}, u32[]{:S(2)}, u32[]{:S(2)}) collective-permute-start(bf16[1536,768]{1,0:T(8,128)(2,1)S(1)} %copy-done.10), channel_id=1, source_target_pairs={{0,3},{1,2},{2,1},{3,0},{4,7},{5,6},{6,5},{7,4}} | collective-permute-start | bytes 7077896 | tf_op jit(solution)/shard_map/ppermute | solution.py:265
  958.4 355.5 %collective-permute-start.31 = (bf16[3840,1536]{1,0:T(8,128)(2,1)}, bf16[3840,1536]{1,0:T(8,128)(2,1)}, u32[]{:S(2)}, u32[]{:S(2)}) collective-permute-start(bf16[3840,1536]{1,0:T(8,128)(2,1)} %pad_maximum_fusion.1), channel_id=1, source_target_pairs={{0,1},{1,0},{2,3},{3,2},{4,5},{5,4},{6,7},{7,6}} | collective-permute-start | bytes 35389448 | tf_op jit(solution)/shard_map/ppermute | solution.py:265
  1127.6 54.4 %collective-permute-start.26 = (bf16[1536,768]{1,0:T(8,128)(2,1)}, bf16[1536,768]{1,0:T(8,128)(2,1)}, u32[]{:S(2)}, u32[]{:S(2)}) collective-permute-start(bf16[1536,768]{1,0:T(8,128)(2,1)} %get-tuple-element.35), channel_id=1, source_target_pairs={{0,2},{1,3},{2,0},{3,1},{4,6},{5,7},{6,4},{7,5}} | collective-permute-start | bytes 7077896 | tf_op jit(solution)/shard_map/ppermute | solution.py:265
  1128.2 102.9 %collective-permute-start.27 = (bf16[1536,768]{1,0:T(8,128)(2,1)}, bf16[1536,768]{1,0:T(8,128)(2,1)}, u32[]{:S(2)}, u32[]{:S(2)}) collective-permute-start(bf16[1536,768]{1,0:T(8,128)(2,1)} %get-tuple-element.34), channel_id=1, source_target_pairs={{0,3},{1,2},{2,1},{3,0},{4,7},{5,6},{6,5},{7,4}} | collective-permute-start | bytes 7077896 | tf_op jit(solution)/shard_map/ppermute | solution.py:265
  1129.2 415.2 %collective-permute-start.37 = (bf16[3840,256]{1,0:T(8,128)(2,1)}, bf16[3840,256]{1,0:T(8,128)(2,1)}, u32[]{:S(2)}, u32[]{:S(2)}) collective-permute-start(bf16[3840,256]{1,0:T(8,128)(2,1)} %pad_maximum_fusion.6), channel_id=1, source_target_pairs={{0,2},{1,3},{2,0},{3,1},{4,6},{5,7},{6,4},{7,5}} | collective-permute-start | bytes 5898248 | tf_op jit(solution)/shard_map/ppermute | solution.py:265
  1129.7 101.3 %copy-start.8 = (bf16[3840,512]{1,0:T(8,128)(2,1)S(1)}, bf16[3840,512]{1,0:T(8,128)(2,1)}, u32[]{:S(2)}) copy-start(bf16[3840,512]{1,0:T(8,128)(2,1)} %pad_maximum_fusion.3) | copy-start | bytes 11796484
  1173.4 344.9 %collective-permute-start.38 = (bf16[3840,256]{1,0:T(8,128)(2,1)}, bf16[3840,256]{1,0:T(8,128)(2,1)}, u32[]{:S(2)}, u32[]{:S(2)}) collective-permute-start(bf16[3840,256]{1,0:T(8,128)(2,1)} %pad_maximum_fusion.7), channel_id=1, source_target_pairs={{0,3},{1,2},{2,1},{3,0},{4,7},{5,6},{6,5},{7,4}} | collective-permute-start | bytes 5898248 | tf_op jit(solution)/shard_map/ppermute | solution.py:265
  1182.0 495.0 %collective-permute-start.42 = (bf16[3840,512]{1,0:T(8,128)(2,1)}, bf16[3840,512]{1,0:T(8,128)(2,1)}, u32[]{:S(2)}, u32[]{:S(2)}) collective-permute-start(bf16[3840,512]{1,0:T(8,128)(2,1)} %pad_maximum_fusion.2), channel_id=1, source_target_pairs={{0,2},{1,3},{2,0},{3,1},{4,6},{5,7},{6,4},{7,5}} | collective-permute-start | bytes 11796488 | tf_op jit(solution)/shard_map/ppermute | solution.py:265
  1231.0 252.8 %collective-permute-start.43 = (bf16[3840,512]{1,0:T(8,128)(2,1)S(1)}, bf16[3840,512]{1,0:T(8,128)(2,1)}, u32[]{:S(2)}, u32[]{:S(2)}) collective-permute-start(bf16[3840,512]{1,0:T(8,128)(2,1)S(1)} %copy-done.8), channel_id=1, source_target_pairs={{0,3},{1,2},{2,1},{3,0},{4,7},{5,6},{6,5},{7,4}} | collective-permute-start | bytes 11796488 | tf_op jit(solution)/shard_map/ppermute | solution.py:265
  1313.9 297.8 %collective-permute-start.48 = (bf16[3840,512]{1,0:T(8,128)(2,1)}, bf16[3840,512]{1,0:T(8,128)(2,1)}, u32[]{:S(2)}, u32[]{:S(2)}) collective-permute-start(bf16[3840,512]{1,0:T(8,128)(2,1)} %pad_maximum_fusion.5), channel_id=1, source_target_pairs={{0,3},{1,2},{2,1},{3,0},{4,7},{5,6},{6,5},{7,4}} | collective-permute-start | bytes 11796488 | tf_op jit(solution)/shard_map/ppermute | solution.py:265
  1483.8 34.4 %copy-start.13 = (bf16[3840,256]{1,0:T(8,128)(2,1)S(1)}, bf16[3840,256]{1,0:T(8,128)(2,1)}, u32[]{:S(2)}) copy-start(bf16[3840,256]{1,0:T(8,128)(2,1)} %pad_maximum_fusion.9) | copy-start | bytes 5898244
  1483.8 127.8 %collective-permute-start.52 = (bf16[3840,256]{1,0:T(8,128)(2,1)}, bf16[3840,256]{1,0:T(8,128)(2,1)S(1)}, u32[]{:S(2)}, u32[]{:S(2)}) collective-permute-start(bf16[3840,256]{1,0:T(8,128)(2,1)} %pad_maximum_fusion.8), channel_id=1, source_target_pairs={{0,2},{1,3},{2,0},{3,1},{4,6},{5,7},{6,4},{7,5}} | collective-permute-start | bytes 5898248 | tf_op jit(solution)/shard_map/ppermute | solution.py:265
  1518.3 134.1 %collective-permute-start.53 = (bf16[3840,256]{1,0:T(8,128)(2,1)S(1)}, bf16[3840,256]{1,0:T(8,128)(2,1)}, u32[]{:S(2)}, u32[]{:S(2)}) collective-permute-start(bf16[3840,256]{1,0:T(8,128)(2,1)S(1)} %copy-done.13), channel_id=1, source_target_pairs={{0,3},{1,2},{2,1},{3,0},{4,7},{5,6},{6,5},{7,4}} | collective-permute-start | bytes 5898248 | tf_op jit(solution)/shard_map/ppermute | solution.py:265
  1544.4 253.4 %collective-permute-start.33 = (bf16[3072,1536]{1,0:T(8,128)(2,1)}, bf16[3072,1536]{1,0:T(8,128)(2,1)}, u32[]{:S(2)}, u32[]{:S(2)}) collective-permute-start(bf16[3072,1536]{1,0:T(8,128)(2,1)} %shard_map.114), channel_id=1, source_target_pairs={{0,1},{1,0},{2,3},{3,2},{4,5},{5,4},{6,7},{7,6}} | collective-permute-start | bytes 28311560 | tf_op jit(solution)/shard_map/ppermute | solution.py:265
  1611.7 65.9 %collective-permute-start.39 = (bf16[6144,256]{1,0:T(8,128)(2,1)}, bf16[6144,256]{1,0:T(8,128)(2,1)}, u32[]{:S(2)}, u32[]{:S(2)}) collective-permute-start(bf16[6144,256]{1,0:T(8,128)(2,1)} %shard_map.119), channel_id=1, source_target_pairs={{0,1},{1,0},{2,3},{3,2},{4,5},{5,4},{6,7},{7,6}} | collective-permute-start | bytes 9437192 | tf_op jit(solution)/shard_map/ppermute | solution.py:265
  1611.7 144.0 %collective-permute-start.44 = (bf16[6144,512]{1,0:T(8,128)(2,1)}, bf16[6144,512]{1,0:T(8,128)(2,1)}, u32[]{:S(2)}, u32[]{:S(2)}) collective-permute-start(bf16[6144,512]{1,0:T(8,128)(2,1)} %shard_map.122), channel_id=1, source_target_pairs={{0,1},{1,0},{2,3},{3,2},{4,5},{5,4},{6,7},{7,6}} | collective-permute-start | bytes 18874376 | tf_op jit(solution)/shard_map/ppermute | solution.py:265
  1652.4 124.6 %collective-permute-start.49 = (bf16[6144,512]{1,0:T(8,128)(2,1)}, bf16[6144,512]{1,0:T(8,128)(2,1)}, u32[]{:S(2)}, u32[]{:S(2)}) collective-permute-start(bf16[6144,512]{1,0:T(8,128)(2,1)} %shard_map.125), channel_id=1, source_target_pairs={{0,1},{1,0},{2,3},{3,2},{4,5},{5,4},{6,7},{7,6}} | collective-permute-start | bytes 18874376 | tf_op jit(solution)/shard_map/ppermute | solution.py:265
  1677.0 99.4 %collective-permute-start.47 = (bf16[3840,512]{1,0:T(8,128)(2,1)}, bf16[3840,512]{1,0:T(8,128)(2,1)S(1)}, u32[]{:S(2)}, u32[]{:S(2)}) collective-permute-start(bf16[3840,512]{1,0:T(8,128)(2,1)} %pad_maximum_fusion.4), channel_id=1, source_target_pairs={{0,2},{1,3},{2,0},{3,1},{4,6},{5,7},{6,4},{7,5}} | collective-permute-start | bytes 11796488 | tf_op jit(solution)/shard_map/ppermute | solution.py:265
  1677.6 63.8 %collective-permute-start.54 = (bf16[6144,256]{1,0:T(8,128)(2,1)}, bf16[6144,256]{1,0:T(8,128)(2,1)}, u32[]{:S(2)}, u32[]{:S(2)}) collective-permute-start(bf16[6144,256]{1,0:T(8,128)(2,1)} %shard_map.128), channel_id=1, source_target_pairs={{0,1},{1,0},{2,3},{3,2},{4,5},{5,4},{6,7},{7,6}} | collective-permute-start | bytes 9437192 | tf_op jit(solution)/shard_map/ppermute | solution.py:265
  1741.4 242.0 %collective-permute-start.32 = (bf16[3072,1536]{1,0:T(8,128)(2,1)}, bf16[3072,1536]{1,0:T(8,128)(2,1)}, u32[]{:S(2)}, u32[]{:S(2)}) collective-permute-start(bf16[3072,1536]{1,0:T(8,128)(2,1)} %shard_map.113), channel_id=1, source_target_pairs={{0,1},{1,0},{2,3},{3,2},{4,5},{5,4},{6,7},{7,6}} | collective-permute-start | bytes 28311560 | tf_op jit(solution)/shard_map/ppermute | solution.py:265
  1755.7 100.4 %collective-permute-start.40 = (bf16[3072,256]{1,0:T(8,128)(2,1)}, bf16[3072,256]{1,0:T(8,128)(2,1)}, u32[]{:S(2)}, u32[]{:S(2)}) collective-permute-start(bf16[3072,256]{1,0:T(8,128)(2,1)} %shard_map.120), channel_id=1, source_target_pairs={{0,4},{4,0},{1,5},{5,1},{2,6},{6,2},{3,7},{7,3}} | collective-permute-start | bytes 4718600 | tf_op jit(solution)/shard_map/ppermute | solution.py:268
  1776.4 81.2 %collective-permute-start.55 = (bf16[3072,256]{1,0:T(8,128)(2,1)}, bf16[3072,256]{1,0:T(8,128)(2,1)}, u32[]{:S(2)}, u32[]{:S(2)}) collective-permute-start(bf16[3072,256]{1,0:T(8,128)(2,1)} %shard_map.129), channel_id=1, source_target_pairs={{0,4},{4,0},{1,5},{5,1},{2,6},{6,2},{3,7},{7,3}} | collective-permute-start | bytes 4718600 | tf_op jit(solution)/shard_map/ppermute | solution.py:268
  1777.0 117.4 %collective-permute-start.45 = (bf16[3072,512]{1,0:T(8,128)(2,1)}, bf16[3072,512]{1,0:T(8,128)(2,1)}, u32[]{:S(2)}, u32[]{:S(2)}) collective-permute-start(bf16[3072,512]{1,0:T(8,128)(2,1)} %shard_map.123), channel_id=1, source_target_pairs={{0,4},{4,0},{1,5},{5,1},{2,6},{6,2},{3,7},{7,3}} | collective-permute-start | bytes 9437192 | tf_op jit(solution)/shard_map/ppermute | solution.py:268
  1797.8 164.1 %collective-permute-start.50 = (bf16[3072,512]{1,0:T(8,128)(2,1)}, bf16[3072,512]{1,0:T(8,128)(2,1)}, u32[]{:S(2)}, u32[]{:S(2)}) collective-permute-start(bf16[3072,512]{1,0:T(8,128)(2,1)} %shard_map.126), channel_id=1, source_target_pairs={{0,4},{4,0},{1,5},{5,1},{2,6},{6,2},{3,7},{7,3}} | collective-permute-start | bytes 9437192 | tf_op jit(solution)/shard_map/ppermute | solution.py:268
  1856.1 173.1 %collective-permute-start.34 = (bf16[3072,512]{1,0:T(8,128)(2,1)S(1)}, bf16[3072,512]{1,0:T(8,128)(2,1)}, u32[]{:S(2)}, u32[]{:S(2)}) collective-permute-start(bf16[3072,512]{1,0:T(8,128)(2,1)S(1)} %copy-done.9), channel_id=1, source_target_pairs={{0,4},{4,0},{1,5},{5,1},{2,6},{6,2},{3,7},{7,3}} | collective-permute-start | bytes 9437192 | tf_op jit(solution)/shard_map/ppermute | solution.py:268
  1857.6 239.0 %collective-permute-start.35 = (bf16[3072,512]{1,0:T(8,128)(2,1)}, bf16[3072,512]{1,0:T(8,128)(2,1)}, u32[]{:S(2)}, u32[]{:S(2)}) collective-permute-start(bf16[3072,512]{1,0:T(8,128)(2,1)} %shard_map.116), channel_id=1, source_target_pairs={{0,4},{4,0},{1,5},{5,1},{2,6},{6,2},{3,7},{7,3}} | collective-permute-start | bytes 9437192 | tf_op jit(solution)/shard_map/ppermute | solution.py:268
  1894.4 268.9 %collective-permute-start.36 = (bf16[3072,512]{1,0:T(8,128)(2,1)}, bf16[3072,512]{1,0:T(8,128)(2,1)}, u32[]{:S(2)}, u32[]{:S(2)}) collective-permute-start(bf16[3072,512]{1,0:T(8,128)(2,1)} %shard_map.117), channel_id=1, source_target_pairs={{0,4},{4,0},{1,5},{5,1},{2,6},{6,2},{3,7},{7,3}} | collective-permute-start | bytes 9437192 | tf_op jit(solution)/shard_map/ppermute | solution.py:268
  1961.8 277.1 %collective-permute-start.41 = (bf16[3072,256]{1,0:T(8,128)(2,1)}, bf16[3072,256]{1,0:T(8,128)(2,1)}, u32[]{:S(2)}, u32[]{:S(2)}) collective-permute-start(bf16[3072,256]{1,0:T(8,128)(2,1)} %shard_map.121), channel_id=1, source_target_pairs={{0,2},{1,3},{2,0},{3,1},{4,6},{5,7},{6,4},{7,5}} | collective-permute-start | bytes 4718600 | tf_op jit(solution)/shard_map/ppermute | solution.py:265
  1983.3 234.2 %collective-permute-start.56 = (bf16[3072,256]{1,0:T(8,128)(2,1)}, bf16[3072,256]{1,0:T(8,128)(2,1)}, u32[]{:S(2)}, u32[]{:S(2)}) collective-permute-start(bf16[3072,256]{1,0:T(8,128)(2,1)} %shard_map.130), channel_id=1, source_target_pairs={{0,2},{1,3},{2,0},{3,1},{4,6},{5,7},{6,4},{7,5}} | collective-permute-start | bytes 4718600 | tf_op jit(solution)/shard_map/ppermute | solution.py:265
  2029.2 188.3 %collective-permute-start.46 = (bf16[3072,512]{1,0:T(8,128)(2,1)}, bf16[3072,512]{1,0:T(8,128)(2,1)S(1)}, u32[]{:S(2)}, u32[]{:S(2)}) collective-permute-start(bf16[3072,512]{1,0:T(8,128)(2,1)} %shard_map.124), channel_id=1, source_target_pairs={{0,2},{1,3},{2,0},{3,1},{4,6},{5,7},{6,4},{7,5}} | collective-permute-start | bytes 9437192 | tf_op jit(solution)/shard_map/ppermute | solution.py:265
  2096.6 120.9 %collective-permute-start.51 = (bf16[3072,512]{1,0:T(8,128)(2,1)}, bf16[3072,512]{1,0:T(8,128)(2,1)}, u32[]{:S(2)}, u32[]{:S(2)}) collective-permute-start(bf16[3072,512]{1,0:T(8,128)(2,1)} %shard_map.127), channel_id=1, source_target_pairs={{0,2},{1,3},{2,0},{3,1},{4,6},{5,7},{6,4},{7,5}} | collective-permute-start | bytes 9437192 | tf_op jit(solution)/shard_map/ppermute | solution.py:265
  (12 other events, 122.2 us)
